TPU v7x, 32 devices: a whole 2x2x4 slice. The times are simulated.
32 devices in a mesh: dp: 16 (over z, y, core), shard: 2 (over x).
Axes of the slice: x: 2, y: 2, z: 4, core: 2. Of those that a mesh axis runs over, the one named last changes fastest.
Arguments:
- inputs: bfloat16 [64, 576, 768], P(('dp', 'shard')), may hold values from -6 to 6
- cotangent: bfloat16 [64, 576, 768], P(('dp', 'shard')), may hold values from -6 to 6
- regions: int32 [576], replicated, may hold values from 0 to 8, as said below
- attend: float32 [768, 2304], P('dp', 'shard'), may hold values from -0.21875 to 0.21875
- attend_first: float32 [768, 2304], P('dp', 'shard'), may hold values from -0.0078125 to 0.0078125
- attend_second: float32 [768, 2304], P('dp', 'shard'), may hold values from 8.138021e-09 to 8.138021e-08
- project: float32 [768, 768], P('dp', 'shard'), may hold values from -0.4375 to 0.4375
- project_first: float32 [768, 768], P('dp', 'shard'), may hold values from -0.0078125 to 0.0078125
- project_second: float32 [768, 768], P('dp', 'shard'), may hold values from 8.138021e-09 to 8.138021e-08
- expand: float32 [768, 3072], P('dp', 'shard'), may hold values from -0.21875 to 0.21875
- expand_first: float32 [768, 3072], P('dp', 'shard'), may hold values from -0.0078125 to 0.0078125
- expand_second: float32 [768, 3072], P('dp', 'shard'), may hold values from 8.138021e-09 to 8.138021e-08
- contract: float32 [3072, 768], P('dp', 'shard'), may hold values from -0.109375 to 0.109375
- contract_first: float32 [3072, 768], P('dp', 'shard'), may hold values from -0.0078125 to 0.0078125
- contract_second: float32 [3072, 768], P('dp', 'shard'), may hold values from 8.138021e-09 to 8.138021e-08
- gains: float32 [2, 768], replicated, may hold values from 0.5 to 1.5
- gains_first: float32 [2, 768], replicated, may hold values from -0.0078125 to 0.0078125
- gains_second: float32 [2, 768], replicated, may hold values from 8.138021e-09 to 8.138021e-08
- shifts: float32 [2, 768], replicated, may hold values from -2 to 2
- shifts_first: float32 [2, 768], replicated, may hold values from -0.0078125 to 0.0078125
- shifts_second: float32 [2, 768], replicated, may hold values from 8.138021e-09 to 8.138021e-08
- biases: float32 [6912], replicated, may hold values from -2 to 2
- biases_first: float32 [6912], replicated, may hold values from -0.0078125 to 0.0078125
- biases_second: float32 [6912], replicated, may hold values from 8.138021e-09 to 8.138021e-08
- position: float32 [529, 24], replicated, may hold values from -4 to 4
- position_first: float32 [529, 24], replicated, may hold values from -0.0078125 to 0.0078125
- position_second: float32 [529, 24], replicated, may hold values from 8.138021e-09 to 8.138021e-08
Outputs:
- block_output: bfloat16 [64, 576, 768], P(('dp', 'shard'))
- input_gradient: float32 [64, 576, 768], P(('dp', 'shard'))
- attend_weight: float32 [768, 2304], P('dp', 'shard')
- attend_momentum: float32 [768, 2304], P('dp', 'shard')
- attend_variance: float32 [768, 2304], P('dp', 'shard')
- attend_copy: bfloat16 [768, 2304], P('dp', 'shard')
- project_weight: float32 [768, 768], P('dp', 'shard')
- project_momentum: float32 [768, 768], P('dp', 'shard')
- project_variance: float32 [768, 768], P('dp', 'shard')
- project_copy: bfloat16 [768, 768], P('dp', 'shard')
- expand_weight: float32 [768, 3072], P('dp', 'shard')
- expand_momentum: float32 [768, 3072], P('dp', 'shard')
- expand_variance: float32 [768, 3072], P('dp', 'shard')
- expand_copy: bfloat16 [768, 3072], P('dp', 'shard')
- contract_weight: float32 [3072, 768], P('dp', 'shard')
- contract_momentum: float32 [3072, 768], P('dp', 'shard')
- contract_variance: float32 [3072, 768], P('dp', 'shard')
- contract_copy: bfloat16 [3072, 768], P('dp', 'shard')
- gains_weight: float32 [2, 768], replicated
- gains_momentum: float32 [2, 768], replicated
- gains_variance: float32 [2, 768], replicated
- shifts_weight: float32 [2, 768], replicated
- shifts_momentum: float32 [2, 768], replicated
- shifts_variance: float32 [2, 768], replicated
- biases_weight: float32 [6912], replicated
- biases_momentum: float32 [6912], replicated
- biases_variance: float32 [6912], replicated
- position_weight: float32 [529, 24], replicated
- position_momentum: float32 [529, 24], replicated
- position_variance: float32 [529, 24], replicated
- norm_pairs: float32 [8, 2], replicated
Inputs may be any that keep to these rules, and one draw needn't show every extreme that they name: `regions`: label of each token of the rolled 24 x 24 grid, row-major: 3 times the band of its row plus the band of its column, where a line's bands are split at 12 and at one drawn position after it, drawn for rows and columns apart.
All inputs are finite; a program needn't handle non-finite values.
Results may differ from a plain program's by a relative error of at most 0.0095.
The roundings to bfloat16 on the way count: a program that leaves them out, or rounds other values in their place, can miss the bound.
Values may be sent and summed in bfloat16 or wider, within the bound.
A program may use at most 256 MiB of HBM per device.

v0:
```python
import jax
import jax.numpy as jnp
from jax import lax
from jax.sharding import PartitionSpec as P

HD = 32
WIN = 12
MB = 2
STEP = 10
HEADS = 24
GRID = 24
SHIFT = 6


beta_one = 0.9
beta_two = 0.999
adam_eps = 1e-06
decay_rate = 0.01
learn_rate = 0.25
norm_eps = 1e-05
masked_score = -100.0


def layer_norm(values, gain_row, shift_row):
    centred = values - jnp.mean(values, axis=-1, keepdims=True)
    spread = jnp.mean(centred * centred, axis=-1, keepdims=True)
    return centred * lax.rsqrt(spread + norm_eps) * gain_row + shift_row


def gelu_exact(values):
    return jax.nn.gelu(values, approximate=False)


def to_windows(values):
    images = values.shape[0]
    channels = values.shape[-1]
    layout = values.reshape(images, GRID, GRID, channels)
    layout = jnp.roll(layout, (-SHIFT, -SHIFT), axis=(1, 2))
    layout = layout.reshape(images, GRID // WIN, WIN, GRID // WIN, WIN, channels)
    return layout.transpose(0, 1, 3, 2, 4, 5).reshape(
        images * (GRID // WIN) ** 2, WIN * WIN, channels
    )


def from_windows(values, images):
    channels = values.shape[-1]
    layout = values.reshape(images, GRID // WIN, GRID // WIN, WIN, WIN, channels)
    layout = layout.transpose(0, 1, 3, 2, 4, 5).reshape(images, GRID, GRID, channels)
    layout = jnp.roll(layout, (SHIFT, SHIFT), axis=(1, 2))
    return layout.reshape(images, GRID * GRID, channels)


def relative_index():
    places = jnp.arange(WIN * WIN, dtype=jnp.int32)
    row_of = places // WIN
    column = places % WIN
    return (row_of[:, None] - row_of[None, :] + WIN - 1) * (2 * WIN - 1) + (
        column[:, None] - column[None, :] + WIN - 1
    )


def window_allowed(regions):
    labels = (
        regions.reshape(GRID // WIN, WIN, GRID // WIN, WIN)
        .transpose(0, 2, 1, 3)
        .reshape((GRID // WIN) ** 2, WIN * WIN)
    )
    return labels[:, :, None] == labels[:, None, :]


def product_left(left, right):
    return lax.dot_general(
        left, right, (((0,), (0,)), ((), ())), preferred_element_type=jnp.float32
    )


def product_right(left, right):
    return lax.dot_general(
        left, right, (((1,), (1,)), ((), ())), preferred_element_type=jnp.float32
    )


def masked(tensor, allowed, images, filler):
    shaped = tensor.reshape(images, allowed.shape[0], HEADS, WIN * WIN, WIN * WIN)
    return jnp.where(allowed[None, :, None], shaped, filler).reshape(tensor.shape)


def attention_scores(query, keyed, table_bias, allowed, images):
    raw = jnp.einsum("wihd,wjhd->whij", query, keyed, preferred_element_type=jnp.float32)
    return masked(raw * HD ** (-0.5) + table_bias[None], allowed, images, masked_score)


def micro_step(
    values_low, cot_low, full, gains, shifts, biases, table_bias, allowed, index, table_rows
):
    attend, project, expand, contract = full
    images = values_low.shape[0]
    width = attend.shape[0]
    hidden_width = expand.shape[1]
    windows_count = images * allowed.shape[0]
    values = values_low.astype(jnp.float32)
    normed, norm_back = jax.vjp(layer_norm, values, gains[0], shifts[0])
    windowed = to_windows(normed.astype(jnp.bfloat16)).reshape(-1, width)
    triple = jnp.dot(windowed, attend, preferred_element_type=jnp.float32) + biases[: 3 * width]
    triple = triple.astype(jnp.bfloat16).reshape(windows_count, WIN * WIN, 3, HEADS, HD)
    query = triple[:, :, 0]
    keyed = triple[:, :, 1]
    valued = triple[:, :, 2]
    scores = attention_scores(query, keyed, table_bias, allowed, images)
    log_total = jax.nn.logsumexp(scores, axis=-1, keepdims=True)
    probs_low = jnp.exp(scores - log_total).astype(jnp.bfloat16)
    mixed = jnp.einsum("whij,wjhd->wihd", probs_low, valued, preferred_element_type=jnp.float32)
    mixed_low = mixed.reshape(windows_count, WIN * WIN, width).astype(jnp.bfloat16)
    merged = from_windows(mixed_low, images).reshape(-1, width)
    branch = (
        jnp.dot(merged, project, preferred_element_type=jnp.float32) + biases[3 * width : 4 * width]
    )
    middle = values + branch.reshape(values.shape)
    normed_two, norm_two_back = jax.vjp(layer_norm, middle, gains[1], shifts[1])
    normed_two_low = normed_two.astype(jnp.bfloat16).reshape(-1, width)
    hidden = (
        jnp.dot(normed_two_low, expand, preferred_element_type=jnp.float32)
        + biases[4 * width : 4 * width + hidden_width]
    )
    active, gelu_back = jax.vjp(gelu_exact, hidden)
    active_low = active.astype(jnp.bfloat16)
    result = middle + (
        jnp.dot(active_low, contract, preferred_element_type=jnp.float32)
        + biases[4 * width + hidden_width :]
    ).reshape(values.shape)
    cot_rows = cot_low.reshape(-1, width)
    cot_float = cot_rows.astype(jnp.float32)
    grad_contract = product_left(active_low, cot_rows)
    grad_bias_contract = jnp.sum(cot_float, axis=0)
    grad_active = product_right(cot_rows, contract)
    grad_hidden_low = gelu_back(grad_active)[0].astype(jnp.bfloat16)
    grad_expand = product_left(normed_two_low, grad_hidden_low)
    grad_bias_expand = jnp.sum(grad_hidden_low, axis=0, dtype=jnp.float32)
    grad_normed_two = product_right(grad_hidden_low, expand).reshape(values.shape)
    grad_middle_part, grad_gain_two, grad_shift_two = norm_two_back(grad_normed_two)
    grad_middle = cot_float.reshape(values.shape) + grad_middle_part
    grad_branch_low = grad_middle.reshape(-1, width).astype(jnp.bfloat16)
    grad_project = product_left(merged, grad_branch_low)
    grad_bias_project = jnp.sum(grad_branch_low, axis=0, dtype=jnp.float32)
    grad_merged_low = (
        product_right(grad_branch_low, project).astype(jnp.bfloat16).reshape(values.shape)
    )
    grad_mixed = to_windows(grad_merged_low).reshape(windows_count, WIN * WIN, HEADS, HD)
    scores_again = attention_scores(query, keyed, table_bias, allowed, images)
    probs = jnp.exp(scores_again - log_total)
    probs_again = probs.astype(jnp.bfloat16)
    grad_probs = jnp.einsum(
        "wihd,wjhd->whij", grad_mixed, valued, preferred_element_type=jnp.float32
    )
    grad_valued = jnp.einsum(
        "whij,wihd->wjhd", probs_again, grad_mixed, preferred_element_type=jnp.float32
    )
    grad_scores = probs * (grad_probs - jnp.sum(probs * grad_probs, axis=-1, keepdims=True))
    grad_scores = masked(grad_scores, allowed, images, 0.0)
    grad_table = jnp.sum(grad_scores, axis=0).transpose(1, 2, 0).reshape(-1, HEADS)
    grad_position = jax.ops.segment_sum(grad_table, index.reshape(-1), num_segments=table_rows)
    grad_raw_low = (grad_scores * HD ** (-0.5)).astype(jnp.bfloat16)
    grad_query = jnp.einsum(
        "whij,wjhd->wihd", grad_raw_low, keyed, preferred_element_type=jnp.float32
    )
    grad_keyed = jnp.einsum(
        "whij,wihd->wjhd", grad_raw_low, query, preferred_element_type=jnp.float32
    )
    grad_triple_low = (
        jnp.stack([grad_query, grad_keyed, grad_valued], axis=2)
        .astype(jnp.bfloat16)
        .reshape(-1, 3 * width)
    )
    grad_attend = product_left(windowed, grad_triple_low)
    grad_bias_attend = jnp.sum(grad_triple_low, axis=0, dtype=jnp.float32)
    grad_windowed = product_right(grad_triple_low, attend).reshape(windows_count, WIN * WIN, width)
    grad_normed = from_windows(grad_windowed, images)
    grad_input_part, grad_gain_one, grad_shift_one = norm_back(grad_normed)
    grad_input = grad_middle + grad_input_part
    grads = (
        grad_attend,
        grad_project,
        grad_expand,
        grad_contract,
        jnp.stack([grad_gain_one, grad_gain_two]),
        jnp.stack([grad_shift_one, grad_shift_two]),
        jnp.concatenate(
            [grad_bias_attend, grad_bias_project, grad_bias_expand, grad_bias_contract]
        ),
        grad_position,
    )
    return (result.astype(jnp.bfloat16), grad_input, grads)


def moments(weight, first, second, gradient, decay):
    momentum = beta_one * first + (1.0 - beta_one) * gradient
    variance = beta_two * second + (1.0 - beta_two) * gradient * gradient
    ratio = (
        momentum / (1.0 - beta_one**STEP) / (jnp.sqrt(variance / (1.0 - beta_two**STEP)) + adam_eps)
    )
    return (momentum, variance, ratio + decay * weight)


def body(
    inputs,
    cotangent,
    regions,
    attend,
    attend_first,
    attend_second,
    project,
    project_first,
    project_second,
    expand,
    expand_first,
    expand_second,
    contract,
    contract_first,
    contract_second,
    gains,
    gains_first,
    gains_second,
    shifts,
    shifts_first,
    shifts_second,
    biases,
    biases_first,
    biases_second,
    position,
    position_first,
    position_second,
):
    masters = (attend, project, expand, contract, gains, shifts, biases, position)
    firsts = (
        attend_first,
        project_first,
        expand_first,
        contract_first,
        gains_first,
        shifts_first,
        biases_first,
        position_first,
    )
    seconds = (
        attend_second,
        project_second,
        expand_second,
        contract_second,
        gains_second,
        shifts_second,
        biases_second,
        position_second,
    )
    dp_count = lax.axis_size("dp")
    shard_count = lax.axis_size("shard")
    tokens_all = inputs.shape[0] * inputs.shape[1] * dp_count * shard_count
    halves = (
        lax.all_gather(attend.astype(jnp.bfloat16), "dp", axis=0, tiled=True),
        lax.all_gather(project.astype(jnp.bfloat16), "dp", axis=0, tiled=True),
        lax.all_gather(expand.astype(jnp.bfloat16), "dp", axis=0, tiled=True),
        lax.all_gather(contract.astype(jnp.bfloat16), "dp", axis=0, tiled=True),
    )
    allowed = window_allowed(regions)
    index = relative_index()
    table_bias = jnp.take(position, index, axis=0).transpose(2, 0, 1)
    per_micro = inputs.shape[0] // MB
    results = []
    input_grads = []
    totals = None
    for micro_index in range(MB):
        full = (
            lax.all_gather(halves[0], "shard", axis=1, tiled=True),
            lax.all_gather(halves[1], "shard", axis=1, tiled=True),
            lax.all_gather(halves[2], "shard", axis=1, tiled=True),
            lax.all_gather(halves[3], "shard", axis=1, tiled=True),
        )
        lower = micro_index * per_micro
        upper = lower + per_micro
        result_low, grad_input, grads = micro_step(
            inputs[lower:upper],
            cotangent[lower:upper],
            full,
            gains,
            shifts,
            biases,
            table_bias,
            allowed,
            index,
            position.shape[0],
        )
        results.append(result_low)
        input_grads.append(grad_input)
        if totals is None:
            totals = grads
        else:
            totals = tuple((before + after for before, after in zip(totals, grads)))
    totals = tuple((entry / tokens_all for entry in totals))
    small_grads = totals[4:]
    small_total = lax.psum(
        (small_grads[0], small_grads[1], small_grads[2], small_grads[3]), ("dp", "shard")
    )
    columns = (
        lax.psum_scatter(
            totals[0].astype(jnp.bfloat16), "shard", scatter_dimension=1, tiled=True
        ).astype(jnp.float32),
        lax.psum_scatter(
            totals[1].astype(jnp.bfloat16), "shard", scatter_dimension=1, tiled=True
        ).astype(jnp.float32),
        lax.psum_scatter(
            totals[2].astype(jnp.bfloat16), "shard", scatter_dimension=1, tiled=True
        ).astype(jnp.float32),
        lax.psum_scatter(
            totals[3].astype(jnp.bfloat16), "shard", scatter_dimension=1, tiled=True
        ).astype(jnp.float32),
    )
    owned = (
        lax.psum_scatter(columns[0], "dp", scatter_dimension=0, tiled=True),
        lax.psum_scatter(columns[1], "dp", scatter_dimension=0, tiled=True),
        lax.psum_scatter(columns[2], "dp", scatter_dimension=0, tiled=True),
        lax.psum_scatter(columns[3], "dp", scatter_dimension=0, tiled=True),
    )
    pieces = [
        moments(masters[slot], firsts[slot], seconds[slot], owned[slot], decay_rate)
        for slot in range(4)
    ]
    partial_value = jnp.stack(
        [
            jnp.stack(
                [jnp.sum(masters[slot] * masters[slot]), jnp.sum(pieces[slot][2] * pieces[slot][2])]
            )
            for slot in range(4)
        ]
    )
    squares = lax.psum(partial_value, ("dp", "shard"))
    matrix_norms = jnp.sqrt(squares)
    outputs = [jnp.concatenate(results, axis=0), jnp.concatenate(input_grads, axis=0)]
    pairs = []
    for slot in range(4):
        momentum, variance, update = pieces[slot]
        fresh = (
            masters[slot]
            - learn_rate * matrix_norms[slot, 0] / (matrix_norms[slot, 1] + adam_eps) * update
        )
        outputs = outputs + [fresh, momentum, variance, fresh.astype(jnp.bfloat16)]
        pairs.append(matrix_norms[slot])
    for slot in range(4):
        weight = masters[4 + slot]
        momentum, variance, update = moments(
            weight, firsts[4 + slot], seconds[4 + slot], small_total[slot], 0.0
        )
        norms = jnp.stack([jnp.sqrt(jnp.sum(weight * weight)), jnp.sqrt(jnp.sum(update * update))])
        fresh = weight - learn_rate * norms[0] / (norms[1] + adam_eps) * update
        outputs = outputs + [fresh, momentum, variance]
        pairs.append(norms)
    outputs = outputs + [jnp.stack(pairs)]
    return tuple(outputs)


def solution(mesh):
    return jax.shard_map(
        body,
        mesh=mesh,
        in_specs=(
            P(("dp", "shard"), None, None),
            P(("dp", "shard"), None, None),
            P(),
            P("dp", "shard"),
            P("dp", "shard"),
            P("dp", "shard"),
            P("dp", "shard"),
            P("dp", "shard"),
            P("dp", "shard"),
            P("dp", "shard"),
            P("dp", "shard"),
            P("dp", "shard"),
            P("dp", "shard"),
            P("dp", "shard"),
            P("dp", "shard"),
            P(),
            P(),
            P(),
            P(),
            P(),
            P(),
            P(),
            P(),
            P(),
            P(),
            P(),
            P(),
        ),
        out_specs=(
            P(("dp", "shard"), None, None),
            P(("dp", "shard"), None, None),
            P("dp", "shard"),
            P("dp", "shard"),
            P("dp", "shard"),
            P("dp", "shard"),
            P("dp", "shard"),
            P("dp", "shard"),
            P("dp", "shard"),
            P("dp", "shard"),
            P("dp", "shard"),
            P("dp", "shard"),
            P("dp", "shard"),
            P("dp", "shard"),
            P("dp", "shard"),
            P("dp", "shard"),
            P("dp", "shard"),
            P("dp", "shard"),
            P(),
            P(),
            P(),
            P(),
            P(),
            P(),
            P(),
            P(),
            P(),
            P(),
            P(),
            P(),
            P(),
        ),
        check_vma=False,
    )
```

profile of v0, /device:TPU:0, one launch (start us, length us, event | category | flops | bytes accessed | tf_op | source)
XLA Modules:
  0.0 1429.5 jit_solution(11946295939760360497)
XLA Ops:
  10.8 43.0 %all-gather.8.cloned.1.call-done = bf16[768,1152]{1,0:T(8,128)(2,1)} async-done(((bf16[48,1152]{1,0:T(8,128)(2,1)}), bf16[768,1152]{1,0:T(8,128)(2,1)}) %all-gather.8.cloned.1.call-update) | async-done | bytes 1769488 | tf_op jit(solution)/shard_map/all_gather | solution.py:258
  54.8 22.8 %all_gather.30 = bf16[768,384]{1,0:T(8,128)(2,1)} all-gather(bf16[48,384]{1,0:T(8,128)(2,1)S(1)} %convert_element_type.238), channel_id=1, replica_groups=mesh['dp'=16,'shard'=2] {'dp'}, dimensions={0}, use_global_device_ids=true | all-gather | bytes 626688 | tf_op jit(solution)/shard_map/all_gather | solution.py:259
  86.7 42.6 %gather_fusion = f32[20736,24]{1,0:T(8,128)} fusion(f32[529,24]{1,0:T(8,128)S(1)} %copy.240, s32[21504]{0:T(1024)} %pad_clamp_fusion), kind=kCustom, calls=%fused_computation | custom fusion | bytes 4064256 | tf_op jit(solution)/shard_map/jit(_take)/gather | solution.py:265
  129.3 12.5 copy.241
  161.8 10.2 reshape.1013
  183.3 9.5 exponential_reduce_fusion
  230.1 10.2 reshape.1005
  250.8 8.7 exponential_reduce_fusion.1
  293.7 38.4 %multiply_convert_fusion.6 = (bf16[576,3072]{1,0:T(8,128)(2,1)S(1)}, f32[576,3072]{1,0:T(8,128)}, bf16[576,3072]{1,0:T(8,128)(2,1)S(1)}, f32[576,3072]{1,0:T(8,128)}, f32[576,3072]{1,0:T(8,128)}) fusion(f32[3072]{0:T(1024)S(1)} %copy-done.113, f32[576,3072]{1,0:T(8,128)S(1)} %fusion.145, bf16[768,3072]{1,0:T(8,128)(2,1)S(1)} %copy-done.120, ...), kind=kOutput, calls=%fused_computation.50 | convolution fusion | flops 2953691136 | bytes 41900544 | tf_op jit(solution)/shard_map/dot_general | solution.py:122
  348.3 57.4 %reduce-scatter.29.cloned.1.call-done = bf16[384,3072]{1,0:T(8,128)(2,1)} async-done(((bf16[768,3072]{1,0:T(8,128)(2,1)}), bf16[384,3072]{1,0:T(8,128)(2,1)}) %reduce-scatter.29.cloned.1.call-update) | async-done | bytes 2359312
  414.2 75.7 %reduce-scatter.23.cloned.1.call-done = f32[192,384]{1,0:T(8,128)} async-done(((f32[3072,384]{1,0:T(8,128)}), f32[192,384]{1,0:T(8,128)}) %reduce-scatter.23.cloned.1.call-update) | async-done | bytes 294928 | tf_op jit(solution)/shard_map/reduce_scatter | solution.py:320
  492.9 41.6 %all-gather.18.cloned.1.call-done = bf16[3072,384]{1,0:T(8,128)(2,1)} async-done(((bf16[192,384]{1,0:T(8,128)(2,1)}), bf16[3072,384]{1,0:T(8,128)(2,1)}) %all-gather.18.cloned.1.call-update) | async-done | bytes 2359312 | tf_op jit(solution)/shard_map/all_gather | solution.py:261
  534.6 62.9 %all-gather.20.cloned.1.call-done = bf16[3072,768]{1,0:T(8,128)(2,1)} async-done(((bf16[3072,384]{1,0:T(8,128)(2,1)}), bf16[3072,768]{1,0:T(8,128)(2,1)}) %all-gather.20.cloned.1.call-update) | async-done | bytes 4718608 | tf_op jit(solution)/shard_map/all_gather | solution.py:275
  597.4 10.0 convert_reduce_fusion.2
  666.2 8.7 convolution_bitcast_fusion.1
  682.0 27.4 %fusion.182 = (f32[24,144,144]{1,2,0:T(8,128)}, f32[4,24,144,144]{2,3,1,0:T(8,128)}) fusion(f32[4,24,144,144]{2,3,1,0:T(8,128)} %fusion.88, f32[4,24,144,144]{2,3,1,0:T(8,128)} %get-tuple-element.280, f32[4,24,144]{2,1,0:T(8,128)S(1)} %copy-done.44, pred[4,144,144]{1,2,0:T(8,128)(4,1)S(1)} %copy-done.36), kind=kOutput, calls=%fused_computation.346 | output fusion | flops 13450895 | bytes 26016768 | tf_op jit(solution)/shard_map/sub | solution.py:158
  709.4 8.7 fusion.47
  723.7 27.2 %fusion.183 = (f32[24,144,144]{1,2,0:T(8,128)}, f32[4,24,144,144]{2,3,1,0:T(8,128)}) fusion(f32[4,24,144,144]{2,3,1,0:T(8,128)} %fusion.89, f32[4,24,144,144]{2,3,1,0:T(8,128)} %get-tuple-element.284, f32[4,24,144]{2,1,0:T(8,128)S(1)} %copy-done.42, pred[4,144,144]{1,2,0:T(8,128)(4,1)S(1)} %copy-done.36), kind=kOutput, calls=%fused_computation.347 | output fusion | flops 13450895 | bytes 26016768 | tf_op jit(solution)/shard_map/sub | solution.py:158
  763.6 11.5 copy.271
  775.1 8.7 convert_element_type.270
  800.0 11.5 copy.272
  811.5 9.3 convert_element_type.271
  848.8 31.3 %reduce-scatter.25.cloned.1.call-done = bf16[1152,768]{1,0:T(8,128)(2,1)} async-done(((bf16[2304,768]{1,0:T(8,128)(2,1)}), bf16[1152,768]{1,0:T(8,128)(2,1)}) %reduce-scatter.25.cloned.1.call-update) | async-done | bytes 1769488
  887.6 12.1 copy.296
  899.7 11.6 reshape.1059
  919.3 11.8 copy.295
  931.2 12.9 reshape.1058
  983.1 11.0 copy.297
  994.1 113.1 %scatter_custom_fusion = f32[529,24]{1,0:T(8,128)} fusion(s32[20736]{0:T(1024)} %reshape.1040, f32[20736,24]{1,0:T(8,128)} %bitcast.303, f32[]{:T(128)} %constant.72.clone.1), kind=kCustom, calls=%fused_computation.231 | custom fusion | flops 497664 | bytes 51296 | tf_op jit(solution)/shard_map/scatter-add | solution.py:161
  1108.9 11.1 copy.298
  1120.1 113.1 %scatter_custom_fusion.1 = f32[529,24]{1,0:T(8,128)} fusion(s32[20736]{0:T(1024)} %reshape.1040, f32[20736,24]{1,0:T(8,128)} %bitcast.302, f32[]{:T(128)} %constant.72.clone.1), kind=kCustom, calls=%fused_computation.229 | custom fusion | flops 497664 | bytes 51296 | tf_op jit(solution)/shard_map/scatter-add | solution.py:161
  1271.4 122.4 %all-reduce.3.cloned.1.call-done = (f32[4,2]{1,0:T(4,128)}, f32[2,768]{1,0:T(2,128)}, f32[2,768]{1,0:T(2,128)}, f32[6912]{0:T(1024)}, f32[529,24]{0,1:T(8,128)}) async-done(((f32[4,2]{1,0:T(4,128)}, f32[2,768]{1,0:T(2,128)}, f32[2,768]{1,0:T(2,128)}, f32[6912]{0:T(1024)}, f32[529,24]{0,1:T(8,128)}), (f32[4,2]{1,0:T(4,128)}, f32[2,768]{1,0:T(2,128)}, f32[2,768]{1,0:T(2,128)}, f32[6912]{0:T(1024)}, ...) | async-done | bytes 90768 | tf_op jit(solution)/shard_map/psum | solution.py:334
  (526 shorter events, 393.2 us)
Async XLA Ops:
  7.2 71.4 %copy-start.90 = (f32[2,768]{1,0:T(2,128)S(1)}, f32[2,768]{1,0:T(2,128)}, u32[]{:S(2)}) copy-start(f32[2,768]{1,0:T(2,128)} %param.45) | copy-start | bytes 18436
  7.2 71.4 %copy-start.89 = (f32[2,768]{1,0:T(2,128)S(1)}, f32[2,768]{1,0:T(2,128)}, u32[]{:S(2)}) copy-start(f32[2,768]{1,0:T(2,128)} %param.42) | copy-start | bytes 18436
  7.2 71.4 %copy-start.1 = (bf16[2,576,768]{2,1,0:T(8,128)(2,1)S(1)}, bf16[2,576,768]{2,1,0:T(8,128)(2,1)}, u32[]{:S(2)}) copy-start(bf16[2,576,768]{2,1,0:T(8,128)(2,1)} %param.27) | copy-start | bytes 5308420
  7.2 46.6 %all-gather.8.cloned.1.call-start = ((), (), s32[]{:S(2)}) async-start(), calls=%async_computation.8 | async-start | bytes 1880064 | tf_op jit(solution)/shard_map/all_gather | solution.py:258
  9.0 141.6 %all-gather.14.cloned.1.call-start = ((), (), s32[]{:S(2)}) async-start(), calls=%async_computation.11 | async-start | bytes 2506752 | tf_op jit(solution)/shard_map/all_gather | solution.py:260
  10.7 140.0 %all-gather.10.cloned.1.call-start = ((), (), s32[]{:S(2)}) async-start(), calls=%async_computation.9 | async-start | bytes 5308416 | tf_op jit(solution)/shard_map/all_gather | solution.py:272
  53.8 228.3 %all-gather.12.cloned.1.call-start = ((), (), s32[]{:S(2)}) async-start(), calls=%async_computation.10 | async-start | bytes 1769472 | tf_op jit(solution)/shard_map/all_gather | solution.py:273
  77.6 209.7 %all-gather.16.cloned.1.call-start = ((), (), s32[]{:S(2)}) async-start(), calls=%async_computation.12 | async-start | bytes 7077888 | tf_op jit(solution)/shard_map/all_gather | solution.py:274
  78.6 215.0 %copy-start.72 = (f32[768]{0:T(1024)}, f32[768]{0:T(1024)S(1)}, u32[]{:S(2)}) copy-start(f32[768]{0:T(1024)S(1)} %get-tuple-element.187) | copy-start | bytes 9220
  150.7 255.0 %reduce-scatter.29.cloned.1.call-start = ((), (), s32[]{:S(2)}) async-start(), calls=%async_computation.22 | async-start | bytes 7077888
  286.2 341.4 %copy-start.19 = (f32[1,576,768]{2,1,0:T(8,128)}, f32[1,576,768]{2,1,0:T(8,128)S(1)}, u32[]{:S(2)}) copy-start(f32[1,576,768]{2,1,0:T(8,128)S(1)} %get-tuple-element.282) | copy-start | bytes 5308420
  293.7 38.4 %copy-start.124 = (f32[576,3072]{1,0:T(8,128)}, f32[576,3072]{1,0:T(8,128)S(1)}, u32[]{:S(2)}) copy-start(f32[576,3072]{1,0:T(8,128)S(1)} %fusion.145) | copy-start | bytes 21233668
  348.2 141.7 %reduce-scatter.23.cloned.1.call-start = ((), (), s32[]{:S(2)}) async-start(), calls=%async_computation.19 | async-start | bytes 5013504 | tf_op jit(solution)/shard_map/reduce_scatter | solution.py:320
  414.1 120.4 %all-gather.18.cloned.1.call-start = ((), (), s32[]{:S(2)}) async-start(), calls=%async_computation.13 | async-start | bytes 2506752 | tf_op jit(solution)/shard_map/all_gather | solution.py:261
  492.8 104.6 %all-gather.20.cloned.1.call-start = ((), (), s32[]{:S(2)}) async-start(), calls=%async_computation.14 | async-start | bytes 7077888 | tf_op jit(solution)/shard_map/all_gather | solution.py:275
  534.5 311.7 %reduce-scatter.27.cloned.1.call-start = ((), (), s32[]{:S(2)}) async-start(), calls=%async_computation.21 | async-start | bytes 1769472
  788.9 91.2 %reduce-scatter.25.cloned.1.call-start = ((), (), s32[]{:S(2)}) async-start(), calls=%async_computation.20 | async-start | bytes 5308416
  832.2 121.0 %reduce-scatter.19.cloned.1.call-start = ((), (), s32[]{:S(2)}) async-start(), calls=%async_computation.17 | async-start | bytes 7077888 | tf_op jit(solution)/shard_map/reduce_scatter | solution.py:309
  846.2 411.4 %reduce-scatter.17.cloned.1.call-start = ((), (), s32[]{:S(2)}) async-start(), calls=%async_computation.16 | async-start | bytes 1253376 | tf_op jit(solution)/shard_map/reduce_scatter | solution.py:318
  848.8 411.0 %reduce-scatter.15.cloned.1.call-start = ((), (), s32[]{:S(2)}) async-start(), calls=%async_computation.15 | async-start | bytes 3760128 | tf_op jit(solution)/shard_map/reduce_scatter | solution.py:317
  884.9 379.3 %reduce-scatter.21.cloned.1.call-start = ((), (), s32[]{:S(2)}) async-start(), calls=%async_computation.18 | async-start | bytes 5013504 | tf_op jit(solution)/shard_map/reduce_scatter | solution.py:319
  957.8 436.0 %all-reduce.3.cloned.1.call-start = ((), (), s32[]{:S(2)}) async-start(), calls=%async_computation.23 | async-start | bytes 208896 | tf_op jit(solution)/shard_map/psum | solution.py:334
  1259.7 157.6 %copy-start.62 = (f32[48,384]{1,0:T(8,128)}, f32[48,384]{1,0:T(8,128)S(1)}, u32[]{:S(2)}) copy-start(f32[48,384]{1,0:T(8,128)S(1)} %get-tuple-element.232) | copy-start | bytes 221188
  1259.8 147.3 %copy-start.65 = (f32[6912]{0:T(1024)S(1)}, f32[6912]{0:T(1024)}, u32[]{:S(2)}) copy-start(f32[6912]{0:T(1024)} %param.48) | copy-start | bytes 82948
  1259.8 150.1 %copy-start.61 = (f32[529,24]{0,1:T(8,128)S(1)}, f32[529,24]{0,1:T(8,128)}, u32[]{:S(2)}) copy-start(f32[529,24]{0,1:T(8,128)} %param.51) | copy-start | bytes 152356
  1261.6 155.8 %copy-start.55 = (f32[48,1152]{1,0:T(8,128)}, f32[48,1152]{1,0:T(8,128)S(1)}, u32[]{:S(2)}) copy-start(f32[48,1152]{1,0:T(8,128)S(1)} %get-tuple-element.230) | copy-start | bytes 663556
  1261.6 155.8 %copy-start.56 = (f32[48,1152]{1,0:T(8,128)}, f32[48,1152]{1,0:T(8,128)S(1)}, u32[]{:S(2)}) copy-start(f32[48,1152]{1,0:T(8,128)S(1)} %get-tuple-element.231) | copy-start | bytes 663556
  1266.1 153.8 %copy-start.50 = (f32[48,1536]{1,0:T(8,128)}, f32[48,1536]{1,0:T(8,128)S(1)}, u32[]{:S(2)}) copy-start(f32[48,1536]{1,0:T(8,128)S(1)} %get-tuple-element.234) | copy-start | bytes 884740
  1266.1 153.8 %copy-start.51 = (f32[48,1536]{1,0:T(8,128)}, f32[48,1536]{1,0:T(8,128)S(1)}, u32[]{:S(2)}) copy-start(f32[48,1536]{1,0:T(8,128)S(1)} %get-tuple-element.235) | copy-start | bytes 884740
  1268.7 151.1 %copy-start.47 = (f32[192,384]{1,0:T(8,128)S(1)}, f32[192,384]{1,0:T(8,128)}, u32[]{:S(2)}) copy-start(f32[192,384]{1,0:T(8,128)} %param.39) | copy-start | bytes 884740
  1268.7 151.1 %copy-start.48 = (f32[192,384]{1,0:T(8,128)S(1)}, f32[192,384]{1,0:T(8,128)}, u32[]{:S(2)}) copy-start(f32[192,384]{1,0:T(8,128)} %get-tuple-element.236) | copy-start | bytes 884740
  1268.7 151.1 %copy-start.49 = (f32[192,384]{1,0:T(8,128)S(1)}, f32[192,384]{1,0:T(8,128)}, u32[]{:S(2)}) copy-start(f32[192,384]{1,0:T(8,128)} %get-tuple-element.237) | copy-start | bytes 884740
  (122 other events, 689.9 us)
Sparse Core Ops, SparseCore 0:
  10.8 42.9 all-gather.7
  56.7 41.4 all-gather.13
  99.7 48.0 all-gather.9
  149.2 22.7 all-gather.11
  173.4 62.6 all-gather.15
  348.3 57.3 reduce-scatter.28
  414.2 75.5 reduce-scatter.22
  492.9 41.4 all-gather.17
  536.0 61.3 all-gather.19
  789.0 21.8 reduce-scatter.26
  832.3 47.7 reduce-scatter.24
  882.2 60.0 reduce-scatter.18
  946.0 58.1 reduce-scatter.16
  1007.9 67.0 reduce-scatter.14
  1078.7 74.4 reduce-scatter.20
  1268.8 124.9 all-reduce.2
where the time goes:
time: 1440 us; the launch traced here: 1430 us
  waiting for transfers between devices  435 us (30%)
  other arithmetic  398 us (28%)
  local copies, waits for them, and re-layouts  310 us (22%)
  matrix products  237 us (16%)
  between operations  27.2 us (2%)
  blocking collectives  22.8 us (2%)
    scatter-add x2, other arithmetic, micro_step(): jax.ops.segment_sum(grad_table, index.reshape(-1), num_segments=table_rows)  226 us
    psum x1, waiting for transfers between devices, body(): squares = lax.psum(partial_value, ('dp', 'shard'))  122 us
    convert_element_type x8, local copies, waits for them, and re-layouts, micro_step(): grad_triple_low = jnp.stack([grad_query, grad_keyed, grad_valued], axis=2...  89.4 us
    unnamed x19, waiting for transfers between devices  89 us
    reduce_scatter x1, waiting for transfers between devices, body(): lax.psum_scatter(columns[3], 'dp', scatter_dimension=0, tiled=True)  75.7 us
    all_gather x1, waiting for transfers between devices, body(): lax.all_gather(halves[3], 'shard', axis=1, tiled=True)  62.9 us
    gather x2, local copies, waits for them, and re-layouts, body(): table_bias = jnp.take(position, index, axis=0).transpose(2, 0, 1)  55.2 us
    sub x2, other arithmetic, micro_step(): grad_probs - jnp.sum(probs * grad_probs, axis=-1, keepdims=True)  54.6 us
  transfers between devices with their start and end apart: 16, of which 7 were waited for; matrix products, arithmetic and copies ran while one was open for 45% of the time, Pallas kernels for 0%

commit v1 on v0

--- a/solution.py
+++ b/solution.py
@@ -1,11 +1,12 @@
 import jax
 import jax.numpy as jnp
 from jax import lax
+from jax.experimental import pallas as pl
+from jax.experimental.pallas import tpu as pltpu
 from jax.sharding import PartitionSpec as P
 
 HD = 32
 WIN = 12
-MB = 2
 STEP = 10
 HEADS = 24
 GRID = 24
@@ -50,22 +51,219 @@
     return layout.reshape(images, GRID * GRID, channels)
 
 
-def relative_index():
-    places = jnp.arange(WIN * WIN, dtype=jnp.int32)
-    row_of = places // WIN
-    column = places % WIN
-    return (row_of[:, None] - row_of[None, :] + WIN - 1) * (2 * WIN - 1) + (
-        column[:, None] - column[None, :] + WIN - 1
-    )
-
-
-def window_allowed(regions):
-    labels = (
+def window_labels(regions):
+    return (
         regions.reshape(GRID // WIN, WIN, GRID // WIN, WIN)
         .transpose(0, 2, 1, 3)
         .reshape((GRID // WIN) ** 2, WIN * WIN)
     )
-    return labels[:, :, None] == labels[:, None, :]
+
+
+AREA = WIN * WIN
+SPAN = 2 * WIN - 1
+REACH = 384
+TABLE_PAD = 640
+HEAD_STEP = 4
+CENTRE = (WIN - 1) * SPAN + WIN - 1
+
+
+def dot00(left, right):
+    return lax.dot_general(
+        left, right, (((0,), (0,)), ((), ())), preferred_element_type=jnp.float32
+    )
+
+
+def dot11(left, right):
+    return lax.dot_general(
+        left, right, (((1,), (1,)), ((), ())), preferred_element_type=jnp.float32
+    )
+
+
+def dot10(left, right):
+    return lax.dot_general(
+        left, right, (((1,), (0,)), ((), ())), preferred_element_type=jnp.float32
+    )
+
+
+def spread_places(shape, table_dim, token_dim):
+    token = lax.broadcasted_iota(jnp.int32, shape, token_dim)
+    place = lax.broadcasted_iota(jnp.int32, shape, table_dim)
+    token_row = token // WIN
+    return place == token + (SPAN - WIN) * token_row
+
+
+def bias_kernel(table_ref, bias_ref):
+    spot = spread_places((REACH, AREA), 0, 1).astype(jnp.bfloat16)
+    table = table_ref[...]
+    for row in range(WIN):
+        rolled = []
+        for column in range(WIN):
+            back = SPAN * (WIN - 1 - row) + WIN - 1 - column
+            rolled.append(pltpu.roll(table, (TABLE_PAD - back) % TABLE_PAD, 1)[:, :REACH])
+        block = jnp.concatenate(rolled, axis=0)
+        high = block.astype(jnp.bfloat16)
+        rest = block - high.astype(jnp.float32)
+        middle = rest.astype(jnp.bfloat16)
+        low = (rest - middle.astype(jnp.float32)).astype(jnp.bfloat16)
+        picked = dot10(high, spot) + (dot10(middle, spot) + dot10(low, spot))
+        for column in range(WIN):
+            bias_ref[row * WIN + column] = picked[column * HEADS : (column + 1) * HEADS]
+
+
+def table_kernel(scores_ref, table_ref):
+    spot = spread_places((AREA, REACH), 1, 0).astype(jnp.bfloat16)
+    total = jnp.zeros((HEADS, TABLE_PAD), jnp.float32)
+    for row in range(WIN):
+        block = scores_ref[row * WIN : (row + 1) * WIN].reshape(WIN * HEADS, AREA)
+        high = block.astype(jnp.bfloat16)
+        low = (block - high.astype(jnp.float32)).astype(jnp.bfloat16)
+        spread = dot10(high, spot) + dot10(low, spot)
+        inner = spread[:HEADS]
+        for column in range(1, WIN):
+            inner = pltpu.roll(inner, 1, 1) + spread[column * HEADS : (column + 1) * HEADS]
+        inner = jnp.concatenate(
+            [inner, jnp.zeros((HEADS, TABLE_PAD - REACH), jnp.float32)], axis=1
+        )
+        if row:
+            total = pltpu.roll(total, SPAN, 1)
+        total = total + inner
+    table_ref[...] = total
+
+
+def table_to_bias(position):
+    rows = position.shape[0]
+    table = jnp.pad(position.T, ((0, 0), (0, TABLE_PAD - rows)))
+    spread = pl.pallas_call(
+        bias_kernel,
+        out_shape=jax.ShapeDtypeStruct((AREA, HEADS, AREA), jnp.float32),
+        name="bias_kernel",
+    )(table)
+    return spread.transpose(1, 0, 2)
+
+
+def scores_to_table(scores, rows):
+    table = pl.pallas_call(
+        table_kernel,
+        out_shape=jax.ShapeDtypeStruct((HEADS, TABLE_PAD), jnp.float32),
+        name="table_kernel",
+    )(scores.transpose(1, 0, 2))
+    return table[:, :rows].T
+
+
+def scores_of(keyed, query, bias, allowed):
+    return jnp.where(allowed, dot00(keyed, query) * HD ** (-0.5) + bias, masked_score)
+
+
+def head_slices(ref, head):
+    width = HEADS * HD
+    return tuple(
+        ref[0, pl.ds(pl.multiple_of(block * width + head * HD, HD), HD), :] for block in range(3)
+    )
+
+
+def forward_kernel(triple_ref, bias_ref, label_ref, column_ref, mixed_ref, log_ref):
+    allowed = column_ref[0] == label_ref[0]
+
+    def step(group, carry):
+        for member in range(HEAD_STEP):
+            head = group * HEAD_STEP + member
+            query, keyed, valued = head_slices(triple_ref, head)
+            scores = scores_of(keyed, query, bias_ref[head], allowed)
+            top = jnp.max(scores, axis=0, keepdims=True)
+            raised = jnp.exp(scores - top)
+            total = jnp.sum(raised, axis=0, keepdims=True)
+            probs = (raised * (1.0 / total)).astype(jnp.bfloat16)
+            mixed_ref[0, pl.ds(pl.multiple_of(head * HD, HD), HD), :] = dot10(
+                valued, probs
+            ).astype(jnp.bfloat16)
+            log_ref[0, head] = top + jnp.log(total)
+        return carry
+
+    lax.fori_loop(0, HEADS // HEAD_STEP, step, 0)
+
+
+def backward_kernel(
+    triple_ref, grad_ref, log_ref, bias_ref, label_ref, column_ref, out_ref, scores_ref
+):
+    allowed = column_ref[0] == label_ref[0]
+    width = HEADS * HD
+
+    @pl.when(pl.program_id(0) == 0)
+    def _():
+        scores_ref[...] = jnp.zeros_like(scores_ref)
+
+    def step(group, carry):
+        for member in range(HEAD_STEP):
+            head = group * HEAD_STEP + member
+            query, keyed, valued = head_slices(triple_ref, head)
+            grad = grad_ref[0, pl.ds(pl.multiple_of(head * HD, HD), HD), :]
+            scores = scores_of(keyed, query, bias_ref[head], allowed)
+            probs = jnp.exp(scores - log_ref[0, head])
+            grad_probs = dot00(valued, grad)
+            weighted = probs * grad_probs
+            mean = jnp.sum(weighted, axis=0, keepdims=True)
+            grad_scores = jnp.where(allowed, weighted - probs * mean, 0.0)
+            scores_ref[head] += grad_scores
+            raw = (grad_scores * HD ** (-0.5)).astype(jnp.bfloat16)
+            results = (
+                dot10(keyed, raw),
+                dot11(query, raw),
+                dot11(grad, probs.astype(jnp.bfloat16)),
+            )
+            for block in range(3):
+                rows = pl.ds(pl.multiple_of(block * width + head * HD, HD), HD)
+                out_ref[0, rows, :] = results[block].astype(jnp.bfloat16)
+        return carry
+
+    lax.fori_loop(0, HEADS // HEAD_STEP, step, 0)
+
+
+def window_block(rows):
+    return pl.BlockSpec((1, rows, AREA), lambda window: (window, 0, 0))
+
+
+def label_blocks(count):
+    return [
+        pl.BlockSpec((1, 1, AREA), lambda window: (window % count, 0, 0)),
+        pl.BlockSpec((1, AREA, 1), lambda window: (window % count, 0, 0)),
+    ]
+
+
+def attend_forward(triple, bias, labels):
+    windows = triple.shape[0]
+    width = HEADS * HD
+    whole = pl.BlockSpec((HEADS, AREA, AREA), lambda window: (0, 0, 0))
+    log_block = pl.BlockSpec((1, HEADS, 1, AREA), lambda window: (window, 0, 0, 0))
+    return pl.pallas_call(
+        forward_kernel,
+        grid=(windows,),
+        in_specs=[window_block(3 * width), whole] + label_blocks(labels.shape[0]),
+        out_specs=[window_block(width), log_block],
+        out_shape=[
+            jax.ShapeDtypeStruct((windows, width, AREA), jnp.bfloat16),
+            jax.ShapeDtypeStruct((windows, HEADS, 1, AREA), jnp.float32),
+        ],
+        name="forward_kernel",
+    )(triple, bias, labels[:, None, :], labels[:, :, None])
+
+
+def attend_backward(triple, grad, log_total, bias, labels):
+    windows = triple.shape[0]
+    width = HEADS * HD
+    whole = pl.BlockSpec((HEADS, AREA, AREA), lambda window: (0, 0, 0))
+    log_block = pl.BlockSpec((1, HEADS, 1, AREA), lambda window: (window, 0, 0, 0))
+    return pl.pallas_call(
+        backward_kernel,
+        grid=(windows,),
+        in_specs=[window_block(3 * width), window_block(width), log_block, whole]
+        + label_blocks(labels.shape[0]),
+        out_specs=[window_block(3 * width), whole],
+        out_shape=[
+            jax.ShapeDtypeStruct((windows, 3 * width, AREA), jnp.bfloat16),
+            jax.ShapeDtypeStruct((HEADS, AREA, AREA), jnp.float32),
+        ],
+        name="backward_kernel",
+    )(triple, grad, log_total, bias, labels[:, None, :], labels[:, :, None])
 
 
 def product_left(left, right):
@@ -80,44 +278,27 @@
     )
 
 
-def masked(tensor, allowed, images, filler):
-    shaped = tensor.reshape(images, allowed.shape[0], HEADS, WIN * WIN, WIN * WIN)
-    return jnp.where(allowed[None, :, None], shaped, filler).reshape(tensor.shape)
-
-
-def attention_scores(query, keyed, table_bias, allowed, images):
-    raw = jnp.einsum("wihd,wjhd->whij", query, keyed, preferred_element_type=jnp.float32)
-    return masked(raw * HD ** (-0.5) + table_bias[None], allowed, images, masked_score)
-
-
-def micro_step(
-    values_low, cot_low, full, gains, shifts, biases, table_bias, allowed, index, table_rows
-):
+def whole_step(values_low, cot_low, full, gains, shifts, biases, bias, labels, table_rows):
     attend, project, expand, contract = full
-    images = values_low.shape[0]
     width = attend.shape[0]
     hidden_width = expand.shape[1]
-    windows_count = images * allowed.shape[0]
+    windows = values_low.shape[0] // AREA
     values = values_low.astype(jnp.float32)
     normed, norm_back = jax.vjp(layer_norm, values, gains[0], shifts[0])
-    windowed = to_windows(normed.astype(jnp.bfloat16)).reshape(-1, width)
-    triple = jnp.dot(windowed, attend, preferred_element_type=jnp.float32) + biases[: 3 * width]
-    triple = triple.astype(jnp.bfloat16).reshape(windows_count, WIN * WIN, 3, HEADS, HD)
-    query = triple[:, :, 0]
-    keyed = triple[:, :, 1]
-    valued = triple[:, :, 2]
-    scores = attention_scores(query, keyed, table_bias, allowed, images)
-    log_total = jax.nn.logsumexp(scores, axis=-1, keepdims=True)
-    probs_low = jnp.exp(scores - log_total).astype(jnp.bfloat16)
-    mixed = jnp.einsum("whij,wjhd->wihd", probs_low, valued, preferred_element_type=jnp.float32)
-    mixed_low = mixed.reshape(windows_count, WIN * WIN, width).astype(jnp.bfloat16)
-    merged = from_windows(mixed_low, images).reshape(-1, width)
+    normed_low = normed.astype(jnp.bfloat16)
+    windowed = normed_low.reshape(windows, AREA, width)
+    triple = jnp.einsum("wtc,ce->wet", windowed, attend, preferred_element_type=jnp.float32)
+    triple = (triple + biases[: 3 * width][None, :, None]).astype(jnp.bfloat16)
+    mixed, log_total = attend_forward(triple, bias, labels)
     branch = (
-        jnp.dot(merged, project, preferred_element_type=jnp.float32) + biases[3 * width : 4 * width]
-    )
-    middle = values + branch.reshape(values.shape)
+        jnp.einsum("wct,ce->wte", mixed, project, preferred_element_type=jnp.float32).reshape(
+            -1, width
+        )
+        + biases[3 * width : 4 * width]
+    )
+    middle = values + branch
     normed_two, norm_two_back = jax.vjp(layer_norm, middle, gains[1], shifts[1])
-    normed_two_low = normed_two.astype(jnp.bfloat16).reshape(-1, width)
+    normed_two_low = normed_two.astype(jnp.bfloat16)
     hidden = (
         jnp.dot(normed_two_low, expand, preferred_element_type=jnp.float32)
         + biases[4 * width : 4 * width + hidden_width]
@@ -127,54 +308,35 @@
     result = middle + (
         jnp.dot(active_low, contract, preferred_element_type=jnp.float32)
         + biases[4 * width + hidden_width :]
-    ).reshape(values.shape)
-    cot_rows = cot_low.reshape(-1, width)
-    cot_float = cot_rows.astype(jnp.float32)
-    grad_contract = product_left(active_low, cot_rows)
+    )
+    cot_float = cot_low.astype(jnp.float32)
+    grad_contract = product_left(active_low, cot_low)
     grad_bias_contract = jnp.sum(cot_float, axis=0)
-    grad_active = product_right(cot_rows, contract)
+    grad_active = product_right(cot_low, contract)
     grad_hidden_low = gelu_back(grad_active)[0].astype(jnp.bfloat16)
     grad_expand = product_left(normed_two_low, grad_hidden_low)
     grad_bias_expand = jnp.sum(grad_hidden_low, axis=0, dtype=jnp.float32)
-    grad_normed_two = product_right(grad_hidden_low, expand).reshape(values.shape)
+    grad_normed_two = product_right(grad_hidden_low, expand)
     grad_middle_part, grad_gain_two, grad_shift_two = norm_two_back(grad_normed_two)
-    grad_middle = cot_float.reshape(values.shape) + grad_middle_part
-    grad_branch_low = grad_middle.reshape(-1, width).astype(jnp.bfloat16)
-    grad_project = product_left(merged, grad_branch_low)
+    grad_middle = cot_float + grad_middle_part
+    grad_branch_low = grad_middle.astype(jnp.bfloat16)
+    grad_branch_windows = grad_branch_low.reshape(windows, AREA, width)
+    grad_project = jnp.einsum(
+        "wct,wte->ce", mixed, grad_branch_windows, preferred_element_type=jnp.float32
+    )
     grad_bias_project = jnp.sum(grad_branch_low, axis=0, dtype=jnp.float32)
-    grad_merged_low = (
-        product_right(grad_branch_low, project).astype(jnp.bfloat16).reshape(values.shape)
-    )
-    grad_mixed = to_windows(grad_merged_low).reshape(windows_count, WIN * WIN, HEADS, HD)
-    scores_again = attention_scores(query, keyed, table_bias, allowed, images)
-    probs = jnp.exp(scores_again - log_total)
-    probs_again = probs.astype(jnp.bfloat16)
-    grad_probs = jnp.einsum(
-        "wihd,wjhd->whij", grad_mixed, valued, preferred_element_type=jnp.float32
-    )
-    grad_valued = jnp.einsum(
-        "whij,wihd->wjhd", probs_again, grad_mixed, preferred_element_type=jnp.float32
-    )
-    grad_scores = probs * (grad_probs - jnp.sum(probs * grad_probs, axis=-1, keepdims=True))
-    grad_scores = masked(grad_scores, allowed, images, 0.0)
-    grad_table = jnp.sum(grad_scores, axis=0).transpose(1, 2, 0).reshape(-1, HEADS)
-    grad_position = jax.ops.segment_sum(grad_table, index.reshape(-1), num_segments=table_rows)
-    grad_raw_low = (grad_scores * HD ** (-0.5)).astype(jnp.bfloat16)
-    grad_query = jnp.einsum(
-        "whij,wjhd->wihd", grad_raw_low, keyed, preferred_element_type=jnp.float32
-    )
-    grad_keyed = jnp.einsum(
-        "whij,wihd->wjhd", grad_raw_low, query, preferred_element_type=jnp.float32
-    )
-    grad_triple_low = (
-        jnp.stack([grad_query, grad_keyed, grad_valued], axis=2)
-        .astype(jnp.bfloat16)
-        .reshape(-1, 3 * width)
-    )
-    grad_attend = product_left(windowed, grad_triple_low)
-    grad_bias_attend = jnp.sum(grad_triple_low, axis=0, dtype=jnp.float32)
-    grad_windowed = product_right(grad_triple_low, attend).reshape(windows_count, WIN * WIN, width)
-    grad_normed = from_windows(grad_windowed, images)
+    grad_mixed = jnp.einsum(
+        "wte,ce->wct", grad_branch_windows, project, preferred_element_type=jnp.float32
+    ).astype(jnp.bfloat16)
+    grad_triple, grad_scores = attend_backward(triple, grad_mixed, log_total, bias, labels)
+    grad_position = scores_to_table(grad_scores, table_rows)
+    grad_attend = jnp.einsum(
+        "wtc,wet->ce", windowed, grad_triple, preferred_element_type=jnp.float32
+    )
+    grad_bias_attend = jnp.sum(grad_triple, axis=(0, 2), dtype=jnp.float32)
+    grad_normed = jnp.einsum(
+        "wet,ce->wtc", grad_triple, attend, preferred_element_type=jnp.float32
+    ).reshape(-1, width)
     grad_input_part, grad_gain_one, grad_shift_one = norm_back(grad_normed)
     grad_input = grad_middle + grad_input_part
     grads = (
@@ -260,40 +422,24 @@
         lax.all_gather(expand.astype(jnp.bfloat16), "dp", axis=0, tiled=True),
         lax.all_gather(contract.astype(jnp.bfloat16), "dp", axis=0, tiled=True),
     )
-    allowed = window_allowed(regions)
-    index = relative_index()
-    table_bias = jnp.take(position, index, axis=0).transpose(2, 0, 1)
-    per_micro = inputs.shape[0] // MB
-    results = []
-    input_grads = []
-    totals = None
-    for micro_index in range(MB):
-        full = (
-            lax.all_gather(halves[0], "shard", axis=1, tiled=True),
-            lax.all_gather(halves[1], "shard", axis=1, tiled=True),
-            lax.all_gather(halves[2], "shard", axis=1, tiled=True),
-            lax.all_gather(halves[3], "shard", axis=1, tiled=True),
-        )
-        lower = micro_index * per_micro
-        upper = lower + per_micro
-        result_low, grad_input, grads = micro_step(
-            inputs[lower:upper],
-            cotangent[lower:upper],
-            full,
-            gains,
-            shifts,
-            biases,
-            table_bias,
-            allowed,
-            index,
-            position.shape[0],
-        )
-        results.append(result_low)
-        input_grads.append(grad_input)
-        if totals is None:
-            totals = grads
-        else:
-            totals = tuple((before + after for before, after in zip(totals, grads)))
+    labels = window_labels(regions)
+    bias = table_to_bias(position)
+    images = inputs.shape[0]
+    width = inputs.shape[2]
+    full = tuple(lax.all_gather(half, "shard", axis=1, tiled=True) for half in halves)
+    result_low, grad_input, totals = whole_step(
+        to_windows(inputs).reshape(-1, width),
+        to_windows(cotangent).reshape(-1, width),
+        full,
+        gains,
+        shifts,
+        biases,
+        bias,
+        labels,
+        position.shape[0],
+    )
+    result_low = from_windows(result_low, images)
+    grad_input = from_windows(grad_input, images)
     totals = tuple((entry / tokens_all for entry in totals))
     small_grads = totals[4:]
     small_total = lax.psum(
@@ -331,9 +477,9 @@
             for slot in range(4)
         ]
     )
-    squares = lax.psum(partial_value, ("dp", "shard"))
+    squares = jnp.sum(lax.all_gather(partial_value, ("dp", "shard")), axis=0)
     matrix_norms = jnp.sqrt(squares)
-    outputs = [jnp.concatenate(results, axis=0), jnp.concatenate(input_grads, axis=0)]
+    outputs = [result_low, grad_input]
     pairs = []
     for slot in range(4):
         momentum, variance, update = pieces[slot]

time: 1440 us -> 1240 us (0.86)
  other arithmetic: 398 us -> 112 us
  local copies, waits for them, and re-layouts: 310 us -> 131 us
  waiting for transfers between devices: 435 us -> 586 us
  Pallas kernels: 0 us -> 132 us
  matrix products: 237 us -> 155 us
  blocking collectives: 22.8 us -> 87.8 us
    scatter-add x2 -> x0, other arithmetic: 226 us -> none  [micro_step(): jax.ops.segment_sum(grad_table, index.reshape(-1), num_segments=table_rows)]
    pallas_call x0 -> x4, Pallas kernels: none -> 132 us  [the longest x1 62.3 us: attend_backward(): pl.pallas_call(backward_kernel, grid=(windows,), in_specs=[window_block(3...]
    convert_element_type x14 -> x4, local copies, waits for them, and re-layouts: 117 us -> 15.3 us  [the longest x3 12.5 us: whole_step(): values = values_low.astype(jnp.float32)]
    reduce_scatter x1, waiting for transfers between devices: 0.01 us -> 75.1 us  [body(): lax.psum_scatter(columns[2], 'dp', scatter_dimension=0, tiled=True)]
    reduce_scatter x1, waiting for transfers between devices: 0.01 us -> 68 us  [body(): lax.psum_scatter(columns[0], 'dp', scatter_dimension=0, tiled=True)]
    all_gather x0 -> x1, blocking collectives: none -> 65.1 us  [body(): squares = jnp.sum(lax.all_gather(partial_value, ('dp', 'shard')), axis=0)]
    gather x2 -> x0, local copies, waits for them, and re-layouts: 55.2 us -> none  [body(): table_bias = jnp.take(position, index, axis=0).transpose(2, 0, 1)]
    dot_general x20 -> x8, matrix products: 159 us -> 104 us  [the longest x1 41.8 us: whole_step(): jnp.dot(normed_two_low, expand, preferred_element_type=jnp.float32)]
  transfers between devices with their start and end apart: 16 -> 16, of which waited for: 7 -> 11; matrix products, arithmetic and copies ran while one was open for 45% -> 22% of each run, Pallas kernels for 0% -> 11%
where the time goes in v1:
time: 1240 us; the launch traced here: 1230 us
  waiting for transfers between devices  586 us (47%)
  matrix products  155 us (12%)
  Pallas kernels  132 us (11%)
  local copies, waits for them, and re-layouts  131 us (11%)
  other arithmetic  112 us (9%)
  blocking collectives  87.8 us (7%)
  between operations  26.6 us (2%)
    reduce_scatter x1, waiting for transfers between devices, body(): lax.psum_scatter(columns[3], 'dp', scatter_dimension=0, tiled=True)  75.7 us
    reduce_scatter x1, waiting for transfers between devices, body(): lax.psum_scatter(columns[2], 'dp', scatter_dimension=0, tiled=True)  75.1 us
    psum x1, waiting for transfers between devices, body(): lax.psum((small_grads[0], small_grads[1], small_grads[2], small_grads[3])...  73.4 us
    all_gather x4, waiting for transfers between devices, body(): lax.all_gather(half, 'shard', axis=1, tiled=True)  68.5 us
    reduce_scatter x1, waiting for transfers between devices, body(): lax.psum_scatter(columns[0], 'dp', scatter_dimension=0, tiled=True)  68 us
    all_gather x1, blocking collectives, body(): squares = jnp.sum(lax.all_gather(partial_value, ('dp', 'shard')), axis=0)  65.1 us
    pallas_call x1, Pallas kernels, attend_backward(): pl.pallas_call(backward_kernel, grid=(windows,), in_specs=[window_block(3...  62.3 us
    unnamed x19, waiting for transfers between devices  60.5 us
  transfers between devices with their start and end apart: 16, of which 11 were waited for; matrix products, arithmetic and copies ran while one was open for 22% of the time, Pallas kernels for 11%

profile of v1, /device:TPU:0, one launch (start us, length us, event | category | flops | bytes accessed | tf_op | source)
XLA Modules:
  0.0 1232.1 jit_solution(7508005899861670952)
XLA Ops:
  10.8 43.0 %all-gather.10.cloned.1.call-done = bf16[768,1152]{1,0:T(8,128)(2,1)} async-done(((bf16[48,1152]{1,0:T(8,128)(2,1)}), bf16[768,1152]{1,0:T(8,128)(2,1)}) %all-gather.10.cloned.1.call-update) | async-done | bytes 1769488 | tf_op jit(solution)/shard_map/all_gather | solution.py:420
  54.8 22.8 %all_gather.32 = bf16[768,384]{1,0:T(8,128)(2,1)} all-gather(bf16[48,384]{1,0:T(8,128)(2,1)S(1)} %convert_element_type.136), channel_id=1, replica_groups=mesh['dp'=16,'shard'=2] {'dp'}, dimensions={0}, use_global_device_ids=true | all-gather | bytes 626688 | tf_op jit(solution)/shard_map/all_gather | solution.py:421
  120.7 5.8 bias_kernel.1
  142.1 5.6 all-gather.12.cloned.1.call-done
  147.8 13.3 %fusion.6.triple_ref = bf16[8,2304,144]{2,1,0:T(8,128)(2,1)} fusion(f32[2304]{0:T(1024)S(1)} %slice-done, bf16[768,2304]{1,0:T(8,128)(2,1)} %all-gather.12.cloned.1.call-done, f32[8,144,768]{2,1,0:T(8,128)} %reshape.367, f32[768]{0:T(1024)} %get-tuple-element.153, f32[768]{0:T(1024)} %get-tuple-element.211, f32[8,144]{1,0:T(8,128)} %rsqrt.24, ...), kind=kOutput, calls=%fused_computation.21 | convolution fusion | flops 4086595584 | bytes 12410880 | tf_op jit(solution)/shard_map/wtc,ce->wet/dot_general | solution.py:290
  161.1 58.1 %forward_kernel.1 = (bf16[8,768,144]{2,1,0:T(8,128)(2,1)}, f32[8,24,1,144]{3,2,1,0:T(1,128)}) custom-call(bf16[8,2304,144]{2,1,0:T(8,128)(2,1)} %fusion.6.triple_ref, f32[24,144,144]{2,1,0:T(8,128)} %bitcast.134, s32[4,1,144]{2,1,0:T(1,128)} %broadcast_in_dim_reshape.10.label_ref, s32[4,144,1]{2,1,0:T(8,128)} %broadcast_in_dim_reshape.11.column_ref), custom_call_target="tpu_custom_call" | custom-call | tf_op jit(solution)/shard_map/forward_kernel/pallas_call | solution.py:237
  219.2 5.6 fusion.27
  237.9 7.9 multiply_reduce_fusion.3
  253.6 41.8 %multiply_convert_fusion = (bf16[1152,3072]{1,0:T(8,128)(2,1)S(1)}, f32[1152,3072]{1,0:T(8,128)}, f32[1152,3072]{1,0:T(8,128)}) fusion(f32[3072]{0:T(1024)S(1)} %slice-done.1, bf16[768,3072]{1,0:T(8,128)(2,1)} %all-gather.18.cloned.1.call-done, f32[1152,768]{1,0:T(8,128)} %fusion.16, f32[768]{0:T(1024)S(1)} %copy-done.75, f32[768]{0:T(1024)S(1)} %copy-done.66, ...), kind=kOutput, calls=%fused_computation.6 | convolution fusion | flops 5673811968 | bytes 43674624 | tf_op jit(solution)/shard_map/dot_general | solution.py:303
  298.2 8.2 multiply_convert_fusion.1
  306.4 6.6 copy.215
  313.1 60.2 %reduce-scatter.29.cloned.1.call-done = bf16[384,3072]{1,0:T(8,128)(2,1)} async-done(((bf16[768,3072]{1,0:T(8,128)(2,1)}), bf16[384,3072]{1,0:T(8,128)(2,1)}) %reduce-scatter.29.cloned.1.call-update) | async-done | bytes 2359312
  381.8 75.7 %reduce-scatter.23.cloned.1.call-done = f32[192,384]{1,0:T(8,128)} async-done(((f32[3072,384]{1,0:T(8,128)}), f32[192,384]{1,0:T(8,128)}) %reduce-scatter.23.cloned.1.call-update) | async-done | bytes 294928 | tf_op jit(solution)/shard_map/reduce_scatter | solution.py:466
  460.1 41.7 %all-gather.20.cloned.1.call-done = bf16[3072,384]{1,0:T(8,128)(2,1)} async-done(((bf16[192,384]{1,0:T(8,128)(2,1)}), bf16[3072,384]{1,0:T(8,128)(2,1)}) %all-gather.20.cloned.1.call-update) | async-done | bytes 2359312 | tf_op jit(solution)/shard_map/all_gather | solution.py:423
  501.9 62.9 %all-gather.22.cloned.1.call-done = bf16[3072,768]{1,0:T(8,128)(2,1)} async-done(((bf16[3072,384]{1,0:T(8,128)(2,1)}), bf16[3072,768]{1,0:T(8,128)(2,1)}) %all-gather.22.cloned.1.call-update) | async-done | bytes 4718608 | tf_op jit(solution)/shard_map/all_gather | solution.py:429
  564.7 19.0 %convert_reduce_fusion.1 = (f32[3072]{0:T(1024)}, bf16[1152,3072]{1,0:T(8,128)(2,1)}) fusion(f32[1152,3072]{1,0:T(8,128)} %get-tuple-element.191, f32[1152,3072]{1,0:T(8,128)} %get-tuple-element.207, bf16[1152,768]{1,0:T(8,128)(2,1)S(1)} %reshape_reshape.4, bf16[3072,768]{1,0:T(8,128)(2,1)} %all-gather.22.cloned.1.call-done), kind=kOutput, calls=%fused_computation.4 | convolution fusion | flops 5492438016 | bytes 41889792 | tf_op jit(solution)/shard_map/dot_general | solution.py:276
  583.8 12.8 %multiply_reduce_fusion = (f32[768]{0:T(1024)}, f32[1152]{0:T(1024)S(1)}, f32[768]{0:T(1024)}, f32[1152,768]{1,0:T(8,128)S(1)}) fusion(f32[1152,768]{1,0:T(8,128)} %fusion.16, f32[1152]{0:T(1024)S(1)} %rsqrt.25, f32[1152]{0:T(1024)S(1)} %div.241, f32[768]{0:T(1024)S(1)} %copy-done.66, bf16[1152,3072]{1,0:T(8,128)(2,1)} %get-tuple-element.210, ...), kind=kOutput, calls=%fused_computation.53 | convolution fusion | flops 5442892800 | bytes 18897408 | tf_op jit(solution)/shard_map/dot_general | solution.py:276
  611.2 62.3 %backward_kernel.1 = (bf16[8,2304,144]{2,1,0:T(8,128)(2,1)}, f32[24,144,144]{2,1,0:T(8,128)}) custom-call(bf16[8,2304,144]{2,1,0:T(8,128)(2,1)} %fusion.6.triple_ref, bf16[8,768,144]{2,1,0:T(8,128)(2,1)} %bitcast.145, f32[8,24,1,144]{3,2,1,0:T(1,128)} %get-tuple-element.36.log_ref, f32[24,144,144]{2,1,0:T(8,128)} %bitcast.135, ...), custom_call_target="tpu_custom_call" | custom-call | tf_op jit(solution)/shard_map/backward_kernel/pallas_call | solution.py:255
  673.5 13.7 %fusion.7 = bf16[768,2304]{1,0:T(8,128)(2,1)} fusion(bf16[8,2304,144]{2,1,0:T(8,128)(2,1)} %get-tuple-element.37, f32[8,144,768]{2,1,0:T(8,128)S(1)} %copy-done.10, f32[768]{0:T(1024)S(1)} %copy-done.76, f32[768]{0:T(1024)S(1)} %copy-done.55, f32[8,144]{1,0:T(8,128)} %rsqrt.24, f32[8,144]{1,0:T(8,128)} %div.238), kind=kOutput, calls=%fused_computation.25 | convolution fusion | flops 4084826112 | bytes 12401664 | tf_op jit(solution)/shard_map/wtc,wet->ce/dot_general | solution.py:333
  687.2 5.7 copy.211
  694.9 11.5 multiply_convert_fusion.2
  709.4 14.2 %fusion.17 = f32[8,144,768]{2,1,0:T(8,128)} fusion(bf16[8,2304,144]{2,1,0:T(8,128)(2,1)} %get-tuple-element.37, bf16[768,2304]{1,0:T(8,128)(2,1)} %all-gather.12.cloned.1.call-done), kind=kOutput, calls=%fused_computation.45 | convolution fusion | flops 4076863488 | bytes 12386304 | tf_op jit(solution)/shard_map/wet,ce->wtc/dot_general | solution.py:337
  728.6 7.5 fusion.20
  745.4 5.5 table_kernel.1
  769.6 33.9 %reduce-scatter.19.cloned.1.call-done = bf16[768,1536]{1,0:T(8,128)(2,1)} async-done(((bf16[768,3072]{1,0:T(8,128)(2,1)}), bf16[768,1536]{1,0:T(8,128)(2,1)}) %reduce-scatter.19.cloned.1.call-update) | async-done | bytes 2359312 | tf_op jit(solution)/shard_map/reduce_scatter | solution.py:455
  810.0 10.4 fusion.21
  835.9 5.6 fusion.10
  861.5 73.4 %all-reduce.4.cloned.1.call-done = (f32[2,768]{1,0:T(2,128)}, f32[2,768]{1,0:T(2,128)}, f32[6912]{0:T(1024)}, f32[529,24]{0,1:T(8,128)}) async-done(((f32[2,768]{1,0:T(2,128)}, f32[2,768]{1,0:T(2,128)}, f32[6912]{0:T(1024)}, f32[529,24]{0,1:T(8,128)}), (f32[2,768]{1,0:T(2,128)}, f32[2,768]{1,0:T(2,128)}, f32[6912]{0:T(1024)}, f32[529,24]{0,1:T(8,128)})) %all-reduce.4.cloned.1.call-update) | async-done | bytes 90736 | tf_op jit(solution)/shard_map/psum | solution.py:445
  950.7 46.8 %reduce-scatter.17.cloned.1.call-done = f32[48,384]{1,0:T(8,128)} async-done(((f32[768,384]{1,0:T(8,128)}), f32[48,384]{1,0:T(8,128)}) %reduce-scatter.17.cloned.1.call-update) | async-done | bytes 73744 | tf_op jit(solution)/shard_map/reduce_scatter | solution.py:464
  1000.4 68.0 %reduce-scatter.15.cloned.1.call-done = f32[48,1152]{1,0:T(8,128)} async-done(((f32[768,1152]{1,0:T(8,128)}), f32[48,1152]{1,0:T(8,128)}) %reduce-scatter.15.cloned.1.call-update) | async-done | bytes 221200 | tf_op jit(solution)/shard_map/reduce_scatter | solution.py:463
  1071.5 75.1 %reduce-scatter.21.cloned.1.call-done = f32[48,1536]{1,0:T(8,128)} async-done(((f32[768,1536]{1,0:T(8,128)}), f32[48,1536]{1,0:T(8,128)}) %reduce-scatter.21.cloned.1.call-update) | async-done | bytes 294928 | tf_op jit(solution)/shard_map/reduce_scatter | solution.py:465
  1149.9 65.1 %all-gather.1 = f32[32,4,2]{1,2,0:T(2,128)S(1)} all-gather(f32[1,4,2]{1,2,0:T(2,128)S(1)} %bitcast.162), channel_id=2, replica_groups=mesh['dp'=16,'shard'=2] {'dp','shard'}, dimensions={0}, use_global_device_ids=true | all-gather | bytes 1056 | tf_op jit(solution)/shard_map/all_gather | solution.py:480
  (340 shorter events, 216.0 us)
Async XLA Ops:
  7.2 46.6 %all-gather.10.cloned.1.call-start = ((), (), s32[]{:S(2)}) async-start(), calls=%async_computation.8 | async-start | bytes 1880064 | tf_op jit(solution)/shard_map/all_gather | solution.py:420
  9.0 133.1 %all-gather.16.cloned.1.call-start = ((), (), s32[]{:S(2)}) async-start(), calls=%async_computation.11 | async-start | bytes 2506752 | tf_op jit(solution)/shard_map/all_gather | solution.py:422
  10.7 137.0 %all-gather.12.cloned.1.call-start = ((), (), s32[]{:S(2)}) async-start(), calls=%async_computation.9 | async-start | bytes 5308416 | tf_op jit(solution)/shard_map/all_gather | solution.py:429
  53.8 165.4 %all-gather.14.cloned.1.call-start = ((), (), s32[]{:S(2)}) async-start(), calls=%async_computation.10 | async-start | bytes 1769472 | tf_op jit(solution)/shard_map/all_gather | solution.py:429
  77.6 176.0 %all-gather.18.cloned.1.call-start = ((), (), s32[]{:S(2)}) async-start(), calls=%async_computation.12 | async-start | bytes 7077888 | tf_op jit(solution)/shard_map/all_gather | solution.py:429
  139.2 458.7 %copy-start.6 = (bf16[1152,768]{1,0:T(8,128)(2,1)}, bf16[1152,768]{1,0:T(8,128)(2,1)S(1)}, u32[]{:S(2)}) copy-start(bf16[1152,768]{1,0:T(8,128)(2,1)S(1)} %reshape_reshape.4) | copy-start | bytes 5308420
  142.1 231.2 %reduce-scatter.29.cloned.1.call-start = ((), (), s32[]{:S(2)}) async-start(), calls=%async_computation.22 | async-start | bytes 7077888
  247.2 349.4 %copy-start.61 = (f32[1152]{0:T(1024)}, f32[1152]{0:T(1024)S(1)}, u32[]{:S(2)}) copy-start(f32[1152]{0:T(1024)S(1)} %rsqrt.25) | copy-start | bytes 13828
  248.1 348.5 %copy-start.60 = (f32[1152]{0:T(1024)}, f32[1152]{0:T(1024)S(1)}, u32[]{:S(2)}) copy-start(f32[1152]{0:T(1024)S(1)} %div.241) | copy-start | bytes 13828
  313.1 144.4 %reduce-scatter.23.cloned.1.call-start = ((), (), s32[]{:S(2)}) async-start(), calls=%async_computation.19 | async-start | bytes 5013504 | tf_op jit(solution)/shard_map/reduce_scatter | solution.py:466
  381.7 120.1 %all-gather.20.cloned.1.call-start = ((), (), s32[]{:S(2)}) async-start(), calls=%async_computation.13 | async-start | bytes 2506752 | tf_op jit(solution)/shard_map/all_gather | solution.py:423
  460.0 104.7 %all-gather.22.cloned.1.call-start = ((), (), s32[]{:S(2)}) async-start(), calls=%async_computation.14 | async-start | bytes 7077888 | tf_op jit(solution)/shard_map/all_gather | solution.py:429
  501.8 256.9 %reduce-scatter.27.cloned.1.call-start = ((), (), s32[]{:S(2)}) async-start(), calls=%async_computation.21 | async-start | bytes 1769472
  605.1 156.4 %reduce-scatter.25.cloned.1.call-start = ((), (), s32[]{:S(2)}) async-start(), calls=%async_computation.20 | async-start | bytes 5308416
  693.0 110.6 %reduce-scatter.19.cloned.1.call-start = ((), (), s32[]{:S(2)}) async-start(), calls=%async_computation.17 | async-start | bytes 7077888 | tf_op jit(solution)/shard_map/reduce_scatter | solution.py:455
  706.4 228.4 %all-reduce.4.cloned.1.call-start = ((), (), s32[]{:S(2)}) async-start(), calls=%async_computation.23 | async-start | bytes 204800 | tf_op jit(solution)/shard_map/psum | solution.py:445
  758.7 238.8 %reduce-scatter.17.cloned.1.call-start = ((), (), s32[]{:S(2)}) async-start(), calls=%async_computation.16 | async-start | bytes 1253376 | tf_op jit(solution)/shard_map/reduce_scatter | solution.py:464
  761.4 306.9 %reduce-scatter.15.cloned.1.call-start = ((), (), s32[]{:S(2)}) async-start(), calls=%async_computation.15 | async-start | bytes 3760128 | tf_op jit(solution)/shard_map/reduce_scatter | solution.py:463
  766.3 380.3 %reduce-scatter.21.cloned.1.call-start = ((), (), s32[]{:S(2)}) async-start(), calls=%async_computation.18 | async-start | bytes 5013504 | tf_op jit(solution)/shard_map/reduce_scatter | solution.py:465
  859.3 287.3 %copy-start.15 = (f32[48,1536]{1,0:T(8,128)S(1)}, f32[48,1536]{1,0:T(8,128)}, u32[]{:S(2)}) copy-start(f32[48,1536]{1,0:T(8,128)} %param.36) | copy-start | bytes 884740
  859.4 287.2 %copy-start.39 = (f32[48,1536]{1,0:T(8,128)S(1)}, f32[48,1536]{1,0:T(8,128)}, u32[]{:S(2)}) copy-start(f32[48,1536]{1,0:T(8,128)} %param.37) | copy-start | bytes 884740
  859.4 287.2 %copy-start.40 = (f32[48,1536]{1,0:T(8,128)S(1)}, f32[48,1536]{1,0:T(8,128)}, u32[]{:S(2)}) copy-start(f32[48,1536]{1,0:T(8,128)} %param.38) | copy-start | bytes 884740
  861.5 288.3 %copy-start.80 = (f32[1,2]{1,0:T(1,128)S(1)}, f32[1,2]{1,0:T(1,128)}, u32[]{:S(2)}) copy-start(f32[1,2]{1,0:T(1,128)} %maximum_bitcast_fusion.3) | copy-start | bytes 28
  942.9 280.6 %copy-start.47 = (f32[6912]{0:T(1024)}, f32[6912]{0:T(1024)S(1)}, u32[]{:S(2)}) copy-start(f32[6912]{0:T(1024)S(1)} %get-tuple-element.160) | copy-start | bytes 82948
  942.9 280.6 %copy-start.48 = (f32[6912]{0:T(1024)}, f32[6912]{0:T(1024)S(1)}, u32[]{:S(2)}) copy-start(f32[6912]{0:T(1024)S(1)} %get-tuple-element.161) | copy-start | bytes 82948
  944.3 279.2 %copy-start.23 = (f32[192,384]{1,0:T(8,128)S(1)}, f32[192,384]{1,0:T(8,128)}, u32[]{:S(2)}) copy-start(f32[192,384]{1,0:T(8,128)} %param.39) | copy-start | bytes 884740
  944.3 279.2 %copy-start.24 = (f32[192,384]{1,0:T(8,128)S(1)}, f32[192,384]{1,0:T(8,128)}, u32[]{:S(2)}) copy-start(f32[192,384]{1,0:T(8,128)} %get-tuple-element.186) | copy-start | bytes 884740
  944.3 279.1 %copy-start.25 = (f32[192,384]{1,0:T(8,128)S(1)}, f32[192,384]{1,0:T(8,128)}, u32[]{:S(2)}) copy-start(f32[192,384]{1,0:T(8,128)} %get-tuple-element.187) | copy-start | bytes 884740
  945.9 278.5 %copy-start.42 = (f32[529,24]{0,1:T(8,128)}, f32[529,24]{0,1:T(8,128)S(1)}, u32[]{:S(2)}) copy-start(f32[529,24]{0,1:T(8,128)S(1)} %get-tuple-element.158) | copy-start | bytes 152356
  945.9 278.5 %copy-start.43 = (f32[529,24]{0,1:T(8,128)}, f32[529,24]{0,1:T(8,128)S(1)}, u32[]{:S(2)}) copy-start(f32[529,24]{0,1:T(8,128)S(1)} %get-tuple-element.159) | copy-start | bytes 152356
  999.0 225.4 %copy-start.37 = (f32[48,384]{1,0:T(8,128)}, f32[48,384]{1,0:T(8,128)S(1)}, u32[]{:S(2)}) copy-start(f32[48,384]{1,0:T(8,128)S(1)} %get-tuple-element.182) | copy-start | bytes 221188
  999.0 225.4 %copy-start.38 = (f32[48,384]{1,0:T(8,128)}, f32[48,384]{1,0:T(8,128)S(1)}, u32[]{:S(2)}) copy-start(f32[48,384]{1,0:T(8,128)S(1)} %get-tuple-element.183) | copy-start | bytes 221188
  (69 other events, 3322.7 us)
Sparse Core Ops, SparseCore 0:
  10.8 42.9 all-gather.9
  56.6 41.4 all-gather.15
  99.7 48.0 all-gather.11
  149.1 22.7 all-gather.13
  173.3 62.6 all-gather.17
  313.2 60.0 reduce-scatter.28
  381.8 75.5 reduce-scatter.22
  460.3 41.4 all-gather.19
  503.4 61.3 all-gather.21
  605.2 21.8 reduce-scatter.26
  693.1 48.1 reduce-scatter.24
  743.4 60.0 reduce-scatter.18
  810.8 124.0 all-reduce.3
  938.3 59.1 reduce-scatter.16
  1001.2 67.1 reduce-scatter.14
  1072.1 74.4 reduce-scatter.20

commit v2 on v1

--- a/solution.py
+++ b/solution.py
@@ -352,6 +352,409 @@
         grad_position,
     )
     return (result.astype(jnp.bfloat16), grad_input, grads)
+
+
+ZS = 4
+SPLIT = 2
+GROUPS = ((0, 1, 2), (3, 4))
+PARTS = ((0, None), (1, None), (3, 0), (2, None), (3, 1))
+
+
+def special_mesh(dp_count, shard_count):
+    return dp_count == ZS * SPLIT * SPLIT and shard_count == SPLIT
+
+
+def places():
+    at = lax.axis_index("dp")
+    return at // 4, lax.rem(at // 2, 2), lax.rem(at, 2), lax.axis_index("shard")
+
+
+def far_z(z, step):
+    return (z, z + 1 - 2 * lax.rem(z, 2), lax.rem(z + 2, 4), 3 - z)[step]
+
+
+def device(z, y, c, x):
+    return {"dp": (z * 2 + y) * 2 + c, "shard": x}
+
+
+def partners(z, y, c, x):
+    return [device(far_z(z, step), y, c, x) for step in (1, 2, 3)] + [
+        device(z, y, c, 1 - x),
+        device(z, 1 - y, c, x),
+        device(z, y, 1 - c, x),
+    ]
+
+
+def greet(devices):
+    barrier = pltpu.get_barrier_semaphore()
+    for one in devices:
+        pl.semaphore_signal(
+            barrier, inc=1, device_id=one, device_id_type=pl.DeviceIdType.MESH
+        )
+    pl.semaphore_wait(barrier, len(devices))
+
+
+def remote(source, target, sends, receives, slot, where):
+    return pltpu.make_async_remote_copy(
+        src_ref=source,
+        dst_ref=target,
+        send_sem=sends.at[slot],
+        recv_sem=receives.at[slot],
+        device_id=where,
+        device_id_type=pl.DeviceIdType.MESH,
+    )
+
+
+def columns_of(ref, x):
+    half = ref.shape[-1] // 2
+    return pl.ds(pl.multiple_of(x * half, 128), half)
+
+
+def gather_kernel(*refs):
+    own, full = refs[:4], refs[4:8]
+    local_sem, sends, receives = refs[8:]
+    z, y, c, x = places()
+    greet(partners(z, y, c, x))
+    count = len(PARTS)
+
+    def own_part(part):
+        matrix, half = PARTS[part]
+        return own[matrix] if half is None else own[matrix].at[half]
+
+    def spot(part, zi, yi, cols):
+        matrix, half = PARTS[part]
+        ref = full[matrix]
+        if half is None:
+            return ref.at[zi, yi, c, :, cols]
+        return ref.at[zi, yi, c, half, :, cols]
+
+    everything = slice(None)
+    started = []
+
+    def launch(source, target, phase, step, part, where):
+        copy = remote(source, target, sends, receives, (phase * 4 + step) * count + part, where)
+        copy.start()
+        started.append(copy)
+        return copy
+
+    flights = {}
+    for step in (1, 2, 3):
+        for part in range(count):
+            cols = columns_of(full[PARTS[part][0]], x)
+            flights[0, step, part] = launch(
+                own_part(part),
+                spot(part, z, y, cols),
+                0,
+                step,
+                part,
+                device(far_z(z, step), y, c, x),
+            )
+    locals_ = []
+    for part in range(count):
+        cols = columns_of(full[PARTS[part][0]], x)
+        copy = pltpu.make_async_copy(own_part(part), spot(part, z, y, cols), local_sem.at[part])
+        copy.start()
+        locals_.append(copy)
+    for copy in locals_:
+        copy.wait()
+    across_x = device(z, y, c, 1 - x)
+    across_y = device(z, 1 - y, c, x)
+    across_core = device(z, y, 1 - c, x)
+
+    def second(step):
+        zi = far_z(z, step)
+        for part in range(count):
+            if step:
+                flights[0, step, part].wait_recv()
+            here = spot(part, zi, y, columns_of(full[PARTS[part][0]], x))
+            where = across_x if part in GROUPS[0] else across_y
+            flights[1, step, part] = launch(here, here, 1, step, part, where)
+
+    def third(step):
+        zi = far_z(z, step)
+        for part in range(count):
+            flights[1, step, part].wait_recv()
+            if part in GROUPS[0]:
+                here, where = spot(part, zi, y, everything), across_y
+            else:
+                cols = columns_of(full[PARTS[part][0]], x)
+                here, where = spot(part, zi, everything, cols), across_x
+            flights[2, step, part] = launch(here, here, 2, step, part, where)
+
+    def fourth(step):
+        zi = far_z(z, step)
+        for part in range(count):
+            flights[2, step, part].wait_recv()
+            here = spot(part, zi, everything, everything)
+            flights[3, step, part] = launch(here, here, 3, step, part, across_core)
+
+    for stage in range(4 + 2):
+        if stage < 4:
+            second(stage)
+        if 0 <= stage - 1 < 4:
+            third(stage - 1)
+        if 0 <= stage - 2 < 4:
+            fourth(stage - 2)
+    for step in range(4):
+        for part in range(count):
+            flights[3, step, part].wait_recv()
+    for copy in started:
+        copy.wait_send()
+
+
+def gather_all(shards):
+    rows = [shard.shape[0] for shard in shards]
+    cols = [shard.shape[1] * 2 for shard in shards]
+    own = list(shards[:3]) + [shards[3].reshape(2, rows[3] // 2, cols[3] // 2)]
+    shapes = [(ZS, 2, 2, rows[m], cols[m]) for m in range(3)] + [
+        (ZS, 2, 2, 2, rows[3] // 2, cols[3])
+    ]
+    anywhere = pl.BlockSpec(memory_space=pl.ANY)
+    slots = 16 * len(PARTS)
+    moved = sum(2 * ZS * 4 * rows[m] * cols[m] for m in range(4))
+    full = pl.pallas_call(
+        gather_kernel,
+        in_specs=[anywhere] * 4,
+        out_specs=[anywhere] * 4,
+        out_shape=[jax.ShapeDtypeStruct(shape, jnp.bfloat16) for shape in shapes],
+        scratch_shapes=[
+            pltpu.SemaphoreType.DMA((len(PARTS),)),
+            pltpu.SemaphoreType.DMA((slots,)),
+            pltpu.SemaphoreType.DMA((slots,)),
+        ],
+        compiler_params=pltpu.CompilerParams(collective_id=0, has_side_effects=True),
+        cost_estimate=pl.CostEstimate(flops=0, bytes_accessed=moved * 4, transcendentals=0),
+        name="gather_kernel",
+    )(*own)
+    return tuple(full[m].reshape(ZS * 4 * rows[m], cols[m]) for m in range(4))
+
+
+def add_rows(first, second, target):
+    rows = target.shape[0]
+
+    def step(index, carry):
+        at = pl.ds(pl.multiple_of(index * 16, 16), 16)
+        total = first(at).astype(jnp.float32) + second(at).astype(jnp.float32)
+        target[at, :] = total.astype(target.dtype)
+        return carry
+
+    lax.fori_loop(0, rows // 16, step, 0)
+
+
+def scatter_kernel(*refs):
+    count = len(PARTS)
+    grads, outs = refs[:4], refs[4:8]
+    own = refs[8 : 8 + count]
+    core_in = refs[8 + count : 8 + 2 * count]
+    two_in = refs[8 + 2 * count : 8 + 3 * count]
+    three_in = refs[8 + 3 * count : 8 + 4 * count]
+    last = refs[8 + 4 * count : 8 + 5 * count]
+    last_in = refs[8 + 5 * count : 8 + 6 * count]
+    local_sem, sends, receives = refs[8 + 6 * count :]
+    z, y, c, x = places()
+    greet(partners(z, y, c, x))
+    across_x = device(z, y, c, 1 - x)
+    across_y = device(z, 1 - y, c, x)
+    across_core = device(z, y, 1 - c, x)
+    order = (3, 2, 1, 0)
+    flights = {}
+    started = []
+
+    def launch(source, target, phase, step, part, where):
+        copy = remote(source, target, sends, receives, (phase * 4 + step) * count + part, where)
+        copy.start()
+        started.append(copy)
+        flights[phase, step, part] = copy
+
+    def block(part, zi, ci):
+        matrix, half = PARTS[part]
+        ref = grads[matrix]
+        return ref.at[zi, :, ci] if half is None else ref.at[zi, :, ci, half]
+
+    held = {}
+    for step in order:
+        zi = far_z(z, step)
+        for part in range(count):
+            launch(block(part, zi, 1 - c), core_in[part].at[step], 0, step, part, across_core)
+            copy = pltpu.make_async_copy(
+                block(part, zi, c), own[part].at[step], local_sem.at[step * count + part]
+            )
+            copy.start()
+            held[step, part] = copy
+
+    def second(step):
+        for part in range(count):
+            held[step, part].wait()
+            flights[0, step, part].wait_recv()
+            for yi in range(2):
+                mine, other = own[part].at[step, yi], core_in[part].at[step, yi]
+                add_rows(lambda at: mine[at, :], lambda at: other[at, :], mine)
+            if part in GROUPS[0]:
+                away = own[part].at[step, :, :, columns_of(own[part], 1 - x)]
+                launch(away, two_in[part].at[step], 1, step, part, across_x)
+            else:
+                launch(own[part].at[step, 1 - y], two_in[part].at[step], 1, step, part, across_y)
+
+    def third(step):
+        for part in range(count):
+            flights[1, step, part].wait_recv()
+            if part in GROUPS[0]:
+                cols = columns_of(own[part], x)
+                for yi in range(2):
+                    mine, other = own[part].at[step, yi], two_in[part].at[step, yi]
+                    add_rows(lambda at: mine[at, cols], lambda at: other[at, :], other)
+                launch(two_in[part].at[step, 1 - y], three_in[part].at[step], 2, step, part, across_y)
+            else:
+                mine, other = own[part].at[step, y], two_in[part].at[step]
+                add_rows(lambda at: mine[at, :], lambda at: other[at, :], other)
+                away = two_in[part].at[step, :, columns_of(own[part], 1 - x)]
+                launch(away, three_in[part].at[step], 2, step, part, across_x)
+
+    def fourth(step):
+        for part in range(count):
+            flights[2, step, part].wait_recv()
+            other = three_in[part].at[step]
+            if part in GROUPS[0]:
+                mine = two_in[part].at[step, y]
+                first = lambda at: mine[at, :]
+            else:
+                mine = two_in[part].at[step]
+                cols = columns_of(own[part], x)
+                first = lambda at: mine[at, cols]
+            add_rows(first, lambda at: other[at, :], last[part].at[step])
+            if step:
+                launch(
+                    last[part].at[step],
+                    last_in[part].at[step - 1],
+                    3,
+                    step,
+                    part,
+                    device(far_z(z, step), y, c, x),
+                )
+
+    for stage in range(4 + 2):
+        if stage < 4:
+            second(order[stage])
+        if 0 <= stage - 1 < 4:
+            third(order[stage - 1])
+        if 0 <= stage - 2 < 4:
+            fourth(order[stage - 2])
+    for part in range(count):
+        for step in (3, 2, 1):
+            flights[3, step, part].wait_recv()
+        matrix, half = PARTS[part]
+        target = outs[matrix] if half is None else outs[matrix].at[half]
+        mine, others = last[part].at[0], last_in[part]
+
+        def finish(index, carry):
+            at = pl.ds(pl.multiple_of(index * 16, 16), 16)
+            total = mine[at, :].astype(jnp.float32)
+            for step in range(3):
+                total = total + others[step, at, :].astype(jnp.float32)
+            target[at, :] = total
+            return carry
+
+        lax.fori_loop(0, target.shape[0] // 16, finish, 0)
+    for copy in started:
+        copy.wait_send()
+
+
+def scatter_all(grads):
+    rows = [grad.shape[0] // 16 for grad in grads]
+    cols = [grad.shape[1] for grad in grads]
+    viewed = [grads[m].reshape(ZS, 2, 2, rows[m], cols[m]) for m in range(3)] + [
+        grads[3].reshape(ZS, 2, 2, 2, rows[3] // 2, cols[3])
+    ]
+    height = [rows[m] if half is None else rows[m] // 2 for m, half in PARTS]
+    breadth = [cols[m] for m, _ in PARTS]
+    both = range(len(PARTS))
+    low = jnp.bfloat16
+    scratch = (
+        [pltpu.VMEM((4, 2, height[p], breadth[p]), low) for p in both]
+        + [pltpu.VMEM((4, 2, height[p], breadth[p]), low) for p in both]
+        + [
+            pltpu.VMEM((4, 2, height[p], breadth[p] // 2), low)
+            if p in GROUPS[0]
+            else pltpu.VMEM((4, height[p], breadth[p]), low)
+            for p in both
+        ]
+        + [pltpu.VMEM((4, height[p], breadth[p] // 2), low) for p in both]
+        + [pltpu.VMEM((4, height[p], breadth[p] // 2), low) for p in both]
+        + [pltpu.VMEM((3, height[p], breadth[p] // 2), low) for p in both]
+    )
+    slots = 16 * len(PARTS)
+    shapes = [(rows[m], cols[m] // 2) for m in range(3)] + [(2, rows[3] // 2, cols[3] // 2)]
+    outs = pl.pallas_call(
+        scatter_kernel,
+        in_specs=[pl.BlockSpec(memory_space=pl.ANY)] * 4,
+        out_specs=[pl.BlockSpec(memory_space=pltpu.VMEM)] * 4,
+        out_shape=[jax.ShapeDtypeStruct(shape, jnp.float32) for shape in shapes],
+        scratch_shapes=scratch
+        + [
+            pltpu.SemaphoreType.DMA((4 * len(PARTS),)),
+            pltpu.SemaphoreType.DMA((slots,)),
+            pltpu.SemaphoreType.DMA((slots,)),
+        ],
+        compiler_params=pltpu.CompilerParams(
+            collective_id=1, has_side_effects=True, vmem_limit_bytes=50 * 2**20
+        ),
+        name="scatter_kernel",
+    )(*viewed)
+    return tuple(outs[:3]) + (outs[3].reshape(rows[3], cols[3] // 2),)
+
+
+def sum_kernel(value_ref, out_ref, incoming, sends, receives):
+    z, y, c, x = places()
+    hops = [
+        device(z, y, 1 - c, x),
+        device(z, y, c, 1 - x),
+        device(z, 1 - y, c, x),
+        device(far_z(z, 1), y, c, x),
+        device(far_z(z, 2), y, c, x),
+    ]
+    greet(hops)
+    source = value_ref
+    for hop in range(5):
+        copy = remote(source, incoming.at[hop], sends, receives, hop, hops[hop])
+        copy.start()
+        copy.wait()
+        out_ref[...] = source[...] + incoming[hop]
+        source = out_ref
+
+
+def sum_all(value, name):
+    return pl.pallas_call(
+        sum_kernel,
+        in_specs=[pl.BlockSpec(memory_space=pltpu.VMEM)],
+        out_specs=pl.BlockSpec(memory_space=pltpu.VMEM),
+        out_shape=jax.ShapeDtypeStruct(value.shape, jnp.float32),
+        scratch_shapes=[
+            pltpu.VMEM((5,) + value.shape, jnp.float32),
+            pltpu.SemaphoreType.DMA((5,)),
+            pltpu.SemaphoreType.DMA((5,)),
+        ],
+        compiler_params=pltpu.CompilerParams(collective_id=name, has_side_effects=True),
+        name="sum_kernel",
+    )(value)
+
+
+def sum_small(arrays):
+    sizes = [array.size for array in arrays]
+    total = sum(sizes)
+    rows = -(-total // 1024) * 8
+    flat = jnp.concatenate([array.reshape(-1) for array in arrays])
+    summed = sum_all(jnp.pad(flat, (0, rows * 128 - total)).reshape(rows, 128), 2).reshape(-1)
+    outs = []
+    at = 0
+    for array, size in zip(arrays, sizes):
+        outs.append(summed[at : at + size].reshape(array.shape))
+        at += size
+    return tuple(outs)
+
+
+def sum_squares(value):
+    wide = jnp.pad(value.reshape(-1), (0, 1024 - value.size)).reshape(8, 128)
+    return sum_all(wide, 3).reshape(-1)[: value.size].reshape(value.shape)
 
 
 def moments(weight, first, second, gradient, decay):
@@ -416,17 +819,17 @@
     dp_count = lax.axis_size("dp")
     shard_count = lax.axis_size("shard")
     tokens_all = inputs.shape[0] * inputs.shape[1] * dp_count * shard_count
-    halves = (
-        lax.all_gather(attend.astype(jnp.bfloat16), "dp", axis=0, tiled=True),
-        lax.all_gather(project.astype(jnp.bfloat16), "dp", axis=0, tiled=True),
-        lax.all_gather(expand.astype(jnp.bfloat16), "dp", axis=0, tiled=True),
-        lax.all_gather(contract.astype(jnp.bfloat16), "dp", axis=0, tiled=True),
-    )
+    special = special_mesh(dp_count, shard_count)
+    shards = tuple(master.astype(jnp.bfloat16) for master in masters[:4])
+    if special:
+        full = gather_all(shards)
+    else:
+        halves = [lax.all_gather(shard, "dp", axis=0, tiled=True) for shard in shards]
+        full = tuple(lax.all_gather(half, "shard", axis=1, tiled=True) for half in halves)
     labels = window_labels(regions)
     bias = table_to_bias(position)
     images = inputs.shape[0]
     width = inputs.shape[2]
-    full = tuple(lax.all_gather(half, "shard", axis=1, tiled=True) for half in halves)
     result_low, grad_input, totals = whole_step(
         to_windows(inputs).reshape(-1, width),
         to_windows(cotangent).reshape(-1, width),
@@ -442,29 +845,20 @@
     grad_input = from_windows(grad_input, images)
     totals = tuple((entry / tokens_all for entry in totals))
     small_grads = totals[4:]
-    small_total = lax.psum(
-        (small_grads[0], small_grads[1], small_grads[2], small_grads[3]), ("dp", "shard")
-    )
-    columns = (
-        lax.psum_scatter(
-            totals[0].astype(jnp.bfloat16), "shard", scatter_dimension=1, tiled=True
-        ).astype(jnp.float32),
-        lax.psum_scatter(
-            totals[1].astype(jnp.bfloat16), "shard", scatter_dimension=1, tiled=True
-        ).astype(jnp.float32),
-        lax.psum_scatter(
-            totals[2].astype(jnp.bfloat16), "shard", scatter_dimension=1, tiled=True
-        ).astype(jnp.float32),
-        lax.psum_scatter(
-            totals[3].astype(jnp.bfloat16), "shard", scatter_dimension=1, tiled=True
-        ).astype(jnp.float32),
-    )
-    owned = (
-        lax.psum_scatter(columns[0], "dp", scatter_dimension=0, tiled=True),
-        lax.psum_scatter(columns[1], "dp", scatter_dimension=0, tiled=True),
-        lax.psum_scatter(columns[2], "dp", scatter_dimension=0, tiled=True),
-        lax.psum_scatter(columns[3], "dp", scatter_dimension=0, tiled=True),
-    )
+    if special:
+        small_total = sum_small(small_grads)
+        owned = scatter_all([total.astype(jnp.bfloat16) for total in totals[:4]])
+    else:
+        small_total = lax.psum(small_grads, ("dp", "shard"))
+        columns = [
+            lax.psum_scatter(
+                total.astype(jnp.bfloat16), "shard", scatter_dimension=1, tiled=True
+            ).astype(jnp.float32)
+            for total in totals[:4]
+        ]
+        owned = tuple(
+            lax.psum_scatter(column, "dp", scatter_dimension=0, tiled=True) for column in columns
+        )
     pieces = [
         moments(masters[slot], firsts[slot], seconds[slot], owned[slot], decay_rate)
         for slot in range(4)
@@ -477,7 +871,10 @@
             for slot in range(4)
         ]
     )
-    squares = jnp.sum(lax.all_gather(partial_value, ("dp", "shard")), axis=0)
+    if special:
+        squares = sum_squares(partial_value)
+    else:
+        squares = lax.psum(partial_value, ("dp", "shard"))
     matrix_norms = jnp.sqrt(squares)
     outputs = [result_low, grad_input]
     pairs = []

time: 1240 us -> 668 us (0.54)
  waiting for transfers between devices: 586 us -> 0 us
  Pallas kernels: 132 us -> 326 us
  blocking collectives: 87.8 us -> 0 us
  other arithmetic: 112 us -> 62.5 us
  matrix products: 155 us -> 135 us
  between operations: 26.6 us -> 13.1 us
    reduce_scatter x5 -> x0, waiting for transfers between devices: 299 us -> none  [the longest x1 75.7 us: body(): lax.psum_scatter(columns[3], 'dp', scatter_dimension=0, tiled=True)]
    pallas_call x0 -> x4, Pallas kernels: none -> 194 us  [the longest x1 83.1 us: gather_all(): pl.pallas_call(gather_kernel, in_specs=[anywhere] * 4, out_specs=[anywher...]
    all_gather x7 -> x0, waiting for transfers between devices: 153 us -> none  [the longest x4 68.5 us: body(): lax.all_gather(half, 'shard', axis=1, tiled=True)]
    all_gather x2 -> x0, blocking collectives: 87.8 us -> none  [the longest x1 65.1 us: body(): squares = jnp.sum(lax.all_gather(partial_value, ('dp', 'shard')), axis=0)]
    psum x1 -> x0, waiting for transfers between devices: 73.4 us -> none  [body(): lax.psum((small_grads[0], small_grads[1], small_grads[2], small_grads[3])...]
    unnamed x19 -> x0, waiting for transfers between devices: 60.5 us -> none
    unnamed x176 -> x166, local copies, waits for them, and re-layouts: 41.8 us -> 8.54 us
    dot_general x0 -> x2, local copies, waits for them, and re-layouts: none -> 15.5 us  [the longest x1 11.2 us: whole_step(): jnp.einsum('wet,ce->wtc', grad_triple, attend, preferred_element_type=jnp...]
  transfers between devices with their start and end apart: 16 -> 0, of which waited for: 11 -> 0; matrix products, arithmetic and copies ran while one was open for 22% -> 0% of each run, Pallas kernels for 11% -> 0%
where the time goes in v2:
time: 668 us; the launch traced here: 659 us
  Pallas kernels  326 us (49%)
  matrix products  135 us (20%)
  local copies, waits for them, and re-layouts  123 us (18%)
  other arithmetic  62.5 us (9%)
  between operations  13.1 us (2%)
    pallas_call x1, Pallas kernels, gather_all(): pl.pallas_call(gather_kernel, in_specs=[anywhere] * 4, out_specs=[anywher...  83.1 us
    pallas_call x1, Pallas kernels, scatter_all(): pl.pallas_call(scatter_kernel, in_specs=[pl.BlockSpec(memory_space=pl.ANY...  79.3 us
    pallas_call x1, Pallas kernels, attend_backward(): pl.pallas_call(backward_kernel, grid=(windows,), in_specs=[window_block(3...  62.6 us
    pallas_call x1, Pallas kernels, attend_forward(): pl.pallas_call(forward_kernel, grid=(windows,), in_specs=[window_block(3...  58.1 us
    dot_general x1, matrix products, whole_step(): jnp.dot(normed_two_low, expand, preferred_element_type=jnp.float32)  39.7 us
    pallas_call x2, Pallas kernels, sum_all(): pl.pallas_call(sum_kernel, in_specs=[pl.BlockSpec(memory_space=pltpu.VMEM...  31.5 us
    dot_general x2, matrix products, product_right(): lax.dot_general(left, right, (((1,), (1,)), ((), ())), preferred_element_...  25.8 us
    pallas_call x2, local copies, waits for them, and re-layouts, attend_backward(): pl.pallas_call(backward_kernel, grid=(windows,), in_specs=[window_block(3...  18 us

profile of v2, /device:TPU:0, one launch (start us, length us, event | category | flops | bytes accessed | tf_op | source)
XLA Modules:
  0.0 659.2 jit_solution(6888386181408016561)
XLA Ops:
  34.9 3.8 reshape.383
  48.9 4.1 reshape_reshape.4
  53.0 3.7 convert_bitcast_fusion
  56.7 5.8 bias_kernel.1
  62.5 5.1 copy.220
  67.5 3.6 copy.184
  71.2 5.5 reshape.375
  82.6 83.1 %gather_kernel.1 = (bf16[4,2,2,48,2304]{4,3,2,1,0:T(8,128)(2,1)}, bf16[4,2,2,48,768]{4,3,2,1,0:T(8,128)(2,1)}, bf16[4,2,2,48,3072]{4,3,2,1,0:T(8,128)(2,1)}, bf16[4,2,2,2,96,768]{5,4,3,2,1,0:T(8,128)(2,1)}) custom-call(bf16[48,1152]{1,0:T(8,128)(2,1)} %convert_element_type.130.refs_0_, bf16[48,384]{1,0:T(8,128)(2,1)} %convert_element_type.131.refs_1_, ...), custom_call_target="tpu_custom_call" | custom-call | bytes 56623104 | tf_op jit(solution)/shard_map/gather_kernel/pallas_call | solution.py:515
  165.6 13.8 %fusion.7.triple_ref = bf16[8,2304,144]{2,1,0:T(8,128)(2,1)} fusion(f32[2304]{0:T(1024)S(1)} %slice-done.1, bf16[768,2304,1]{1,0,2:T(8,128)(2,1)} %bitcast.180, bf16[8,144,768]{2,1,0:T(8,128)(2,1)} %reshape.383), kind=kOutput, calls=%fused_computation.25 | convolution fusion | flops 4082171904 | bytes 10626048 | tf_op jit(solution)/shard_map/wtc,ce->wet/dot_general | solution.py:290
  179.5 58.1 %forward_kernel.1 = (bf16[8,768,144]{2,1,0:T(8,128)(2,1)}, f32[8,24,1,144]{3,2,1,0:T(1,128)}) custom-call(bf16[8,2304,144]{2,1,0:T(8,128)(2,1)} %fusion.7.triple_ref, f32[24,144,144]{2,1,0:T(8,128)} %bitcast.144, s32[4,1,144]{2,1,0:T(1,128)} %broadcast_in_dim_reshape.10.label_ref, s32[4,144,1]{2,1,0:T(8,128)} %broadcast_in_dim_reshape.11.column_ref), custom_call_target="tpu_custom_call" | custom-call | tf_op jit(solution)/shard_map/forward_kernel/pallas_call | solution.py:237
  237.6 4.3 copy.172
  241.9 3.6 fusion.55
  246.4 39.7 %multiply_convert_fusion = (bf16[1152,3072]{1,0:T(8,128)(2,1)}, f32[1152,3072]{1,0:T(8,128)}, f32[1152,3072]{1,0:T(8,128)}) fusion(f32[3072]{0:T(1024)S(1)} %slice-done, bf16[768,3072]{1,0:T(8,128)(2,1)S(1)} %bitcast.176, f32[1152,768]{1,0:T(8,128)S(1)} %get-tuple-element.223, f32[768]{0:T(1024)S(1)} %copy-done.67, f32[768]{0:T(1024)S(1)} %get-tuple-element.230, ...), kind=kOutput, calls=%fused_computation.6 | convolution fusion | flops 5673811968 | bytes 43674624 | tf_op jit(solution)/shard_map/dot_general | solution.py:303
  286.1 19.1 %convert_reduce_fusion.1 = (f32[3072]{0:T(1024)}, bf16[1152,3072]{1,0:T(8,128)(2,1)}) fusion(f32[1152,3072]{1,0:T(8,128)} %get-tuple-element.205, f32[1152,3072]{1,0:T(8,128)} %get-tuple-element.224, bf16[1152,768]{1,0:T(8,128)(2,1)S(1)} %copy-done.3, bf16[3072,768]{1,0:T(8,128)(2,1)} %bitcast.178), kind=kOutput, calls=%fused_computation.4 | convolution fusion | flops 5492438016 | bytes 41889792 | tf_op jit(solution)/shard_map/dot_general | solution.py:276
  305.2 10.8 %fusion.11 = bf16[1152,768]{1,0:T(8,128)(2,1)} fusion(f32[1152,768]{1,0:T(8,128)} %copy-done.6, bf16[1152,3072]{1,0:T(8,128)(2,1)} %get-tuple-element.204, bf16[3072,768]{1,0:T(8,128)(2,1)} %bitcast.179, f32[768]{0:T(1024)S(1)} %copy-done.69), kind=kOutput, calls=%fused_computation.51 | convolution fusion | flops 5438472192 | bytes 17107968 | tf_op jit(solution)/shard_map/dot_general | solution.py:309
  316.1 8.4 %multiply_convert_fusion.1 = bf16[3072,768]{1,0:T(8,128)(2,1)} fusion(bf16[1152,3072]{1,0:T(8,128)(2,1)S(1)} %copy-done.78, bf16[1152,768]{1,0:T(8,128)(2,1)S(1)} %copy-done.3), kind=kOutput, calls=%fused_computation.21 | convolution fusion | flops 5440536576 | bytes 13565952 | tf_op jit(solution)/shard_map/dot_general | solution.py:270
  324.5 6.7 %multiply_reduce_fusion = (f32[768]{0:T(1024)S(1)}, f32[1152]{0:T(1024)S(1)}, f32[768]{0:T(1024)S(1)}, f32[1152,768]{1,0:T(8,128)S(1)}) fusion(f32[1152,768]{1,0:T(8,128)S(1)} %copy-done.7, f32[1152]{0:T(1024)S(1)} %fusion.30, f32[1152]{0:T(1024)S(1)} %broadcast_multiply_fusion.1, f32[768]{0:T(1024)S(1)} %get-tuple-element.230, ...), kind=kOutput, calls=%fused_computation.40 | convolution fusion | flops 5442892800 | bytes 18897408 | tf_op jit(solution)/shard_map/dot_general | solution.py:276
  334.0 9.3 %multiply_convert_fusion.2 = bf16[768,3072]{1,0:T(8,128)(2,1)} fusion(bf16[1152,3072]{1,0:T(8,128)(2,1)S(1)} %copy-done.77, f32[1152,768]{1,0:T(8,128)S(1)} %copy-done.7, f32[768]{0:T(1024)S(1)} %copy-done.68, f32[768]{0:T(1024)S(1)} %get-tuple-element.230, f32[1152]{0:T(1024)S(1)} %copy-done.55, f32[1152]{0:T(1024)S(1)} %copy-done.37), kind=kOutput, calls=%fused_computation.22 | convolution fusion | flops 5444960256 | bytes 15350784 | tf_op jit(solution)/shard_map/dot_general | solution.py:270
  343.3 4.0 reshape.348
  364.2 62.6 %backward_kernel.1 = (bf16[8,2304,144]{2,1,0:T(8,128)(2,1)}, f32[24,144,144]{2,1,0:T(8,128)}) custom-call(bf16[8,2304,144]{2,1,0:T(8,128)(2,1)} %fusion.7.triple_ref, bf16[8,768,144]{2,1,0:T(8,128)(2,1)} %bitcast.153, f32[8,24,1,144]{3,2,1,0:T(1,128)} %get-tuple-element.48.log_ref, f32[24,144,144]{2,1,0:T(8,128)} %bitcast.145, ...), custom_call_target="tpu_custom_call" | custom-call | tf_op jit(solution)/shard_map/backward_kernel/pallas_call | solution.py:255
  426.8 5.8 copy.219
  432.7 5.5 table_kernel.1
  439.0 5.3 convert_reduce_fusion
  444.7 11.2 %copy.180 = bf16[8,144,2304]{2,1,0:T(8,128)(2,1)} copy(bf16[8,144,2304]{1,2,0:T(8,128)(2,1)} %bitcast.139) | data formatting | bytes 10616832 | tf_op jit(solution)/shard_map/wet,ce->wtc/dot_general | solution.py:337
  456.0 9.8 %multiply_reduce_fusion.1 = (f32[768]{0:T(1024)S(1)}, f32[1152]{0:T(1024)S(1)}, f32[768]{0:T(1024)S(1)}, f32[1152,768]{1,0:T(8,128)S(1)}) fusion(f32[1152,768]{1,0:T(8,128)} %copy-done.8, f32[1152]{0:T(1024)S(1)} %copy-done.52, f32[1152]{0:T(1024)S(1)} %copy-done.53, f32[768]{0:T(1024)S(1)} %copy-done.51, bf16[1152,2304]{1,0:T(8,128)(2,1)} %bitcast.158, ...), kind=kOutput, calls=%fused_computation.41 | convolution fusion | flops 4083938560 | bytes 15948288 | tf_op jit(solution)/shard_map/wet,ce->wtc/dot_general | solution.py:337
  471.7 19.0 %sum_kernel.3 = f32[184,128]{1,0:T(8,128)} custom-call(f32[184,128]{1,0:T(8,128)} %fusion.24.value_ref), custom_call_target="tpu_custom_call" | custom-call | tf_op jit(solution)/shard_map/sum_kernel/pallas_call | solution.py:726
  508.3 4.8 reshape.354
  513.1 5.4 copy.183
  523.9 12.1 %copy.189 = bf16[8,2304,144]{1,0,2:T(8,128)(2,1)} copy(bf16[8,2304,144]{2,1,0:T(8,128)(2,1)} %get-tuple-element.49) | data formatting | bytes 10616832 | tf_op jit(solution)/shard_map/backward_kernel/pallas_call | solution.py:255
  536.0 10.4 %fusion.6 = bf16[768,2304]{1,0:T(8,128)(2,1)} fusion(bf16[8,2304,144]{1,0,2:T(8,128)(2,1)} %copy.189, f32[8,144,768]{2,0,1:T(8,128)} %reshape.375, f32[768]{0:T(1024)S(1)} %copy-done.60, f32[768]{0:T(1024)S(1)} %copy-done.51, f32[8,144]{0,1:T(8,128)S(1)} %copy-done.45, f32[8,144]{0,1:T(8,128)S(1)} %copy-done.44), kind=kOutput, calls=%fused_computation.24 | convolution fusion | flops 4084826112 | bytes 12401664 | tf_op jit(solution)/shard_map/wtc,wet->ce/dot_general | solution.py:333
  546.5 79.3 %scatter_kernel.1 = (f32[48,1152]{1,0:T(8,128)S(1)}, f32[48,384]{1,0:T(8,128)S(1)}, f32[48,1536]{1,0:T(8,128)S(1)}, f32[2,96,384]{2,1,0:T(8,128)S(1)}) custom-call(bf16[4,2,2,48,2304]{4,3,2,1,0:T(8,128)(2,1)} %bitcast.161, bf16[4,2,2,48,768]{4,3,2,1,0:T(8,128)(2,1)S(1)} %bitcast.138, bf16[4,2,2,48,3072]{4,3,2,1,0:T(8,128)(2,1)} %bitcast.160, ...), custom_call_target="tpu_custom_call" | custom-call | tf_op jit(solution)/shard_map/scatter_kernel/pallas_call | solution.py:687
  635.4 12.5 %sum_kernel.2 = f32[8,128]{1,0:T(8,128)} custom-call(f32[8,128]{1,0:T(8,128)} %pad_bitcast_fusion.value_ref), custom_call_target="tpu_custom_call" | custom-call | tf_op jit(solution)/shard_map/sum_kernel/pallas_call | solution.py:726
  (292 shorter events, 109.9 us)
Async XLA Ops:
  3.5 26.5 %copy-start.59 = (f32[768]{0:T(1024)}, f32[768]{0:T(1024)S(1)}, u32[]{:S(2)}) copy-start(f32[768]{0:T(1024)S(1)} %get-tuple-element.169) | copy-start | bytes 9220
  79.4 86.3 %slice-start.1 = ((f32[6912]{0:T(1024)}), f32[2304]{0:T(1024)S(1)}, s32[]{:S(2)}) async-start(f32[6912]{0:T(1024)} %param.48), calls=%async_computation.1 | async-start | bytes 24576 | tf_op jit(solution)/shard_map/slice | solution.py:291
  82.5 159.4 %copy-start.8 = (f32[1152,768]{1,0:T(8,128)}, f32[1152,768]{1,0:T(8,128)S(1)}, u32[]{:S(2)}) copy-start(f32[1152,768]{1,0:T(8,128)S(1)} %reshape.374) | copy-start | bytes 10616836
  245.6 40.5 %copy-start.6 = (f32[1152,768]{1,0:T(8,128)}, f32[1152,768]{1,0:T(8,128)S(1)}, u32[]{:S(2)}) copy-start(f32[1152,768]{1,0:T(8,128)S(1)} %get-tuple-element.223) | copy-start | bytes 10616836
  245.6 78.9 %copy-start.36 = (f32[1152]{0:T(1024)}, f32[1152]{0:T(1024)S(1)}, u32[]{:S(2)}) copy-start(f32[1152]{0:T(1024)S(1)} %broadcast_multiply_fusion.1) | copy-start | bytes 13828
  246.2 39.9 %copy-start.38 = (f32[1152]{0:T(1024)}, f32[1152]{0:T(1024)S(1)}, u32[]{:S(2)}) copy-start(f32[1152]{0:T(1024)S(1)} %multiply_reduce_fusion.4) | copy-start | bytes 13828
  246.4 78.1 %copy-start.54 = (f32[1152]{0:T(1024)}, f32[1152]{0:T(1024)S(1)}, u32[]{:S(2)}) copy-start(f32[1152]{0:T(1024)S(1)} %fusion.30) | copy-start | bytes 13828
  246.4 39.8 %copy-start.3 = (bf16[1152,768]{1,0:T(8,128)(2,1)S(1)}, bf16[1152,768]{1,0:T(8,128)(2,1)}, u32[]{:S(2)}) copy-start(bf16[1152,768]{1,0:T(8,128)(2,1)} %reshape_reshape.4) | copy-start | bytes 5308420
  468.4 27.1 %copy-start.49 = (f32[2,768]{1,0:T(2,128)S(1)}, f32[2,768]{1,0:T(2,128)}, u32[]{:S(2)}) copy-start(f32[2,768]{1,0:T(2,128)} %param.45) | copy-start | bytes 18436
  468.4 27.1 %copy-start.65 = (f32[2,768]{1,0:T(2,128)S(1)}, f32[2,768]{1,0:T(2,128)}, u32[]{:S(2)}) copy-start(f32[2,768]{1,0:T(2,128)} %param.46) | copy-start | bytes 18436
  468.4 27.1 %copy-start.66 = (f32[2,768]{1,0:T(2,128)S(1)}, f32[2,768]{1,0:T(2,128)}, u32[]{:S(2)}) copy-start(f32[2,768]{1,0:T(2,128)} %param.47) | copy-start | bytes 18436
  468.4 31.8 %copy-start.29 = (f32[6912]{0:T(1024)S(1)}, f32[6912]{0:T(1024)}, u32[]{:S(2)}) copy-start(f32[6912]{0:T(1024)} %param.48) | copy-start | bytes 82948
  468.4 31.8 %copy-start.56 = (f32[6912]{0:T(1024)S(1)}, f32[6912]{0:T(1024)}, u32[]{:S(2)}) copy-start(f32[6912]{0:T(1024)} %param.49) | copy-start | bytes 82948
  468.5 31.8 %copy-start.57 = (f32[6912]{0:T(1024)S(1)}, f32[6912]{0:T(1024)}, u32[]{:S(2)}) copy-start(f32[6912]{0:T(1024)} %param.50) | copy-start | bytes 82948
  468.5 36.3 %copy-start.22 = (f32[529,24]{0,1:T(8,128)S(1)}, f32[529,24]{0,1:T(8,128)}, u32[]{:S(2)}) copy-start(f32[529,24]{0,1:T(8,128)} %param.51) | copy-start | bytes 152356
  468.5 36.3 %copy-start.46 = (f32[529,24]{0,1:T(8,128)S(1)}, f32[529,24]{0,1:T(8,128)}, u32[]{:S(2)}) copy-start(f32[529,24]{0,1:T(8,128)} %param.52) | copy-start | bytes 152356
  468.5 36.3 %copy-start.47 = (f32[529,24]{0,1:T(8,128)S(1)}, f32[529,24]{0,1:T(8,128)}, u32[]{:S(2)}) copy-start(f32[529,24]{0,1:T(8,128)} %param.53) | copy-start | bytes 152356
  546.4 79.4 %copy-start.21 = (f32[48,384]{1,0:T(8,128)S(1)}, f32[48,384]{1,0:T(8,128)}, u32[]{:S(2)}) copy-start(f32[48,384]{1,0:T(8,128)} %param.33) | copy-start | bytes 221188
  546.4 79.4 %copy-start.40 = (f32[48,384]{1,0:T(8,128)S(1)}, f32[48,384]{1,0:T(8,128)}, u32[]{:S(2)}) copy-start(f32[48,384]{1,0:T(8,128)} %param.34) | copy-start | bytes 221188
  546.4 79.5 %copy-start.41 = (f32[48,384]{1,0:T(8,128)S(1)}, f32[48,384]{1,0:T(8,128)}, u32[]{:S(2)}) copy-start(f32[48,384]{1,0:T(8,128)} %param.35) | copy-start | bytes 221188
  546.4 81.5 %copy-start.13 = (f32[48,1152]{1,0:T(8,128)S(1)}, f32[48,1152]{1,0:T(8,128)}, u32[]{:S(2)}) copy-start(f32[48,1152]{1,0:T(8,128)} %param.30) | copy-start | bytes 663556
  546.4 81.5 %copy-start.32 = (f32[48,1152]{1,0:T(8,128)S(1)}, f32[48,1152]{1,0:T(8,128)}, u32[]{:S(2)}) copy-start(f32[48,1152]{1,0:T(8,128)} %param.31) | copy-start | bytes 663556
  546.4 81.5 %copy-start.33 = (f32[48,1152]{1,0:T(8,128)S(1)}, f32[48,1152]{1,0:T(8,128)}, u32[]{:S(2)}) copy-start(f32[48,1152]{1,0:T(8,128)} %param.32) | copy-start | bytes 663556
  546.5 83.7 %copy-start.12 = (f32[48,1536]{1,0:T(8,128)S(1)}, f32[48,1536]{1,0:T(8,128)}, u32[]{:S(2)}) copy-start(f32[48,1536]{1,0:T(8,128)} %param.36) | copy-start | bytes 884740
  546.5 83.7 %copy-start.25 = (f32[48,1536]{1,0:T(8,128)S(1)}, f32[48,1536]{1,0:T(8,128)}, u32[]{:S(2)}) copy-start(f32[48,1536]{1,0:T(8,128)} %param.37) | copy-start | bytes 884740
  546.5 83.7 %copy-start.26 = (f32[48,1536]{1,0:T(8,128)S(1)}, f32[48,1536]{1,0:T(8,128)}, u32[]{:S(2)}) copy-start(f32[48,1536]{1,0:T(8,128)} %param.38) | copy-start | bytes 884740
  626.6 31.4 %copy-start.23 = (f32[48,384]{1,0:T(8,128)}, f32[48,384]{1,0:T(8,128)S(1)}, u32[]{:S(2)}) copy-start(f32[48,384]{1,0:T(8,128)S(1)} %get-tuple-element.194) | copy-start | bytes 221188
  626.6 31.4 %copy-start.24 = (f32[48,384]{1,0:T(8,128)}, f32[48,384]{1,0:T(8,128)S(1)}, u32[]{:S(2)}) copy-start(f32[48,384]{1,0:T(8,128)S(1)} %get-tuple-element.195) | copy-start | bytes 221188
  628.8 30.1 %copy-start.19 = (f32[48,1152]{1,0:T(8,128)}, f32[48,1152]{1,0:T(8,128)S(1)}, u32[]{:S(2)}) copy-start(f32[48,1152]{1,0:T(8,128)S(1)} %get-tuple-element.192) | copy-start | bytes 663556
  628.8 30.1 %copy-start.20 = (f32[48,1152]{1,0:T(8,128)}, f32[48,1152]{1,0:T(8,128)S(1)}, u32[]{:S(2)}) copy-start(f32[48,1152]{1,0:T(8,128)S(1)} %get-tuple-element.193) | copy-start | bytes 663556
  631.1 27.8 %copy-start.15 = (f32[48,1536]{1,0:T(8,128)}, f32[48,1536]{1,0:T(8,128)S(1)}, u32[]{:S(2)}) copy-start(f32[48,1536]{1,0:T(8,128)S(1)} %get-tuple-element.196) | copy-start | bytes 884740
  631.1 27.8 %copy-start.16 = (f32[48,1536]{1,0:T(8,128)}, f32[48,1536]{1,0:T(8,128)S(1)}, u32[]{:S(2)}) copy-start(f32[48,1536]{1,0:T(8,128)S(1)} %get-tuple-element.197) | copy-start | bytes 884740
  (51 other events, 527.9 us)

commit v3 on v1

--- a/solution.py
+++ b/solution.py
@@ -30,25 +30,6 @@
 
 def gelu_exact(values):
     return jax.nn.gelu(values, approximate=False)
-
-
-def to_windows(values):
-    images = values.shape[0]
-    channels = values.shape[-1]
-    layout = values.reshape(images, GRID, GRID, channels)
-    layout = jnp.roll(layout, (-SHIFT, -SHIFT), axis=(1, 2))
-    layout = layout.reshape(images, GRID // WIN, WIN, GRID // WIN, WIN, channels)
-    return layout.transpose(0, 1, 3, 2, 4, 5).reshape(
-        images * (GRID // WIN) ** 2, WIN * WIN, channels
-    )
-
-
-def from_windows(values, images):
-    channels = values.shape[-1]
-    layout = values.reshape(images, GRID // WIN, GRID // WIN, WIN, WIN, channels)
-    layout = layout.transpose(0, 1, 3, 2, 4, 5).reshape(images, GRID, GRID, channels)
-    layout = jnp.roll(layout, (SHIFT, SHIFT), axis=(1, 2))
-    return layout.reshape(images, GRID * GRID, channels)
 
 
 def window_labels(regions):
@@ -218,6 +199,76 @@
     lax.fori_loop(0, HEADS // HEAD_STEP, step, 0)
 
 
+def entry_kernel(value_ref, cot_ref, gain_ref, shift_ref, value_out, cot_out, norm_out, turned):
+    for source, target in ((cot_ref, cot_out), (value_ref, value_out)):
+        for row in range(GRID):
+            line = source[0, row * GRID : (row + 1) * GRID, :].astype(jnp.float32)
+            line = pltpu.roll(line, GRID - SHIFT, 0)
+            place = (row - SHIFT) % GRID
+            down, within = place // WIN, place % WIN
+            for across in range(GRID // WIN):
+                at = (down * (GRID // WIN) + across) * AREA + within * WIN
+                turned[at : at + WIN, :] = line[across * WIN : (across + 1) * WIN]
+        if source is cot_ref:
+            target[...] = turned[...].astype(jnp.bfloat16)
+
+    def step(index, carry):
+        at = pl.ds(pl.multiple_of(index * 48, 48), 48)
+        values = turned[at, :]
+        value_out[at, :] = values.astype(jnp.bfloat16)
+        norm_out[at, :] = layer_norm(values, gain_ref[...], shift_ref[...]).astype(jnp.bfloat16)
+        return carry
+
+    lax.fori_loop(0, GRID * GRID // 48, step, 0)
+
+
+def enter(values, cot, gain, shift):
+    images, tokens, width = values.shape
+    image = pl.BlockSpec((1, tokens, width), lambda index: (index, 0, 0))
+    line = pl.BlockSpec((1, width), lambda index: (0, 0))
+    rows = pl.BlockSpec((tokens, width), lambda index: (index, 0))
+    return pl.pallas_call(
+        entry_kernel,
+        grid=(images,),
+        in_specs=[image, image, line, line],
+        out_specs=[rows] * 3,
+        out_shape=[jax.ShapeDtypeStruct((images * tokens, width), jnp.bfloat16)] * 3,
+        scratch_shapes=[pltpu.VMEM((tokens, width), jnp.float32)],
+        name="entry_kernel",
+    )(values, cot, gain[None], shift[None])
+
+
+def exit_kernel(result_ref, grad_ref, result_out, grad_out, turned):
+    for source, target in ((result_ref, result_out), (grad_ref, grad_out)):
+        turned[...] = source[...].astype(jnp.float32)
+        for row in range(GRID):
+            place = (row - SHIFT) % GRID
+            down, within = place // WIN, place % WIN
+            starts = [(down * (GRID // WIN) + across) * AREA + within * WIN for across in range(2)]
+            line = jnp.concatenate([turned[at : at + WIN, :] for at in starts], axis=0)
+            line = pltpu.roll(line, SHIFT, 0)
+            target[0, row * GRID : (row + 1) * GRID, :] = line.astype(target.dtype)
+
+
+def leave(result, grad, images):
+    width = result.shape[1]
+    tokens = GRID * GRID
+    image = pl.BlockSpec((1, tokens, width), lambda index: (index, 0, 0))
+    rows = pl.BlockSpec((tokens, width), lambda index: (index, 0))
+    return pl.pallas_call(
+        exit_kernel,
+        grid=(images,),
+        in_specs=[rows] * 2,
+        out_specs=[image] * 2,
+        out_shape=[
+            jax.ShapeDtypeStruct((images, tokens, width), jnp.bfloat16),
+            jax.ShapeDtypeStruct((images, tokens, width), jnp.float32),
+        ],
+        scratch_shapes=[pltpu.VMEM((tokens, width), jnp.float32)],
+        name="exit_kernel",
+    )(result, grad)
+
+
 def window_block(rows):
     return pl.BlockSpec((1, rows, AREA), lambda window: (window, 0, 0))
 
@@ -229,41 +280,81 @@
     ]
 
 
-def attend_forward(triple, bias, labels):
+def attend_forward(triple, bias, labels, shards):
     windows = triple.shape[0]
     width = HEADS * HD
     whole = pl.BlockSpec((HEADS, AREA, AREA), lambda window: (0, 0, 0))
     log_block = pl.BlockSpec((1, HEADS, 1, AREA), lambda window: (window, 0, 0, 0))
-    return pl.pallas_call(
-        forward_kernel,
+    in_specs = [window_block(3 * width), whole] + label_blocks(labels.shape[0])
+    out_specs = [window_block(width), log_block]
+    out_shape = [
+        jax.ShapeDtypeStruct((windows, width, AREA), jnp.bfloat16),
+        jax.ShapeDtypeStruct((windows, HEADS, 1, AREA), jnp.float32),
+    ]
+    arrays = (triple, bias, labels[:, None, :], labels[:, :, None])
+    if shards is None:
+        return pl.pallas_call(
+            forward_kernel,
+            grid=(windows,),
+            in_specs=in_specs,
+            out_specs=out_specs,
+            out_shape=out_shape,
+            name="forward_kernel",
+        )(*arrays)
+    anywhere = pl.BlockSpec(memory_space=pl.ANY)
+    full_shapes = [(ZS, 2, 2, shard.shape[0], 2 * shard.shape[1]) for shard in shards]
+    mixed, log_total, *full = pl.pallas_call(
+        forward_riding,
         grid=(windows,),
-        in_specs=[window_block(3 * width), whole] + label_blocks(labels.shape[0]),
-        out_specs=[window_block(width), log_block],
-        out_shape=[
-            jax.ShapeDtypeStruct((windows, width, AREA), jnp.bfloat16),
-            jax.ShapeDtypeStruct((windows, HEADS, 1, AREA), jnp.float32),
-        ],
+        in_specs=in_specs + [anywhere] * 3,
+        out_specs=out_specs + [anywhere] * 3,
+        out_shape=out_shape + [jax.ShapeDtypeStruct(shape, jnp.bfloat16) for shape in full_shapes],
+        scratch_shapes=comm_sems(3),
+        compiler_params=pltpu.CompilerParams(collective_id=4, has_side_effects=True),
         name="forward_kernel",
-    )(triple, bias, labels[:, None, :], labels[:, :, None])
-
-
-def attend_backward(triple, grad, log_total, bias, labels):
+    )(*arrays, *shards)
+    full = [each.reshape(ZS * 4 * shard.shape[0], -1) for each, shard in zip(full, shards)]
+    return mixed, log_total, full
+
+
+def attend_backward(triple, grad, log_total, bias, labels, grads):
     windows = triple.shape[0]
     width = HEADS * HD
     whole = pl.BlockSpec((HEADS, AREA, AREA), lambda window: (0, 0, 0))
     log_block = pl.BlockSpec((1, HEADS, 1, AREA), lambda window: (window, 0, 0, 0))
-    return pl.pallas_call(
-        backward_kernel,
+    in_specs = [window_block(3 * width), window_block(width), log_block, whole]
+    in_specs = in_specs + label_blocks(labels.shape[0])
+    out_specs = [window_block(3 * width), whole]
+    out_shape = [
+        jax.ShapeDtypeStruct((windows, 3 * width, AREA), jnp.bfloat16),
+        jax.ShapeDtypeStruct((HEADS, AREA, AREA), jnp.float32),
+    ]
+    arrays = (triple, grad, log_total, bias, labels[:, None, :], labels[:, :, None])
+    if grads is None:
+        return pl.pallas_call(
+            backward_kernel,
+            grid=(windows,),
+            in_specs=in_specs,
+            out_specs=out_specs,
+            out_shape=out_shape,
+            name="backward_kernel",
+        )(*arrays)
+    sizes = [(grad.shape[0] // 16, grad.shape[1]) for grad in grads]
+    heights, widths = zip(*sizes)
+    out = pl.pallas_call(
+        backward_riding,
         grid=(windows,),
-        in_specs=[window_block(3 * width), window_block(width), log_block, whole]
-        + label_blocks(labels.shape[0]),
-        out_specs=[window_block(3 * width), whole],
-        out_shape=[
-            jax.ShapeDtypeStruct((windows, 3 * width, AREA), jnp.bfloat16),
-            jax.ShapeDtypeStruct((HEADS, AREA, AREA), jnp.float32),
-        ],
+        in_specs=in_specs + [pl.BlockSpec(memory_space=pl.ANY)] * 3,
+        out_specs=out_specs + [pl.BlockSpec(memory_space=pltpu.VMEM)] * 3,
+        out_shape=out_shape
+        + [jax.ShapeDtypeStruct((rows, cols // 2), jnp.float32) for rows, cols in sizes],
+        scratch_shapes=scatter_scratch(heights, widths) + comm_sems(3),
+        compiler_params=pltpu.CompilerParams(
+            collective_id=5, has_side_effects=True, vmem_limit_bytes=60 * 2**20
+        ),
         name="backward_kernel",
-    )(triple, grad, log_total, bias, labels[:, None, :], labels[:, :, None])
+    )(*arrays, *[grad.reshape(ZS, 2, 2, rows, cols) for grad, (rows, cols) in zip(grads, sizes)])
+    return out[0], out[1], out[2:]
 
 
 def product_left(left, right):
@@ -278,18 +369,23 @@
     )
 
 
-def whole_step(values_low, cot_low, full, gains, shifts, biases, bias, labels, table_rows):
-    attend, project, expand, contract = full
+def whole_step(
+    values_low, cot_low, normed_low, full, shards, gains, shifts, biases, bias, labels, rows, scale
+):
+    attend = full[0]
     width = attend.shape[0]
-    hidden_width = expand.shape[1]
+    hidden_width = biases.shape[0] - 5 * width
     windows = values_low.shape[0] // AREA
     values = values_low.astype(jnp.float32)
-    normed, norm_back = jax.vjp(layer_norm, values, gains[0], shifts[0])
-    normed_low = normed.astype(jnp.bfloat16)
+    norm_back = jax.vjp(layer_norm, values, gains[0], shifts[0])[1]
     windowed = normed_low.reshape(windows, AREA, width)
     triple = jnp.einsum("wtc,ce->wet", windowed, attend, preferred_element_type=jnp.float32)
     triple = (triple + biases[: 3 * width][None, :, None]).astype(jnp.bfloat16)
-    mixed, log_total = attend_forward(triple, bias, labels)
+    if shards is None:
+        mixed, log_total = attend_forward(triple, bias, labels, None)
+        project, expand, contract = full[1:]
+    else:
+        mixed, log_total, (project, expand, contract) = attend_forward(triple, bias, labels, shards)
     branch = (
         jnp.einsum("wct,ce->wte", mixed, project, preferred_element_type=jnp.float32).reshape(
             -1, width
@@ -328,8 +424,18 @@
     grad_mixed = jnp.einsum(
         "wte,ce->wct", grad_branch_windows, project, preferred_element_type=jnp.float32
     ).astype(jnp.bfloat16)
-    grad_triple, grad_scores = attend_backward(triple, grad_mixed, log_total, bias, labels)
-    grad_position = scores_to_table(grad_scores, table_rows)
+    others = tuple(
+        (grad * scale).astype(jnp.bfloat16) for grad in (grad_project, grad_expand, grad_contract)
+    )
+    if shards is None:
+        grad_triple, grad_scores = attend_backward(
+            triple, grad_mixed, log_total, bias, labels, None
+        )
+    else:
+        grad_triple, grad_scores, others = attend_backward(
+            triple, grad_mixed, log_total, bias, labels, others
+        )
+    grad_position = scores_to_table(grad_scores, rows)
     grad_attend = jnp.einsum(
         "wtc,wet->ce", windowed, grad_triple, preferred_element_type=jnp.float32
     )
@@ -339,11 +445,8 @@
     ).reshape(-1, width)
     grad_input_part, grad_gain_one, grad_shift_one = norm_back(grad_normed)
     grad_input = grad_middle + grad_input_part
-    grads = (
-        grad_attend,
-        grad_project,
-        grad_expand,
-        grad_contract,
+    grads = ((grad_attend * scale).astype(jnp.bfloat16),) + tuple(others)
+    small = (
         jnp.stack([grad_gain_one, grad_gain_two]),
         jnp.stack([grad_shift_one, grad_shift_two]),
         jnp.concatenate(
@@ -351,7 +454,456 @@
         ),
         grad_position,
     )
-    return (result.astype(jnp.bfloat16), grad_input, grads)
+    small = tuple(grad * scale for grad in small)
+    return (result.astype(jnp.bfloat16), grad_input, grads, small)
+
+
+ZS = 4
+SPLIT = 2
+ATTEND_PARTS = ((0, 0), (0, 1), (0, 2))
+OTHER_PARTS = ((0, None), (1, None), (2, None))
+
+
+def special_mesh(dp_count, shard_count):
+    return dp_count == ZS * SPLIT * SPLIT and shard_count == SPLIT
+
+
+def places():
+    at = lax.axis_index("dp")
+    return at // 4, lax.rem(at // 2, 2), lax.rem(at, 2), lax.axis_index("shard")
+
+
+def far_z(z, step):
+    return (z, z + 1 - 2 * lax.rem(z, 2), lax.rem(z + 2, 4), 3 - z)[step]
+
+
+def device(z, y, c, x):
+    return {"dp": (z * 2 + y) * 2 + c, "shard": x}
+
+
+def partners(z, y, c, x):
+    return [device(far_z(z, step), y, c, x) for step in (1, 2, 3)] + [
+        device(z, y, c, 1 - x),
+        device(z, 1 - y, c, x),
+        device(z, y, 1 - c, x),
+    ]
+
+
+def greet(devices):
+    barrier = pltpu.get_barrier_semaphore()
+    for one in devices:
+        pl.semaphore_signal(
+            barrier, inc=1, device_id=one, device_id_type=pl.DeviceIdType.MESH
+        )
+    pl.semaphore_wait(barrier, len(devices))
+
+
+def remote(source, target, sends, receives, slot, where):
+    return pltpu.make_async_remote_copy(
+        src_ref=source,
+        dst_ref=target,
+        send_sem=sends.at[slot],
+        recv_sem=receives.at[slot],
+        device_id=where,
+        device_id_type=pl.DeviceIdType.MESH,
+    )
+
+
+def columns_of(ref, x):
+    half = ref.shape[-1] // 2
+    return pl.ds(pl.multiple_of(x * half, 128), half)
+
+
+def x_first(parts, step, part):
+    lone = 2 if parts is ATTEND_PARTS else 0
+    if part == lone:
+        return step % 2 == 0
+    return part == (0 if parts is ATTEND_PARTS else 1)
+
+
+class Gather:
+    def __init__(self, parts, own, full, sems):
+        self.parts, self.own, self.full = parts, own, full
+        self.local_sem, self.sends, self.receives = sems
+        self.count = len(parts)
+        self.at = places()
+
+    def own_part(self, part):
+        matrix, piece = self.parts[part]
+        return self.own[matrix] if piece is None else self.own[matrix].at[piece]
+
+    def spot(self, part, zi, yi, cols):
+        matrix, piece = self.parts[part]
+        c = self.at[2]
+        if piece is None:
+            return self.full[matrix].at[zi, yi, c, :, cols]
+        return self.full[matrix].at[zi, yi, c, piece, :, cols]
+
+    def flight(self, phase, step, part):
+        z, y, c, x = self.at
+        zi = far_z(z, step)
+        cols = columns_of(self.full[self.parts[part][0]], x)
+        everything = slice(None)
+        first = x_first(self.parts, step, part)
+        if phase == 0:
+            here = self.own_part(part)
+            there = self.spot(part, z, y, cols)
+            where = device(zi, y, c, x)
+        elif phase == 1:
+            here = there = self.spot(part, zi, y, cols)
+            where = device(z, y, c, 1 - x) if first else device(z, 1 - y, c, x)
+        elif phase == 2 and first:
+            here = there = self.spot(part, zi, y, everything)
+            where = device(z, 1 - y, c, x)
+        elif phase == 2:
+            here = there = self.spot(part, zi, everything, cols)
+            where = device(z, y, c, 1 - x)
+        else:
+            here = there = self.spot(part, zi, everything, everything)
+            where = device(z, y, 1 - c, x)
+        slot = (phase * 4 + step) * self.count + part
+        return remote(here, there, self.sends, self.receives, slot, where)
+
+    def begin(self):
+        z, y, c, x = self.at
+        greet(partners(z, y, c, x))
+        for step in (1, 2, 3):
+            for part in range(self.count):
+                self.flight(0, step, part).start()
+        copies = []
+        for part in range(self.count):
+            cols = columns_of(self.full[self.parts[part][0]], x)
+            copies.append(
+                pltpu.make_async_copy(
+                    self.own_part(part), self.spot(part, z, y, cols), self.local_sem.at[part]
+                )
+            )
+        for copy in copies:
+            copy.start()
+        for copy in copies:
+            copy.wait()
+
+    def advance(self, phase, step):
+        for part in range(self.count):
+            if phase > 1 or step:
+                self.flight(phase - 1, step, part).wait_recv()
+            self.flight(phase, step, part).start()
+
+    def stage(self, number):
+        for phase in (1, 2, 3):
+            if 0 <= number - phase + 1 < 4:
+                self.advance(phase, number - phase + 1)
+
+    def finish(self):
+        for step in range(4):
+            for part in range(self.count):
+                self.flight(3, step, part).wait_recv()
+        for phase in range(4):
+            for step in range(0 if phase else 1, 4):
+                for part in range(self.count):
+                    self.flight(phase, step, part).wait_send()
+
+
+def comm_sems(count):
+    return [
+        pltpu.SemaphoreType.DMA((4 * count,)),
+        pltpu.SemaphoreType.DMA((16 * count,)),
+        pltpu.SemaphoreType.DMA((16 * count,)),
+    ]
+
+
+def gather_kernel(own_ref, full_ref, *sems):
+    gather = Gather(ATTEND_PARTS, (own_ref,), (full_ref,), sems)
+    gather.begin()
+    for number in range(6):
+        gather.stage(number)
+    gather.finish()
+
+
+def gather_one(shard):
+    rows, half = shard.shape
+    anywhere = pl.BlockSpec(memory_space=pl.ANY)
+    full = pl.pallas_call(
+        gather_kernel,
+        in_specs=[anywhere],
+        out_specs=anywhere,
+        out_shape=jax.ShapeDtypeStruct((ZS, 2, 2, 3, rows // 3, 2 * half), jnp.bfloat16),
+        scratch_shapes=comm_sems(len(ATTEND_PARTS)),
+        compiler_params=pltpu.CompilerParams(collective_id=0, has_side_effects=True),
+        name="gather_kernel",
+    )(shard.reshape(3, rows // 3, half))
+    return full.reshape(ZS * 4 * rows, 2 * half)
+
+
+def add_rows(first, second, target):
+    rows = target.shape[0]
+
+    def step(index, carry):
+        at = pl.ds(pl.multiple_of(index * 16, 16), 16)
+        total = first(at).astype(jnp.float32) + second(at).astype(jnp.float32)
+        target[at, :] = total.astype(target.dtype)
+        return carry
+
+    lax.fori_loop(0, rows // 16, step, 0)
+
+
+class Scatter:
+    order = (3, 2, 1, 0)
+
+    def __init__(self, parts, grads, outs, scratch, sems):
+        self.parts, self.grads, self.outs = parts, grads, outs
+        self.local_sem, self.sends, self.receives = sems
+        self.count = count = len(parts)
+        self.at = places()
+        self.own = scratch[:count]
+        self.core_in = scratch[count : 2 * count]
+        self.two_x = scratch[2 * count : 3 * count]
+        self.two_y = scratch[3 * count : 4 * count]
+        self.three_in = scratch[4 * count : 5 * count]
+        self.last = scratch[5 * count : 6 * count]
+        self.last_in = scratch[6 * count : 7 * count]
+
+    def block(self, part, zi, ci):
+        matrix, piece = self.parts[part]
+        ref = self.grads[matrix]
+        return ref.at[zi, :, ci] if piece is None else ref.at[zi, :, ci, piece]
+
+    def local(self, step, part):
+        z, y, c, x = self.at
+        return pltpu.make_async_copy(
+            self.block(part, far_z(z, step), c),
+            self.own[part].at[step],
+            self.local_sem.at[step * self.count + part],
+        )
+
+    def flight(self, phase, step, part):
+        z, y, c, x = self.at
+        own = self.own[part]
+        first = x_first(self.parts, step, part)
+        across_x, across_y = device(z, y, c, 1 - x), device(z, 1 - y, c, x)
+        other_cols = columns_of(own, 1 - x)
+        if phase == 0:
+            here = self.block(part, far_z(z, step), 1 - c)
+            there, where = self.core_in[part].at[step], device(z, y, 1 - c, x)
+        elif phase == 1 and first:
+            here = own.at[step, :, :, other_cols]
+            there, where = self.two_x[part].at[step], across_x
+        elif phase == 1:
+            here = own.at[step, 1 - y]
+            there, where = self.two_y[part].at[step], across_y
+        elif phase == 2 and first:
+            here = self.two_x[part].at[step, 1 - y]
+            there, where = self.three_in[part].at[step], across_y
+        elif phase == 2:
+            here = self.two_y[part].at[step, :, other_cols]
+            there, where = self.three_in[part].at[step], across_x
+        else:
+            here, there = self.last[part].at[step], self.last_in[part].at[step - 1]
+            where = device(far_z(z, step), y, c, x)
+        slot = (phase * 4 + step) * self.count + part
+        return remote(here, there, self.sends, self.receives, slot, where)
+
+    def begin(self):
+        greet(partners(*self.at))
+        for step in self.order:
+            for part in range(self.count):
+                self.flight(0, step, part).start()
+                self.local(step, part).start()
+
+    def second(self, step):
+        for part in range(self.count):
+            self.local(step, part).wait()
+            self.flight(0, step, part).wait_recv()
+            for yi in range(2):
+                mine, other = self.own[part].at[step, yi], self.core_in[part].at[step, yi]
+                add_rows(lambda at: mine[at, :], lambda at: other[at, :], mine)
+            self.flight(1, step, part).start()
+
+    def third(self, step):
+        z, y, c, x = self.at
+        for part in range(self.count):
+            self.flight(1, step, part).wait_recv()
+            if x_first(self.parts, step, part):
+                cols = columns_of(self.own[part], x)
+                for yi in range(2):
+                    mine, other = self.own[part].at[step, yi], self.two_x[part].at[step, yi]
+                    add_rows(lambda at: mine[at, cols], lambda at: other[at, :], other)
+            else:
+                mine, other = self.own[part].at[step, y], self.two_y[part].at[step]
+                add_rows(lambda at: mine[at, :], lambda at: other[at, :], other)
+            self.flight(2, step, part).start()
+
+    def fourth(self, step):
+        z, y, c, x = self.at
+        for part in range(self.count):
+            self.flight(2, step, part).wait_recv()
+            other = self.three_in[part].at[step]
+            if x_first(self.parts, step, part):
+                mine = self.two_x[part].at[step, y]
+                first = lambda at: mine[at, :]
+            else:
+                mine = self.two_y[part].at[step]
+                cols = columns_of(self.own[part], x)
+                first = lambda at: mine[at, cols]
+            add_rows(first, lambda at: other[at, :], self.last[part].at[step])
+            if step:
+                self.flight(3, step, part).start()
+
+    def stage(self, number):
+        if number < 4:
+            self.second(self.order[number])
+        if 0 <= number - 1 < 4:
+            self.third(self.order[number - 1])
+        if 0 <= number - 2 < 4:
+            self.fourth(self.order[number - 2])
+
+    def finish(self):
+        for part in range(self.count):
+            for step in (3, 2, 1):
+                self.flight(3, step, part).wait_recv()
+            matrix, piece = self.parts[part]
+            target = self.outs[matrix] if piece is None else self.outs[matrix].at[piece]
+            mine, others = self.last[part].at[0], self.last_in[part]
+
+            def total(index, carry):
+                at = pl.ds(pl.multiple_of(index * 16, 16), 16)
+                value = mine[at, :].astype(jnp.float32)
+                for step in range(3):
+                    value = value + others[step, at, :].astype(jnp.float32)
+                target[at, :] = value
+                return carry
+
+            lax.fori_loop(0, target.shape[0] // 16, total, 0)
+        for phase in range(4):
+            for step in range(1 if phase == 3 else 0, 4):
+                for part in range(self.count):
+                    self.flight(phase, step, part).wait_send()
+
+
+def scatter_scratch(heights, widths):
+    low = jnp.bfloat16
+    sizes = list(zip(heights, widths))
+    return (
+        [pltpu.VMEM((4, 2, h, w), low) for h, w in sizes]
+        + [pltpu.VMEM((4, 2, h, w), low) for h, w in sizes]
+        + [pltpu.VMEM((4, 2, h, w // 2), low) for h, w in sizes]
+        + [pltpu.VMEM((4, h, w), low) for h, w in sizes]
+        + [pltpu.VMEM((4, h, w // 2), low) for h, w in sizes]
+        + [pltpu.VMEM((4, h, w // 2), low) for h, w in sizes]
+        + [pltpu.VMEM((3, h, w // 2), low) for h, w in sizes]
+    )
+
+
+def scatter_kernel(grad_ref, out_ref, *rest):
+    scatter = Scatter(ATTEND_PARTS, (grad_ref,), (out_ref,), rest[:-3], rest[-3:])
+    scatter.begin()
+    for number in range(6):
+        scatter.stage(number)
+    scatter.finish()
+
+
+def scatter_one(grad):
+    rows, cols = grad.shape[0] // 16, grad.shape[1]
+    count = len(ATTEND_PARTS)
+    out = pl.pallas_call(
+        scatter_kernel,
+        in_specs=[pl.BlockSpec(memory_space=pl.ANY)],
+        out_specs=pl.BlockSpec(memory_space=pltpu.VMEM),
+        out_shape=jax.ShapeDtypeStruct((3, rows // 3, cols // 2), jnp.float32),
+        scratch_shapes=scatter_scratch([rows // 3] * count, [cols] * count) + comm_sems(count),
+        compiler_params=pltpu.CompilerParams(
+            collective_id=1, has_side_effects=True, vmem_limit_bytes=40 * 2**20
+        ),
+        name="scatter_kernel",
+    )(grad.reshape(ZS, 2, 2, 3, rows // 3, cols))
+    return out.reshape(rows, cols // 2)
+
+
+def at_steps(actions):
+    for number, action in actions:
+        pl.when(pl.program_id(0) == number)(action)
+
+
+def forward_riding(triple_ref, bias_ref, label_ref, column_ref, *rest):
+    gather = Gather(OTHER_PARTS, rest[:3], rest[5:8], rest[8:])
+
+    def start():
+        gather.begin()
+        gather.stage(0)
+
+    at_steps(
+        [(0, start)] + [(number, lambda number=number: gather.stage(number)) for number in range(1, 6)]
+    )
+    forward_kernel(triple_ref, bias_ref, label_ref, column_ref, rest[3], rest[4])
+    at_steps([(pl.num_programs(0) - 1, gather.finish)])
+
+
+def backward_riding(
+    triple_ref, grad_ref, log_ref, bias_ref, label_ref, column_ref, *rest
+):
+    scatter = Scatter(OTHER_PARTS, rest[:3], rest[5:8], rest[8:-3], rest[-3:])
+    at_steps(
+        [(0, scatter.begin)]
+        + [(number + 1, lambda number=number: scatter.stage(number)) for number in range(6)]
+    )
+    backward_kernel(
+        triple_ref, grad_ref, log_ref, bias_ref, label_ref, column_ref, rest[3], rest[4]
+    )
+    at_steps([(pl.num_programs(0) - 1, scatter.finish)])
+
+
+def sum_kernel(value_ref, out_ref, incoming, sends, receives):
+    z, y, c, x = places()
+    hops = [
+        device(z, y, 1 - c, x),
+        device(z, y, c, 1 - x),
+        device(z, 1 - y, c, x),
+        device(far_z(z, 1), y, c, x),
+        device(far_z(z, 2), y, c, x),
+    ]
+    greet(hops)
+    source = value_ref
+    for hop in range(5):
+        copy = remote(source, incoming.at[hop], sends, receives, hop, hops[hop])
+        copy.start()
+        copy.wait()
+        out_ref[...] = source[...] + incoming[hop]
+        source = out_ref
+
+
+def sum_all(value, name):
+    return pl.pallas_call(
+        sum_kernel,
+        in_specs=[pl.BlockSpec(memory_space=pltpu.VMEM)],
+        out_specs=pl.BlockSpec(memory_space=pltpu.VMEM),
+        out_shape=jax.ShapeDtypeStruct(value.shape, jnp.float32),
+        scratch_shapes=[
+            pltpu.VMEM((5,) + value.shape, jnp.float32),
+            pltpu.SemaphoreType.DMA((5,)),
+            pltpu.SemaphoreType.DMA((5,)),
+        ],
+        compiler_params=pltpu.CompilerParams(collective_id=name, has_side_effects=True),
+        name="sum_kernel",
+    )(value)
+
+
+def sum_small(arrays):
+    sizes = [array.size for array in arrays]
+    total = sum(sizes)
+    rows = -(-total // 1024) * 8
+    flat = jnp.concatenate([array.reshape(-1) for array in arrays])
+    summed = sum_all(jnp.pad(flat, (0, rows * 128 - total)).reshape(rows, 128), 2).reshape(-1)
+    outs = []
+    at = 0
+    for array, size in zip(arrays, sizes):
+        outs.append(summed[at : at + size].reshape(array.shape))
+        at += size
+    return tuple(outs)
+
+
+def sum_squares(value):
+    wide = jnp.pad(value.reshape(-1), (0, 1024 - value.size)).reshape(8, 128)
+    return sum_all(wide, 3).reshape(-1)[: value.size].reshape(value.shape)
 
 
 def moments(weight, first, second, gradient, decay):
@@ -416,55 +968,44 @@
     dp_count = lax.axis_size("dp")
     shard_count = lax.axis_size("shard")
     tokens_all = inputs.shape[0] * inputs.shape[1] * dp_count * shard_count
-    halves = (
-        lax.all_gather(attend.astype(jnp.bfloat16), "dp", axis=0, tiled=True),
-        lax.all_gather(project.astype(jnp.bfloat16), "dp", axis=0, tiled=True),
-        lax.all_gather(expand.astype(jnp.bfloat16), "dp", axis=0, tiled=True),
-        lax.all_gather(contract.astype(jnp.bfloat16), "dp", axis=0, tiled=True),
-    )
+    special = special_mesh(dp_count, shard_count)
+    shards = tuple(master.astype(jnp.bfloat16) for master in masters[:4])
+    if special:
+        full = (gather_one(shards[0]),)
+    else:
+        halves = [lax.all_gather(shard, "dp", axis=0, tiled=True) for shard in shards]
+        full = tuple(lax.all_gather(half, "shard", axis=1, tiled=True) for half in halves)
     labels = window_labels(regions)
     bias = table_to_bias(position)
     images = inputs.shape[0]
-    width = inputs.shape[2]
-    full = tuple(lax.all_gather(half, "shard", axis=1, tiled=True) for half in halves)
-    result_low, grad_input, totals = whole_step(
-        to_windows(inputs).reshape(-1, width),
-        to_windows(cotangent).reshape(-1, width),
+    values_low, cot_low, normed_low = enter(inputs, cotangent, gains[0], shifts[0])
+    result_low, grad_input, grads, small_grads = whole_step(
+        values_low,
+        cot_low,
+        normed_low,
         full,
+        shards[1:] if special else None,
         gains,
         shifts,
         biases,
         bias,
         labels,
         position.shape[0],
-    )
-    result_low = from_windows(result_low, images)
-    grad_input = from_windows(grad_input, images)
-    totals = tuple((entry / tokens_all for entry in totals))
-    small_grads = totals[4:]
-    small_total = lax.psum(
-        (small_grads[0], small_grads[1], small_grads[2], small_grads[3]), ("dp", "shard")
-    )
-    columns = (
-        lax.psum_scatter(
-            totals[0].astype(jnp.bfloat16), "shard", scatter_dimension=1, tiled=True
-        ).astype(jnp.float32),
-        lax.psum_scatter(
-            totals[1].astype(jnp.bfloat16), "shard", scatter_dimension=1, tiled=True
-        ).astype(jnp.float32),
-        lax.psum_scatter(
-            totals[2].astype(jnp.bfloat16), "shard", scatter_dimension=1, tiled=True
-        ).astype(jnp.float32),
-        lax.psum_scatter(
-            totals[3].astype(jnp.bfloat16), "shard", scatter_dimension=1, tiled=True
-        ).astype(jnp.float32),
-    )
-    owned = (
-        lax.psum_scatter(columns[0], "dp", scatter_dimension=0, tiled=True),
-        lax.psum_scatter(columns[1], "dp", scatter_dimension=0, tiled=True),
-        lax.psum_scatter(columns[2], "dp", scatter_dimension=0, tiled=True),
-        lax.psum_scatter(columns[3], "dp", scatter_dimension=0, tiled=True),
-    )
+        1.0 / tokens_all,
+    )
+    result_low, grad_input = leave(result_low, grad_input, images)
+    if special:
+        small_total = sum_small(small_grads)
+        owned = (scatter_one(grads[0]),) + tuple(grads[1:])
+    else:
+        small_total = lax.psum(small_grads, ("dp", "shard"))
+        columns = [
+            lax.psum_scatter(grad, "shard", scatter_dimension=1, tiled=True).astype(jnp.float32)
+            for grad in grads
+        ]
+        owned = tuple(
+            lax.psum_scatter(column, "dp", scatter_dimension=0, tiled=True) for column in columns
+        )
     pieces = [
         moments(masters[slot], firsts[slot], seconds[slot], owned[slot], decay_rate)
         for slot in range(4)
@@ -477,7 +1018,10 @@
             for slot in range(4)
         ]
     )
-    squares = jnp.sum(lax.all_gather(partial_value, ("dp", "shard")), axis=0)
+    if special:
+        squares = sum_squares(partial_value)
+    else:
+        squares = lax.psum(partial_value, ("dp", "shard"))
     matrix_norms = jnp.sqrt(squares)
     outputs = [result_low, grad_input]
     pairs = []

time: 1240 us -> 558 us (0.45)
  waiting for transfers between devices: 586 us -> 0 us
  Pallas kernels: 132 us -> 284 us
  blocking collectives: 87.8 us -> 0 us
  local copies, waits for them, and re-layouts: 131 us -> 53.4 us
  other arithmetic: 112 us -> 62.5 us
  matrix products: 155 us -> 138 us
  between operations: 26.6 us -> 13.1 us
    reduce_scatter x5 -> x0, waiting for transfers between devices: 299 us -> none  [the longest x1 75.7 us: body(): lax.psum_scatter(columns[3], 'dp', scatter_dimension=0, tiled=True)]
    all_gather x7 -> x0, waiting for transfers between devices: 153 us -> none  [the longest x4 68.5 us: body(): lax.all_gather(half, 'shard', axis=1, tiled=True)]
    pallas_call x2 -> x8, Pallas kernels: 120 us -> 272 us  [the longest x1 87.4 us: attend_forward(): pl.pallas_call(forward_riding, grid=(windows,), in_specs=in_specs + [anyw...]
    all_gather x2 -> x0, blocking collectives: 87.8 us -> none  [the longest x1 65.1 us: body(): squares = jnp.sum(lax.all_gather(partial_value, ('dp', 'shard')), axis=0)]
    psum x1 -> x0, waiting for transfers between devices: 73.4 us -> none  [body(): lax.psum((small_grads[0], small_grads[1], small_grads[2], small_grads[3])...]
    unnamed x19 -> x0, waiting for transfers between devices: 60.5 us -> none
    unnamed x176 -> x106, local copies, waits for them, and re-layouts: 41.8 us -> 1.29 us
    reshape x4 -> x7, local copies, waits for them, and re-layouts: 18.4 us -> 2.76 us  [the longest x1 1.74 us: sum_small(): flat = jnp.concatenate([array.reshape(-1) for array in arrays])]
  transfers between devices with their start and end apart: 16 -> 0, of which waited for: 11 -> 0; matrix products, arithmetic and copies ran while one was open for 22% -> 0% of each run, Pallas kernels for 11% -> 0%
where the time goes in v3:
time: 558 us; the launch traced here: 551 us
  Pallas kernels  284 us (51%)
  matrix products  138 us (25%)
  other arithmetic  62.5 us (11%)
  local copies, waits for them, and re-layouts  53.4 us (10%)
  between operations  13.1 us (2%)
    pallas_call x1, Pallas kernels, attend_forward(): pl.pallas_call(forward_riding, grid=(windows,), in_specs=in_specs + [anyw...  87.4 us
    pallas_call x1, Pallas kernels, attend_backward(): pl.pallas_call(backward_riding, grid=(windows,), in_specs=in_specs + [pl....  82.2 us
    dot_general x1, matrix products, whole_step(): jnp.dot(normed_two_low, expand, preferred_element_type=jnp.float32)  39.5 us
    pallas_call x2, Pallas kernels, sum_all(): pl.pallas_call(sum_kernel, in_specs=[pl.BlockSpec(memory_space=pltpu.VMEM...  35 us
    pallas_call x1, Pallas kernels, gather_one(): pl.pallas_call(gather_kernel, in_specs=[anywhere], out_specs=anywhere, ou...  30.3 us
    dot_general x2, matrix products, product_right(): lax.dot_general(left, right, (((1,), (1,)), ((), ())), preferred_element_...  30.2 us
    pallas_call x1, Pallas kernels, scatter_one(): pl.pallas_call(scatter_kernel, in_specs=[pl.BlockSpec(memory_space=pl.ANY...  23.8 us
    dot_general x2, matrix products, product_left(): lax.dot_general(left, right, (((0,), (0,)), ((), ())), preferred_element_...  19.9 us

profile of v3, /device:TPU:0, one launch (start us, length us, event | category | flops | bytes accessed | tf_op | source)
XLA Modules:
  0.0 551.1 jit_solution(15038340304545384746)
XLA Ops:
  16.0 30.3 %gather_kernel.1 = bf16[4,2,2,3,16,2304]{5,4,3,2,1,0:T(8,128)(2,1)} custom-call(bf16[3,16,1152]{2,1,0:T(8,128)(2,1)} %bitcast.134), custom_call_target="tpu_custom_call" | custom-call | tf_op jit(solution)/shard_map/gather_kernel/pallas_call | solution.py:626
  46.3 5.8 %bias_kernel.1 = f32[144,24,144]{2,1,0:T(8,128)} custom-call(f32[24,640]{1,0:T(8,128)} %pad.12.table_ref), custom_call_target="tpu_custom_call" | custom-call | tf_op jit(solution)/shard_map/bias_kernel/pallas_call | solution.py:117
  52.1 4.9 copy.149
  57.0 9.1 %entry_kernel.1 = (bf16[1152,768]{1,0:T(8,128)(2,1)}, bf16[1152,768]{1,0:T(8,128)(2,1)}, bf16[1152,768]{1,0:T(8,128)(2,1)}) custom-call(bf16[2,576,768]{2,1,0:T(8,128)(2,1)} %value_ref.1, bf16[2,576,768]{2,1,0:T(8,128)(2,1)} %cot_ref.1, f32[1,768]{1,0:T(1,128)} %get-tuple-element.189.gain_ref, f32[1,768]{1,0:T(1,128)} %get-tuple-element.191.shift_ref), custom_call_target="tpu_custom_call" | custom-call | tf_op jit(solution)/shard_map/entry_kernel/pallas_call | solution.py:230
  66.2 11.3 %fusion.6.triple_ref = bf16[8,2304,144]{2,1,0:T(8,128)(2,1)} fusion(f32[2304]{0:T(1024)S(1)} %slice-done.1, bf16[8,144,768]{2,1,0:T(8,128)(2,1)} %bitcast.143, bf16[768,2304,1]{1,0,2:T(8,128)(2,1)S(1)} %bitcast.127), kind=kOutput, calls=%fused_computation.21 | convolution fusion | flops 4082171904 | bytes 10626048 | tf_op jit(solution)/shard_map/wtc,ce->wet/dot_general | solution.py:382
  77.4 87.4 %forward_kernel.1 = (bf16[8,768,144]{2,1,0:T(8,128)(2,1)}, f32[8,24,1,144]{3,2,1,0:T(1,128)}, bf16[4,2,2,48,768]{4,3,2,1,0:T(8,128)(2,1)}, bf16[4,2,2,48,3072]{4...) custom-call(bf16[8,2304,144]{2,1,0:T(8,128)(2,1)} %fusion.6.triple_ref, f32[24,144,144]{2,1,0:T(8,128)} %bitcast.119, ...), custom_call_target="tpu_custom_call" | custom-call | tf_op jit(solution)/shard_map/forward_kernel/pallas_call | solution.py:306
  164.8 3.2 copy.126
  168.1 3.1 fusion.55
  172.5 39.5 %multiply_convert_fusion = (bf16[1152,3072]{1,0:T(8,128)(2,1)}, f32[1152,3072]{1,0:T(8,128)}, f32[1152,3072]{1,0:T(8,128)}) fusion(f32[3072]{0:T(1024)S(1)} %slice-done, bf16[768,3072]{1,0:T(8,128)(2,1)S(1)} %bitcast.139, f32[1152,768]{1,0:T(8,128)S(1)} %get-tuple-element.201, f32[768]{0:T(1024)S(1)} %copy-done.44, f32[768]{0:T(1024)S(1)} %get-tuple-element.144, ...), kind=kOutput, calls=%fused_computation.6 | convolution fusion | flops 5673811968 | bytes 43674624 | tf_op jit(solution)/shard_map/dot_general | solution.py:399
  212.0 21.2 %convert_reduce_fusion.1 = (f32[3072]{0:T(1024)}, bf16[1152,3072]{1,0:T(8,128)(2,1)}) fusion(f32[1152,3072]{1,0:T(8,128)} %get-tuple-element.178, f32[1152,3072]{1,0:T(8,128)} %get-tuple-element.202, bf16[1152,768]{1,0:T(8,128)(2,1)} %get-tuple-element.52, bf16[3072,768]{1,0:T(8,128)(2,1)} %bitcast.141), kind=kOutput, calls=%fused_computation.4 | convolution fusion | flops 5492438016 | bytes 41889792 | tf_op jit(solution)/shard_map/dot_general | solution.py:367
  233.2 10.3 %fusion.17.result_ref = bf16[1152,768]{1,0:T(8,128)(2,1)} fusion(f32[1152,768]{1,0:T(8,128)S(1)} %copy-done.5, bf16[1152,3072]{1,0:T(8,128)(2,1)} %get-tuple-element.177, bf16[3072,768]{1,0:T(8,128)(2,1)} %bitcast.142, f32[768]{0:T(1024)S(1)} %copy-done.46), kind=kOutput, calls=%fused_computation.52 | convolution fusion | flops 5438472192 | bytes 17107968 | tf_op jit(solution)/shard_map/dot_general | solution.py:405
  243.6 8.3 %multiply_convert_fusion.1 = bf16[3072,768]{1,0:T(8,128)(2,1)} fusion(bf16[1152,3072]{1,0:T(8,128)(2,1)S(1)} %copy-done.50, bf16[1152,768]{1,0:T(8,128)(2,1)S(1)} %copy-done.8), kind=kOutput, calls=%fused_computation.22 | convolution fusion | flops 5440536576 | bytes 13565952 | tf_op jit(solution)/shard_map/dot_general | solution.py:361
  251.9 9.0 %multiply_reduce_fusion = (f32[768]{0:T(1024)S(1)}, f32[1152]{0:T(1024)S(1)}, f32[768]{0:T(1024)S(1)}, f32[1152,768]{1,0:T(8,128)S(1)}) fusion(f32[1152,768]{1,0:T(8,128)S(1)} %copy-done.5, f32[1152]{0:T(1024)S(1)} %copy-done.38, f32[1152]{0:T(1024)S(1)} %copy-done.27, f32[768]{0:T(1024)S(1)} %get-tuple-element.144, ...), kind=kOutput, calls=%fused_computation.47 | convolution fusion | flops 5442892800 | bytes 18897408 | tf_op jit(solution)/shard_map/dot_general | solution.py:367
  262.9 11.6 %multiply_convert_fusion.2 = bf16[768,3072]{1,0:T(8,128)(2,1)} fusion(bf16[1152,3072]{1,0:T(8,128)(2,1)} %get-tuple-element.206, f32[1152,768]{1,0:T(8,128)S(1)} %copy-done.6, f32[768]{0:T(1024)S(1)} %copy-done.45, f32[768]{0:T(1024)S(1)} %get-tuple-element.144, f32[1152]{0:T(1024)S(1)} %copy-done.38, f32[1152]{0:T(1024)S(1)} %copy-done.27), kind=kOutput, calls=%fused_computation.23 | convolution fusion | flops 5444960256 | bytes 15350784 | tf_op jit(solution)/shard_map/dot_general | solution.py:361
  277.0 2.9 fusion.18
  279.9 2.8 convolution_convert_fusion
  282.8 4.4 copy.127
  287.1 82.2 %backward_kernel.1 = (bf16[8,2304,144]{2,1,0:T(8,128)(2,1)}, f32[24,144,144]{2,1,0:T(8,128)}, f32[48,384]{1,0:T(8,128)}, f32[48,1536]{1,0:T(8,128)}, f32[192,384]{1,0:T(8,128)}) custom-call(bf16[8,2304,144]{2,1,0:T(8,128)(2,1)} %fusion.6.triple_ref, bf16[8,768,144]{2,1,0:T(8,128)(2,1)} %bitcast.122, f32[8,24,1,144]{3,2,1,0:T(1,128)} %get-tuple-element.53.log_ref, ...), custom_call_target="tpu_custom_call" | custom-call | tf_op jit(solution)/shard_map/backward_kernel/pallas_call | solution.py:344
  369.4 6.0 %convert_reduce_fusion = f32[2304]{0:T(1024)} fusion(bf16[8,2304,144]{2,1,0:T(8,128)(2,1)} %get-tuple-element.54), kind=kLoop, calls=%fused_computation.1 | loop fusion | flops 5306112 | bytes 5317632 | tf_op jit(solution)/shard_map/reduce_sum | solution.py:442
  375.4 2.2 multiply_reduce_fusion.10
  379.0 2.8 multiply_reduce_fusion.6
  386.1 9.3 %fusion.7 = bf16[768,2304]{1,0:T(8,128)(2,1)S(1)} fusion(bf16[8,144,768]{2,1,0:T(8,128)(2,1)} %bitcast.144, bf16[8,2304,144]{2,1,0:T(8,128)(2,1)S(1)} %copy-done), kind=kOutput, calls=%fused_computation.25 | convolution fusion | flops 4080402432 | bytes 10616832 | tf_op jit(solution)/shard_map/wtc,wet->ce/dot_general | solution.py:439
  395.5 23.8 %scatter_kernel.1 = f32[3,16,1152]{2,1,0:T(8,128)S(1)} custom-call(bf16[4,2,2,3,16,2304]{5,4,3,2,1,0:T(8,128)(2,1)S(1)} %bitcast.117), custom_call_target="tpu_custom_call" | custom-call | tf_op jit(solution)/shard_map/scatter_kernel/pallas_call | solution.py:808
  422.9 14.3 %sum_kernel.2 = f32[8,128]{1,0:T(8,128)} custom-call(f32[8,128]{1,0:T(8,128)} %pad_bitcast_fusion.value_ref), custom_call_target="tpu_custom_call" | custom-call | tf_op jit(solution)/shard_map/sum_kernel/pallas_call | solution.py:875
  454.2 3.8 copy.148
  458.1 5.5 %table_kernel.1 = f32[24,640]{1,0:T(8,128)} custom-call(f32[144,24,144]{2,1,0:T(8,128)} %bitcast.121), custom_call_target="tpu_custom_call" | custom-call | tf_op jit(solution)/shard_map/table_kernel/pallas_call | solution.py:126
  468.5 11.1 %copy.131 = bf16[8,144,2304]{2,1,0:T(8,128)(2,1)} copy(bf16[8,144,2304]{1,2,0:T(8,128)(2,1)} %bitcast.118) | data formatting | bytes 10616832 | tf_op jit(solution)/shard_map/wet,ce->wtc/dot_general | solution.py:443
  479.5 9.1 %fusion.13 = (f32[1152]{0:T(1024)S(1)}, f32[1152]{0:T(1024)S(1)}, f32[1152,768]{1,0:T(8,128)S(1)}) fusion(bf16[1152,768]{1,0:T(8,128)(2,1)} %get-tuple-element.46, f32[1152]{0:T(1024)S(1)} %broadcast_multiply_fusion, f32[768]{0:T(1024)S(1)} %copy-done.35, bf16[1152,2304]{1,0:T(8,128)(2,1)} %bitcast.123, bf16[768,2304]{1,0:T(8,128)(2,1)} %bitcast.126), kind=kOutput, calls=%fused_computation.40 | convolution fusion | flops 4083054592 | bytes 14172672 | tf_op jit(solution)/shard_map/wet,ce->wtc/dot_general | solution.py:443
  488.7 2.7 fusion.16
  497.3 5.3 convert_reduce_fusion.3
  503.3 20.7 %sum_kernel.3 = f32[184,128]{1,0:T(8,128)} custom-call(f32[184,128]{1,0:T(8,128)} %fusion.24.value_ref), custom_call_target="tpu_custom_call" | custom-call | tf_op jit(solution)/shard_map/sum_kernel/pallas_call | solution.py:875
  546.1 4.5 exit_kernel.1
  (186 shorter events, 69.5 us)
Async XLA Ops:
  57.0 9.1 %copy-start.10 = (bf16[4,2,2,3,16,2304]{5,4,3,2,1,0:T(8,128)(2,1)S(1)}, bf16[4,2,2,3,16,2304]{5,4,3,2,1,0:T(8,128)(2,1)}, u32[]{:S(2)}) copy-start(bf16[4,2,2,3,16,2304]{5,4,3,2,1,0:T(8,128)(2,1)} %gather_kernel.1) | copy-start | bytes 10616836
  57.0 9.1 %slice-start.1 = ((f32[6912]{0:T(1024)}), f32[2304]{0:T(1024)S(1)}, s32[]{:S(2)}) async-start(f32[6912]{0:T(1024)} %param.48), calls=%async_computation.1 | async-start | bytes 24576 | tf_op jit(solution)/shard_map/slice | solution.py:383
  171.2 40.8 %copy-start.4 = (f32[1152,768]{1,0:T(8,128)}, f32[1152,768]{1,0:T(8,128)S(1)}, u32[]{:S(2)}) copy-start(f32[1152,768]{1,0:T(8,128)S(1)} %get-tuple-element.201) | copy-start | bytes 10616836
  171.3 40.7 %copy-start.26 = (f32[1152]{0:T(1024)}, f32[1152]{0:T(1024)S(1)}, u32[]{:S(2)}) copy-start(f32[1152]{0:T(1024)S(1)} %broadcast_multiply_fusion.1) | copy-start | bytes 13828
  172.5 39.5 %copy-start.37 = (f32[1152]{0:T(1024)}, f32[1152]{0:T(1024)S(1)}, u32[]{:S(2)}) copy-start(f32[1152]{0:T(1024)S(1)} %fusion.30) | copy-start | bytes 13828
  212.0 21.2 %copy-start.5 = (f32[1152,768]{1,0:T(8,128)S(1)}, f32[1152,768]{1,0:T(8,128)}, u32[]{:S(2)}) copy-start(f32[1152,768]{1,0:T(8,128)} %copy-done.4) | copy-start | bytes 10616836
  212.0 21.2 %copy-start.46 = (f32[768]{0:T(1024)S(1)}, f32[768]{0:T(1024)}, u32[]{:S(2)}) copy-start(f32[768]{0:T(1024)} %get-tuple-element.183) | copy-start | bytes 9220
  233.2 10.3 %copy-start.8 = (bf16[1152,768]{1,0:T(8,128)(2,1)S(1)}, bf16[1152,768]{1,0:T(8,128)(2,1)}, u32[]{:S(2)}) copy-start(bf16[1152,768]{1,0:T(8,128)(2,1)} %get-tuple-element.52) | copy-start | bytes 5308420
  233.2 10.3 %copy-start.50 = (bf16[1152,3072]{1,0:T(8,128)(2,1)S(1)}, bf16[1152,3072]{1,0:T(8,128)(2,1)}, u32[]{:S(2)}) copy-start(bf16[1152,3072]{1,0:T(8,128)(2,1)} %get-tuple-element.177) | copy-start | bytes 21233668
  251.9 9.6 %copy-start.30 = (f32[1152]{0:T(1024)S(1)}, f32[1152]{0:T(1024)}, u32[]{:S(2)}) copy-start(f32[1152]{0:T(1024)} %copy-done.29) | copy-start | bytes 13828
  251.9 9.6 %copy-start.6 = (f32[1152,768]{1,0:T(8,128)S(1)}, f32[1152,768]{1,0:T(8,128)}, u32[]{:S(2)}) copy-start(f32[1152,768]{1,0:T(8,128)} %copy-done.4) | copy-start | bytes 10616836
  262.9 12.2 %copy-start.2 = (bf16[1152,768]{1,0:T(8,128)(2,1)S(1)}, bf16[1152,768]{1,0:T(8,128)(2,1)}, u32[]{:S(2)}) copy-start(bf16[1152,768]{1,0:T(8,128)(2,1)} %get-tuple-element.46) | copy-start | bytes 5308420
  287.1 88.3 %copy-start.15 = (f32[48,384]{1,0:T(8,128)S(1)}, f32[48,384]{1,0:T(8,128)}, u32[]{:S(2)}) copy-start(f32[48,384]{1,0:T(8,128)} %param.33) | copy-start | bytes 221188
  287.1 88.3 %copy-start.31 = (f32[48,384]{1,0:T(8,128)S(1)}, f32[48,384]{1,0:T(8,128)}, u32[]{:S(2)}) copy-start(f32[48,384]{1,0:T(8,128)} %param.34) | copy-start | bytes 221188
  287.1 88.3 %copy-start.32 = (f32[48,384]{1,0:T(8,128)S(1)}, f32[48,384]{1,0:T(8,128)}, u32[]{:S(2)}) copy-start(f32[48,384]{1,0:T(8,128)} %param.35) | copy-start | bytes 221188
  287.1 91.8 %copy-start.13 = (f32[48,1536]{1,0:T(8,128)S(1)}, f32[48,1536]{1,0:T(8,128)}, u32[]{:S(2)}) copy-start(f32[48,1536]{1,0:T(8,128)} %param.36) | copy-start | bytes 884740
  369.3 13.8 %copy-start.12 = (f32[192,384]{1,0:T(8,128)S(1)}, f32[192,384]{1,0:T(8,128)}, u32[]{:S(2)}) copy-start(f32[192,384]{1,0:T(8,128)} %param.39) | copy-start | bytes 884740
  369.3 13.8 %copy-start.16 = (f32[192,384]{1,0:T(8,128)S(1)}, f32[192,384]{1,0:T(8,128)}, u32[]{:S(2)}) copy-start(f32[192,384]{1,0:T(8,128)} %param.40) | copy-start | bytes 884740
  369.3 13.8 %copy-start.17 = (f32[192,384]{1,0:T(8,128)S(1)}, f32[192,384]{1,0:T(8,128)}, u32[]{:S(2)}) copy-start(f32[192,384]{1,0:T(8,128)} %param.41) | copy-start | bytes 884740
  369.3 13.8 %copy-start.18 = (f32[192,384]{1,0:T(8,128)S(1)}, f32[192,384]{1,0:T(8,128)}, u32[]{:S(2)}) copy-start(f32[192,384]{1,0:T(8,128)} %get-tuple-element.59) | copy-start | bytes 884740
  369.4 16.8 %copy-start = (bf16[8,2304,144]{2,1,0:T(8,128)(2,1)S(1)}, bf16[8,2304,144]{2,1,0:T(8,128)(2,1)}, u32[]{:S(2)}) copy-start(bf16[8,2304,144]{2,1,0:T(8,128)(2,1)} %get-tuple-element.54) | copy-start | bytes 15925252
  395.4 23.9 %copy-start.14 = (f32[48,1152]{1,0:T(8,128)S(1)}, f32[48,1152]{1,0:T(8,128)}, u32[]{:S(2)}) copy-start(f32[48,1152]{1,0:T(8,128)} %param.30) | copy-start | bytes 663556
  395.4 23.9 %copy-start.21 = (f32[48,1152]{1,0:T(8,128)S(1)}, f32[48,1152]{1,0:T(8,128)}, u32[]{:S(2)}) copy-start(f32[48,1152]{1,0:T(8,128)} %param.31) | copy-start | bytes 663556
  395.4 23.9 %copy-start.22 = (f32[48,1152]{1,0:T(8,128)S(1)}, f32[48,1152]{1,0:T(8,128)}, u32[]{:S(2)}) copy-start(f32[48,1152]{1,0:T(8,128)} %param.32) | copy-start | bytes 663556
  440.2 14.0 %copy-start.9 = (f32[24,144,144]{2,1,0:T(8,128)S(1)}, f32[24,144,144]{2,1,0:T(8,128)}, u32[]{:S(2)}) copy-start(f32[24,144,144]{2,1,0:T(8,128)} %get-tuple-element.60) | copy-start | bytes 5971972
  468.5 11.1 %copy-start.35 = (f32[768]{0:T(1024)S(1)}, f32[768]{0:T(1024)}, u32[]{:S(2)}) copy-start(f32[768]{0:T(1024)} %get-tuple-element.143) | copy-start | bytes 9220
  479.5 9.1 %copy-start.3 = (bf16[1152,768]{1,0:T(8,128)(2,1)S(1)}, bf16[1152,768]{1,0:T(8,128)(2,1)}, u32[]{:S(2)}) copy-start(bf16[1152,768]{1,0:T(8,128)(2,1)} %get-tuple-element.46) | copy-start | bytes 5308420
  479.5 9.1 %copy-start.36 = (f32[768]{0:T(1024)S(1)}, f32[768]{0:T(1024)}, u32[]{:S(2)}) copy-start(f32[768]{0:T(1024)} %get-tuple-element.143) | copy-start | bytes 9220
  536.7 13.8 %copy-start.24 = (f32[6912]{0:T(1024)}, f32[6912]{0:T(1024)S(1)}, u32[]{:S(2)}) copy-start(f32[6912]{0:T(1024)S(1)} %get-tuple-element.147) | copy-start | bytes 82948
  536.7 13.8 %copy-start.25 = (f32[6912]{0:T(1024)}, f32[6912]{0:T(1024)S(1)}, u32[]{:S(2)}) copy-start(f32[6912]{0:T(1024)S(1)} %get-tuple-element.148) | copy-start | bytes 82948
  541.6 8.9 %copy-start.19 = (f32[529,24]{0,1:T(8,128)}, f32[529,24]{0,1:T(8,128)S(1)}, u32[]{:S(2)}) copy-start(f32[529,24]{0,1:T(8,128)S(1)} %get-tuple-element.145) | copy-start | bytes 152356
  541.6 9.0 %copy-start.20 = (f32[529,24]{0,1:T(8,128)}, f32[529,24]{0,1:T(8,128)S(1)}, u32[]{:S(2)}) copy-start(f32[529,24]{0,1:T(8,128)S(1)} %get-tuple-element.146) | copy-start | bytes 152356
  (23 other events, 91.8 us)

commit v4 on v3

--- a/solution.py
+++ b/solution.py
@@ -1,3 +1,5 @@
+import functools
+
 import jax
 import jax.numpy as jnp
 from jax import lax
@@ -26,10 +28,6 @@
     centred = values - jnp.mean(values, axis=-1, keepdims=True)
     spread = jnp.mean(centred * centred, axis=-1, keepdims=True)
     return centred * lax.rsqrt(spread + norm_eps) * gain_row + shift_row
-
-
-def gelu_exact(values):
-    return jax.nn.gelu(values, approximate=False)
 
 
 def window_labels(regions):
@@ -357,16 +355,97 @@
     return out[0], out[1], out[2:]
 
 
-def product_left(left, right):
-    return lax.dot_general(
-        left, right, (((0,), (0,)), ((), ())), preferred_element_type=jnp.float32
-    )
-
-
-def product_right(left, right):
-    return lax.dot_general(
-        left, right, (((1,), (1,)), ((), ())), preferred_element_type=jnp.float32
-    )
+FEED_TILE = 512
+FEED_ROWS = 192
+
+
+def feed_kernel(
+    scale,
+    norm_ref,
+    turned_ref,
+    cot_ref,
+    middle_ref,
+    expand_ref,
+    contract_ref,
+    bias_in_ref,
+    bias_out_ref,
+    result_ref,
+    back_ref,
+    grad_contract_ref,
+    grad_expand_ref,
+    grad_bias_ref,
+    total,
+    active_all,
+    grad_all,
+):
+    tile = pl.program_id(0)
+    rows = norm_ref.shape[0]
+
+    @pl.when(tile == 0)
+    def _():
+        back_ref[...] = jnp.zeros_like(back_ref)
+        total[...] = middle_ref[...] + bias_out_ref[...]
+
+    def step(index, carry):
+        for member in range(2):
+            at = pl.ds(pl.multiple_of((index * 2 + member) * FEED_ROWS, FEED_ROWS), FEED_ROWS)
+            hidden = dot10(norm_ref[at, :], expand_ref[...]) + bias_in_ref[...]
+            grad_active = dot11(cot_ref[at, :], contract_ref[...])
+            share = 0.5 + 0.5 * lax.erf(hidden * 0.5**0.5)
+            bell = jnp.exp(-0.5 * hidden * hidden) * 0.3989422804014327
+            active = (hidden * share).astype(jnp.bfloat16)
+            grad_hidden = grad_active * (share + hidden * bell)
+            grad_low = grad_hidden.astype(jnp.bfloat16)
+            active_all[at, :] = active
+            grad_all[at, :] = grad_low
+            total[at, :] += dot10(active, contract_ref[...])
+            back_ref[at, :] += dot11(grad_low, expand_ref[...])
+            carry = carry + jnp.sum(
+                grad_low.astype(jnp.float32).reshape(FEED_ROWS // 8, 8, FEED_TILE), axis=0
+            )
+        return carry
+
+    sums = lax.fori_loop(
+        0, rows // (2 * FEED_ROWS), step, jnp.zeros((8, FEED_TILE), jnp.float32)
+    )
+    grad_bias_ref[...] = jnp.sum(sums, axis=0, keepdims=True)
+    grad_contract_ref[...] = (dot00(active_all[...], cot_ref[...]) * scale).astype(jnp.bfloat16)
+    grad_expand_ref[...] = (dot10(turned_ref[...], grad_all[...]) * scale).astype(jnp.bfloat16)
+
+    @pl.when(tile == pl.num_programs(0) - 1)
+    def _():
+        result_ref[...] = total[...].astype(jnp.bfloat16)
+
+
+def feed(norm, cot, middle, expand, contract, bias_in, bias_out, scale):
+    rows, width = norm.shape
+    hidden = expand.shape[1]
+    whole = pl.BlockSpec((rows, width), lambda tile: (0, 0))
+    turned = pl.BlockSpec((width, rows), lambda tile: (0, 0))
+    wide = pl.BlockSpec((width, FEED_TILE), lambda tile: (0, tile))
+    tall = pl.BlockSpec((FEED_TILE, width), lambda tile: (tile, 0))
+    line = pl.BlockSpec((1, FEED_TILE), lambda tile: (0, tile))
+    out_line = pl.BlockSpec((1, width), lambda tile: (0, 0))
+    return pl.pallas_call(
+        functools.partial(feed_kernel, scale),
+        grid=(hidden // FEED_TILE,),
+        in_specs=[whole, turned, whole, whole, wide, tall, line, out_line],
+        out_specs=[whole, whole, tall, wide, line],
+        out_shape=[
+            jax.ShapeDtypeStruct((rows, width), jnp.bfloat16),
+            jax.ShapeDtypeStruct((rows, width), jnp.float32),
+            jax.ShapeDtypeStruct((hidden, width), jnp.bfloat16),
+            jax.ShapeDtypeStruct((width, hidden), jnp.bfloat16),
+            jax.ShapeDtypeStruct((1, hidden), jnp.float32),
+        ],
+        scratch_shapes=[
+            pltpu.VMEM((rows, width), jnp.float32),
+            pltpu.VMEM((rows, FEED_TILE), jnp.bfloat16),
+            pltpu.VMEM((rows, FEED_TILE), jnp.bfloat16),
+        ],
+        compiler_params=pltpu.CompilerParams(vmem_limit_bytes=56 * 2**20),
+        name="feed_kernel",
+    )(norm, norm.T, cot, middle, expand, contract, bias_in[None], bias_out[None])
 
 
 def whole_step(
@@ -395,24 +474,18 @@
     middle = values + branch
     normed_two, norm_two_back = jax.vjp(layer_norm, middle, gains[1], shifts[1])
     normed_two_low = normed_two.astype(jnp.bfloat16)
-    hidden = (
-        jnp.dot(normed_two_low, expand, preferred_element_type=jnp.float32)
-        + biases[4 * width : 4 * width + hidden_width]
-    )
-    active, gelu_back = jax.vjp(gelu_exact, hidden)
-    active_low = active.astype(jnp.bfloat16)
-    result = middle + (
-        jnp.dot(active_low, contract, preferred_element_type=jnp.float32)
-        + biases[4 * width + hidden_width :]
-    )
     cot_float = cot_low.astype(jnp.float32)
-    grad_contract = product_left(active_low, cot_low)
     grad_bias_contract = jnp.sum(cot_float, axis=0)
-    grad_active = product_right(cot_low, contract)
-    grad_hidden_low = gelu_back(grad_active)[0].astype(jnp.bfloat16)
-    grad_expand = product_left(normed_two_low, grad_hidden_low)
-    grad_bias_expand = jnp.sum(grad_hidden_low, axis=0, dtype=jnp.float32)
-    grad_normed_two = product_right(grad_hidden_low, expand)
+    result, grad_normed_two, grad_contract, grad_expand, grad_bias_expand = feed(
+        normed_two_low,
+        cot_low,
+        middle,
+        expand,
+        contract,
+        biases[4 * width : 4 * width + hidden_width],
+        biases[4 * width + hidden_width :],
+        scale,
+    )
     grad_middle_part, grad_gain_two, grad_shift_two = norm_two_back(grad_normed_two)
     grad_middle = cot_float + grad_middle_part
     grad_branch_low = grad_middle.astype(jnp.bfloat16)
@@ -424,9 +497,7 @@
     grad_mixed = jnp.einsum(
         "wte,ce->wct", grad_branch_windows, project, preferred_element_type=jnp.float32
     ).astype(jnp.bfloat16)
-    others = tuple(
-        (grad * scale).astype(jnp.bfloat16) for grad in (grad_project, grad_expand, grad_contract)
-    )
+    others = ((grad_project * scale).astype(jnp.bfloat16), grad_expand, grad_contract)
     if shards is None:
         grad_triple, grad_scores = attend_backward(
             triple, grad_mixed, log_total, bias, labels, None
@@ -447,15 +518,11 @@
     grad_input = grad_middle + grad_input_part
     grads = ((grad_attend * scale).astype(jnp.bfloat16),) + tuple(others)
     small = (
-        jnp.stack([grad_gain_one, grad_gain_two]),
-        jnp.stack([grad_shift_one, grad_shift_two]),
-        jnp.concatenate(
-            [grad_bias_attend, grad_bias_project, grad_bias_expand, grad_bias_contract]
-        ),
+        (grad_gain_one, grad_gain_two, grad_shift_one, grad_shift_two),
+        (grad_bias_attend, grad_bias_project, grad_bias_expand[0], grad_bias_contract),
         grad_position,
     )
-    small = tuple(grad * scale for grad in small)
-    return (result.astype(jnp.bfloat16), grad_input, grads, small)
+    return (result, grad_input, grads, small)
 
 
 ZS = 4
@@ -852,7 +919,28 @@
     at_steps([(pl.num_programs(0) - 1, scatter.finish)])
 
 
-def sum_kernel(value_ref, out_ref, incoming, sends, receives):
+def total_of(values):
+    return jnp.sum(jnp.sum(values, axis=0, keepdims=True), axis=1, keepdims=True)
+
+
+def finish_kernel(scale, *refs):
+    refs = list(refs)
+
+    def take(count):
+        taken = refs[:count]
+        del refs[:count]
+        return taken
+
+    owned, masters, firsts, seconds = take(4), take(4), take(4), take(4)
+    lines, bias_lines, (table_grad,) = take(4), take(4), take(1)
+    small_masters, small_firsts, small_seconds = take(4), take(4), take(4)
+    outs = [take(4) for _ in range(4)]
+    small_outs = [take(3) for _ in range(4)]
+    (pair_ref,) = take(1)
+    updates = take(4)
+    packs = take(3)
+    incoming = take(3)
+    square_ref, square_in, sends, receives = refs
     z, y, c, x = places()
     hops = [
         device(z, y, 1 - c, x),
@@ -862,48 +950,150 @@
         device(far_z(z, 2), y, c, x),
     ]
     greet(hops)
-    source = value_ref
+    for row in range(4):
+        packs[0][row : row + 1, :] = lines[row][...]
+    start = 0
+    for part in bias_lines:
+        packs[1][:, start : start + part.shape[1]] = part[...]
+        start += part.shape[1]
+    packs[2][...] = table_grad[...]
+
+    def matrix(slot):
+        rows, width = masters[slot].shape
+
+        def step(index, carry):
+            at = pl.ds(pl.multiple_of(index * 16, 16), 16)
+            weight = masters[slot][at, :]
+            momentum, variance, update = moments(
+                weight, firsts[slot][at, :], seconds[slot][at, :], owned[slot][at, :], decay_rate
+            )
+            outs[slot][1][at, :] = momentum
+            outs[slot][2][at, :] = variance
+            updates[slot][at, :] = update
+            return (carry[0] + weight * weight, carry[1] + update * update)
+
+        zero = jnp.zeros((16, width), jnp.float32)
+        left, right = lax.fori_loop(0, rows // 16, step, (zero, zero))
+        return total_of(left), total_of(right)
+
+    squares = []
     for hop in range(5):
-        copy = remote(source, incoming.at[hop], sends, receives, hop, hops[hop])
+        copies = [
+            remote(packs[k], incoming[k].at[hop], sends, receives, hop * 3 + k, hops[hop])
+            for k in range(3)
+        ]
+        for copy in copies:
+            copy.start()
+        if hop < 4:
+            squares.append(matrix(hop))
+        for k in range(3):
+            copies[k].wait()
+            packs[k][...] = packs[k][...] + incoming[k][hop]
+    place = lax.broadcasted_iota(jnp.int32, (8, 128), 0)
+    lane = lax.broadcasted_iota(jnp.int32, (8, 128), 1)
+    vector = jnp.zeros((8, 128), jnp.float32)
+    for slot in range(4):
+        for side in range(2):
+            here = (place == slot) & (lane == side)
+            vector = jnp.where(here, squares[slot][side], vector)
+    square_ref[...] = vector
+    small_grads = (packs[0].at[0:2], packs[0].at[2:4], packs[1], packs[2])
+    small_updates = []
+    for hop in range(5):
+        copy = remote(square_ref, square_in.at[hop], sends, receives, 15 + hop, hops[hop])
         copy.start()
+        if hop < 4:
+            weight = small_masters[hop][...]
+            momentum, variance, update = moments(
+                weight,
+                small_firsts[hop][...],
+                small_seconds[hop][...],
+                small_grads[hop][...] * scale,
+                0.0,
+            )
+            small_outs[hop][1][...] = momentum
+            small_outs[hop][2][...] = variance
+            left = jnp.sqrt(total_of(weight * weight))
+            right = jnp.sqrt(total_of(update * update))
+            small_outs[hop][0][...] = weight - learn_rate * left / (right + adam_eps) * update
+            small_updates.append((left, right))
         copy.wait()
-        out_ref[...] = source[...] + incoming[hop]
-        source = out_ref
-
-
-def sum_all(value, name):
-    return pl.pallas_call(
-        sum_kernel,
-        in_specs=[pl.BlockSpec(memory_space=pltpu.VMEM)],
-        out_specs=pl.BlockSpec(memory_space=pltpu.VMEM),
-        out_shape=jax.ShapeDtypeStruct(value.shape, jnp.float32),
-        scratch_shapes=[
-            pltpu.VMEM((5,) + value.shape, jnp.float32),
-            pltpu.SemaphoreType.DMA((5,)),
-            pltpu.SemaphoreType.DMA((5,)),
+        square_ref[...] = square_ref[...] + square_in[hop]
+    norms = jnp.sqrt(square_ref[...])
+    pairs = norms
+    for slot in range(4):
+        for side in range(2):
+            here = (place == 4 + slot) & (lane == side)
+            pairs = jnp.where(here, small_updates[slot][side], pairs)
+    pair_ref[...] = pairs
+    for slot in range(4):
+        left, right = norms[slot : slot + 1, 0:1], norms[slot : slot + 1, 1:2]
+        rate = learn_rate * left / (right + adam_eps)
+
+        def apply(index, carry):
+            at = pl.ds(pl.multiple_of(index * 16, 16), 16)
+            fresh = masters[slot][at, :] - rate * updates[slot][at, :]
+            outs[slot][0][at, :] = fresh
+            outs[slot][3][at, :] = fresh.astype(jnp.bfloat16)
+            return carry
+
+        lax.fori_loop(0, masters[slot].shape[0] // 16, apply, 0)
+
+
+def finish_all(owned, masters, firsts, seconds, small, scale):
+    shapes = [master.shape for master in masters[:4]]
+    flat = lambda entry: entry[None] if entry.ndim == 1 else entry
+    small_masters = [flat(entry) for entry in masters[4:]]
+    small_firsts = [flat(entry) for entry in firsts[4:]]
+    small_seconds = [flat(entry) for entry in seconds[4:]]
+    small_shapes = [entry.shape for entry in small_masters]
+    wide = jnp.float32
+    out_shape = []
+    for shape in shapes:
+        out_shape = out_shape + [jax.ShapeDtypeStruct(shape, wide)] * 3
+        out_shape = out_shape + [jax.ShapeDtypeStruct(shape, jnp.bfloat16)]
+    for shape in small_shapes:
+        out_shape = out_shape + [jax.ShapeDtypeStruct(shape, wide)] * 3
+    out_shape = out_shape + [jax.ShapeDtypeStruct((8, 128), wide)]
+    pack_shapes = [(4, small_shapes[0][1]), small_shapes[2], small_shapes[3]]
+    args = (
+        tuple(owned)
+        + tuple(masters[:4])
+        + tuple(firsts[:4])
+        + tuple(seconds[:4])
+        + tuple(line[None] for line in small[0])
+        + tuple(line[None] for line in small[1])
+        + (small[2],)
+        + tuple(small_masters)
+        + tuple(small_firsts)
+        + tuple(small_seconds)
+    )
+    inside = pl.BlockSpec(memory_space=pltpu.VMEM)
+    outs = pl.pallas_call(
+        functools.partial(finish_kernel, scale),
+        in_specs=[inside] * len(args),
+        out_specs=[inside] * len(out_shape),
+        out_shape=out_shape,
+        scratch_shapes=[pltpu.VMEM(shape, wide) for shape in shapes]
+        + [pltpu.VMEM(shape, wide) for shape in pack_shapes]
+        + [pltpu.VMEM((5,) + shape, wide) for shape in pack_shapes]
+        + [
+            pltpu.VMEM((8, 128), wide),
+            pltpu.VMEM((5, 8, 128), wide),
+            pltpu.SemaphoreType.DMA((20,)),
+            pltpu.SemaphoreType.DMA((20,)),
         ],
-        compiler_params=pltpu.CompilerParams(collective_id=name, has_side_effects=True),
-        name="sum_kernel",
-    )(value)
-
-
-def sum_small(arrays):
-    sizes = [array.size for array in arrays]
-    total = sum(sizes)
-    rows = -(-total // 1024) * 8
-    flat = jnp.concatenate([array.reshape(-1) for array in arrays])
-    summed = sum_all(jnp.pad(flat, (0, rows * 128 - total)).reshape(rows, 128), 2).reshape(-1)
-    outs = []
-    at = 0
-    for array, size in zip(arrays, sizes):
-        outs.append(summed[at : at + size].reshape(array.shape))
-        at += size
-    return tuple(outs)
-
-
-def sum_squares(value):
-    wide = jnp.pad(value.reshape(-1), (0, 1024 - value.size)).reshape(8, 128)
-    return sum_all(wide, 3).reshape(-1)[: value.size].reshape(value.shape)
+        compiler_params=pltpu.CompilerParams(
+            collective_id=2, has_side_effects=True, vmem_limit_bytes=40 * 2**20
+        ),
+        name="finish_kernel",
+    )(*args)
+    outs = list(outs)
+    for slot in range(4):
+        for side in range(3):
+            at = 16 + 3 * slot + side
+            outs[at] = outs[at].reshape(masters[4 + slot].shape)
+    return outs[:-1] + [outs[-1][:, :2]]
 
 
 def moments(weight, first, second, gradient, decay):
@@ -995,17 +1185,26 @@
     )
     result_low, grad_input = leave(result_low, grad_input, images)
     if special:
-        small_total = sum_small(small_grads)
         owned = (scatter_one(grads[0]),) + tuple(grads[1:])
-    else:
-        small_total = lax.psum(small_grads, ("dp", "shard"))
-        columns = [
-            lax.psum_scatter(grad, "shard", scatter_dimension=1, tiled=True).astype(jnp.float32)
-            for grad in grads
-        ]
-        owned = tuple(
-            lax.psum_scatter(column, "dp", scatter_dimension=0, tiled=True) for column in columns
-        )
+        rest = finish_all(owned, masters, firsts, seconds, small_grads, 1.0 / tokens_all)
+        return tuple([result_low, grad_input] + rest)
+    lines, bias_lines, table_grad = small_grads
+    small_total = lax.psum(
+        (
+            jnp.stack(lines[:2]) / tokens_all,
+            jnp.stack(lines[2:]) / tokens_all,
+            jnp.concatenate(bias_lines) / tokens_all,
+            table_grad / tokens_all,
+        ),
+        ("dp", "shard"),
+    )
+    columns = [
+        lax.psum_scatter(grad, "shard", scatter_dimension=1, tiled=True).astype(jnp.float32)
+        for grad in grads
+    ]
+    owned = tuple(
+        lax.psum_scatter(column, "dp", scatter_dimension=0, tiled=True) for column in columns
+    )
     pieces = [
         moments(masters[slot], firsts[slot], seconds[slot], owned[slot], decay_rate)
         for slot in range(4)
@@ -1018,10 +1217,7 @@
             for slot in range(4)
         ]
     )
-    if special:
-        squares = sum_squares(partial_value)
-    else:
-        squares = lax.psum(partial_value, ("dp", "shard"))
+    squares = lax.psum(partial_value, ("dp", "shard"))
     matrix_norms = jnp.sqrt(squares)
     outputs = [result_low, grad_input]
     pairs = []

time: 558 us -> 539 us (0.966)
  matrix products: 138 us -> 38.3 us
  Pallas kernels: 284 us -> 358 us
  local copies, waits for them, and re-layouts: 53.4 us -> 102 us
  other arithmetic: 62.5 us -> 27.9 us
  between operations: 13.1 us -> 1.74 us
    dot_general x6 -> x0, matrix products: 99.9 us -> none  [the longest x1 39.5 us: whole_step(): jnp.dot(normed_two_low, expand, preferred_element_type=jnp.float32)]
    pallas_call x2, Pallas kernels: 35 us -> 110 us  [the longest x1 54.9 us: finish_all(): pl.pallas_call(functools.partial(finish_kernel, scale), in_specs=[inside]...]
    unnamed x106 -> x212, local copies, waits for them, and re-layouts: 1.29 us -> 61.6 us
    reduce_sum x8 -> x0, other arithmetic: 15 us -> none  [the longest x4 8.15 us: body(): jnp.sum(masters[slot] * masters[slot])]
    another operation x9 -> x0, other arithmetic: 5.78 us -> none  [the longest x5 5.47 us: body(): jnp.stack([jnp.stack([jnp.sum(masters[slot] * masters[slot]), jnp.sum(pie...]
where the time goes in v4:
time: 539 us; the launch traced here: 528 us
  Pallas kernels  358 us (66%)
  local copies, waits for them, and re-layouts  102 us (19%)
  matrix products  38.3 us (7%)
  other arithmetic  27.9 us (5%)
    pallas_call x1, Pallas kernels, attend_forward(): pl.pallas_call(forward_riding, grid=(windows,), in_specs=in_specs + [anyw...  87.4 us
    pallas_call x1, Pallas kernels, attend_backward(): pl.pallas_call(backward_riding, grid=(windows,), in_specs=in_specs + [pl....  82.3 us
    unnamed x212, local copies, waits for them, and re-layouts  61.6 us
    pallas_call x1, Pallas kernels, finish_all(): pl.pallas_call(functools.partial(finish_kernel, scale), in_specs=[inside]...  54.9 us
    pallas_call x1, Pallas kernels, feed(): pl.pallas_call(functools.partial(feed_kernel, scale), grid=(hidden // FEE...  54.8 us
    pallas_call x1, Pallas kernels, gather_one(): pl.pallas_call(gather_kernel, in_specs=[anywhere], out_specs=anywhere, ou...  30.3 us
    pallas_call x1, Pallas kernels, scatter_one(): pl.pallas_call(scatter_kernel, in_specs=[pl.BlockSpec(memory_space=pl.ANY...  23.8 us
    dot_general x1, matrix products, whole_step(): jnp.einsum('wtc,ce->wet', windowed, attend, preferred_element_type=jnp.fl...  12 us

profile of v4, /device:TPU:0, one launch (start us, length us, event | category | flops | bytes accessed | tf_op | source)
XLA Modules:
  0.0 528.4 jit_solution(11571521508756661028)
XLA Ops:
  3.4 8.8 %entry_kernel.1 = (bf16[1152,768]{1,0:T(8,128)(2,1)}, bf16[1152,768]{1,0:T(8,128)(2,1)}, bf16[1152,768]{1,0:T(8,128)(2,1)}) custom-call(bf16[2,576,768]{2,1,0:T(8,128)(2,1)} %value_ref.1, bf16[2,576,768]{2,1,0:T(8,128)(2,1)} %cot_ref.1, f32[1,768]{1,0:T(1,128)} %get-tuple-element.242.gain_ref, f32[1,768]{1,0:T(1,128)} %get-tuple-element.244.shift_ref), custom_call_target="tpu_custom_call" | custom-call | tf_op jit(solution)/shard_map/entry_kernel/pallas_call | solution.py:228
  12.8 30.3 %gather_kernel.1 = bf16[4,2,2,3,16,2304]{5,4,3,2,1,0:T(8,128)(2,1)} custom-call(bf16[3,16,1152]{2,1,0:T(8,128)(2,1)} %bitcast.78), custom_call_target="tpu_custom_call" | custom-call | tf_op jit(solution)/shard_map/gather_kernel/pallas_call | solution.py:693
  43.1 12.0 %fusion.triple_ref = bf16[8,2304,144]{2,1,0:T(8,128)(2,1)} fusion(f32[2304]{0:T(1024)S(1)} %slice-done, bf16[8,144,768]{2,1,0:T(8,128)(2,1)S(1)} %bitcast.83, bf16[768,2304,1]{1,0,2:T(8,128)(2,1)} %bitcast.71), kind=kOutput, calls=%fused_computation.2 | convolution fusion | flops 4082171904 | bytes 10626048 | tf_op jit(solution)/shard_map/wtc,ce->wet/dot_general | solution.py:461
  57.5 5.8 %bias_kernel.1 = f32[144,24,144]{2,1,0:T(8,128)} custom-call(f32[24,640]{1,0:T(8,128)} %pad.4.table_ref), custom_call_target="tpu_custom_call" | custom-call | tf_op jit(solution)/shard_map/bias_kernel/pallas_call | solution.py:115
  63.3 4.9 copy.127
  70.2 87.4 %forward_kernel.1 = (bf16[8,768,144]{2,1,0:T(8,128)(2,1)}, f32[8,24,1,144]{3,2,1,0:T(1,128)}, bf16[4,2,2,48,768]{4,3,2,1,0:T(8,128)(2,1)}, bf16[4,2,2,48,3072]{4...) custom-call(bf16[8,2304,144]{2,1,0:T(8,128)(2,1)} %fusion.triple_ref, f32[24,144,144]{2,1,0:T(8,128)} %bitcast.62, ...), custom_call_target="tpu_custom_call" | custom-call | tf_op jit(solution)/shard_map/forward_kernel/pallas_call | solution.py:304
  157.6 4.9 copy.103
  162.6 3.5 fusion.19
  168.5 2.2 copy.104.turned_ref
  170.7 3.8 add_convert_fusion.1.norm_ref
  175.7 54.8 %feed_kernel.1 = (bf16[1152,768]{1,0:T(8,128)(2,1)}, f32[1152,768]{1,0:T(8,128)}, bf16[3072,768]{1,0:T(8,128)(2,1)}, bf16[768,3072]{1,0:T(8,128)(2,1)}, f32[1,3072]{1,0:T(1,128)}) custom-call(bf16[1152,768]{1,0:T(8,128)(2,1)} %add_convert_fusion.1.norm_ref, bf16[768,1152]{1,0:T(8,128)(2,1)} %copy.104.turned_ref, ...), custom_call_target="tpu_custom_call" | custom-call | tf_op jit(solution)/shard_map/feed_kernel/pallas_call | solution.py:429
  230.6 3.5 multiply_reduce_fusion
  238.6 2.9 fusion.10
  241.5 2.8 convolution_convert_fusion
  244.3 4.4 copy.105
  248.8 82.3 %backward_kernel.1 = (bf16[8,2304,144]{2,1,0:T(8,128)(2,1)}, f32[24,144,144]{2,1,0:T(8,128)}, f32[48,384]{1,0:T(8,128)}, f32[48,1536]{1,0:T(8,128)}, f32[192,384]{1,0:T(8,128)}) custom-call(bf16[8,2304,144]{2,1,0:T(8,128)(2,1)} %fusion.triple_ref, bf16[8,768,144]{2,1,0:T(8,128)(2,1)} %bitcast.65, f32[8,24,1,144]{3,2,1,0:T(1,128)} %get-tuple-element.89.log_ref, ...), custom_call_target="tpu_custom_call" | custom-call | tf_op jit(solution)/shard_map/backward_kernel/pallas_call | solution.py:342
  331.0 11.2 %copy.109 = bf16[8,144,2304]{2,1,0:T(8,128)(2,1)} copy(bf16[8,144,2304]{1,2,0:T(8,128)(2,1)} %bitcast.61) | data formatting | bytes 10616832 | tf_op jit(solution)/shard_map/wet,ce->wtc/dot_general | solution.py:514
  342.2 8.9 %fusion.15 = (f32[768]{0:T(1024)S(1)}, f32[1152]{0:T(1024)S(1)}, f32[1152]{0:T(1024)S(1)}, f32[1152,768]{1,0:T(8,128)S(1)}) fusion(f32[768]{0:T(1024)S(1)} %get-tuple-element.230, f32[1152]{0:T(1024)S(1)} %broadcast_multiply_fusion, bf16[1152,768]{1,0:T(8,128)(2,1)} %get-tuple-element.80, bf16[1152,2304]{1,0:T(8,128)(2,1)} %bitcast.66, ...), kind=kOutput, calls=%fused_computation.47 | convolution fusion | flops 4083938304 | bytes 14175744 | tf_op jit(solution)/shard_map/wet,ce->wtc/dot_general | solution.py:514
  351.2 1.6 fusion.9
  353.2 3.3 convert_reduce_fusion.2
  356.5 1.6 copy-done.70
  358.6 8.1 %fusion.1 = bf16[768,2304]{1,0:T(8,128)(2,1)S(1)} fusion(bf16[8,144,768]{2,1,0:T(8,128)(2,1)S(1)} %bitcast.84, bf16[8,2304,144]{2,1,0:T(8,128)(2,1)S(1)} %copy-done.70), kind=kOutput, calls=%fused_computation.4 | convolution fusion | flops 4080402432 | bytes 10616832 | tf_op jit(solution)/shard_map/wtc,wet->ce/dot_general | solution.py:510
  366.7 23.8 %scatter_kernel.1 = f32[3,16,1152]{2,1,0:T(8,128)S(1)} custom-call(bf16[4,2,2,3,16,2304]{5,4,3,2,1,0:T(8,128)(2,1)S(1)} %bitcast.57), custom_call_target="tpu_custom_call" | custom-call | tf_op jit(solution)/shard_map/scatter_kernel/pallas_call | solution.py:875
  391.7 3.8 copy.126
  395.5 5.5 %table_kernel.1 = f32[24,640]{1,0:T(8,128)} custom-call(f32[144,24,144]{2,1,0:T(8,128)} %bitcast.64), custom_call_target="tpu_custom_call" | custom-call | tf_op jit(solution)/shard_map/table_kernel/pallas_call | solution.py:124
  402.1 5.3 %convert_reduce_fusion = f32[2304]{0:T(1024)S(1)} fusion(bf16[8,2304,144]{2,1,0:T(8,128)(2,1)} %get-tuple-element.92), kind=kLoop, calls=%fused_computation | loop fusion | flops 5306112 | bytes 5317632 | tf_op jit(solution)/shard_map/reduce_sum | solution.py:513
  427.6 54.9 %finish_kernel.1 = (f32[48,1152]{1,0:T(8,128)S(1)}, f32[48,1152]{1,0:T(8,128)S(1)}, f32[48,1152]{1,0:T(8,128)S(1)}, bf16[48,1152]{1,0:T(8,128)(2,1)S(1)}, f32[48...) custom-call(f32[48,1152]{1,0:T(8,128)S(1)} %bitcast.59, ...), custom_call_target="tpu_custom_call" | custom-call | tf_op jit(solution)/shard_map/finish_kernel/pallas_call | solution.py:1072
  497.9 1.8 copy.116
  499.7 1.8 copy.117
  501.5 1.8 copy.118
  503.2 1.5 reduce.3
  508.9 4.6 exit_kernel.1
  (247 shorter events, 72.8 us)
Async XLA Ops:
  0.7 11.5 %copy-start.2 = (f32[48,1152]{1,0:T(8,128)S(1)}, f32[48,1152]{1,0:T(8,128)}, u32[]{:S(2)}) copy-start(f32[48,1152]{1,0:T(8,128)} %refs_4_.1) | copy-start | bytes 663556
  3.4 39.7 %slice-start = ((f32[6912]{0:T(1024)}), f32[2304]{0:T(1024)S(1)}, s32[]{:S(2)}) async-start(f32[6912]{0:T(1024)} %param.48), calls=%async_computation | async-start | bytes 24576 | tf_op jit(solution)/shard_map/slice | solution.py:462
  12.1 31.0 %copy-start.88 = (bf16[1152,768]{1,0:T(8,128)(2,1)S(1)}, bf16[1152,768]{1,0:T(8,128)(2,1)}, u32[]{:S(2)}) copy-start(bf16[1152,768]{1,0:T(8,128)(2,1)} %get-tuple-element.81) | copy-start | bytes 5308420
  43.1 12.1 %copy-start.87 = (s32[576]{0:T(1024)S(1)}, s32[576]{0:T(1024)}, u32[]{:S(2)}) copy-start(s32[576]{0:T(1024)} %param.29) | copy-start | bytes 6916
  43.1 13.7 %copy-start.80 = (f32[529,24]{0,1:T(8,128)S(1)}, f32[529,24]{0,1:T(8,128)}, u32[]{:S(2)}) copy-start(f32[529,24]{0,1:T(8,128)} %param.51) | copy-start | bytes 152356
  63.3 6.3 %copy-start.13 = (f32[48,384]{1,0:T(8,128)S(1)}, f32[48,384]{1,0:T(8,128)}, u32[]{:S(2)}) copy-start(f32[48,384]{1,0:T(8,128)} %refs_5_.1) | copy-start | bytes 221188
  175.7 54.8 %copy-start.69 = (f32[1152,768]{1,0:T(8,128)S(1)}, f32[1152,768]{1,0:T(8,128)}, u32[]{:S(2)}) copy-start(f32[1152,768]{1,0:T(8,128)} %copy-done.68) | copy-start | bytes 10616836
  342.2 9.0 %copy-start.76 = (bf16[1152,768]{1,0:T(8,128)(2,1)S(1)}, bf16[1152,768]{1,0:T(8,128)(2,1)}, u32[]{:S(2)}) copy-start(bf16[1152,768]{1,0:T(8,128)(2,1)} %get-tuple-element.80) | copy-start | bytes 5308420
  366.7 25.0 %copy-start.78 = (f32[24,144,144]{2,1,0:T(8,128)S(1)}, f32[24,144,144]{2,1,0:T(8,128)}, u32[]{:S(2)}) copy-start(f32[24,144,144]{2,1,0:T(8,128)} %get-tuple-element.99) | copy-start | bytes 5971972
  402.0 7.3 %copy-start.83 = (f32[529,24]{0,1:T(8,128)S(1)}, f32[529,24]{0,1:T(8,128)}, u32[]{:S(2)}) copy-start(f32[529,24]{0,1:T(8,128)} %param.52) | copy-start | bytes 152356
  402.0 7.4 %copy-start.84 = (f32[529,24]{0,1:T(8,128)S(1)}, f32[529,24]{0,1:T(8,128)}, u32[]{:S(2)}) copy-start(f32[529,24]{0,1:T(8,128)} %param.53) | copy-start | bytes 152356
  402.0 7.6 %copy-start.82 = (f32[6912]{0:T(1024)S(1)}, f32[6912]{0:T(1024)}, u32[]{:S(2)}) copy-start(f32[6912]{0:T(1024)} %param.48) | copy-start | bytes 82948
  402.0 7.6 %copy-start.85 = (f32[6912]{0:T(1024)S(1)}, f32[6912]{0:T(1024)}, u32[]{:S(2)}) copy-start(f32[6912]{0:T(1024)} %param.49) | copy-start | bytes 82948
  402.0 7.6 %copy-start.86 = (f32[6912]{0:T(1024)S(1)}, f32[6912]{0:T(1024)}, u32[]{:S(2)}) copy-start(f32[6912]{0:T(1024)} %param.50) | copy-start | bytes 82948
  402.1 7.7 %copy-start.43 = (f32[2,768]{1,0:T(2,128)S(1)}, f32[2,768]{1,0:T(2,128)}, u32[]{:S(2)}) copy-start(f32[2,768]{1,0:T(2,128)} %refs_25_.1) | copy-start | bytes 18436
  497.9 15.6 %copy-start.22 = (f32[48,1152]{1,0:T(8,128)S(1)}, f32[48,1152]{1,0:T(8,128)}, u32[]{:S(2)}) copy-start(f32[48,1152]{1,0:T(8,128)} %copy-done.21) | copy-start | bytes 663556
  497.9 16.3 %copy-start.20 = (f32[48,1152]{1,0:T(8,128)S(1)}, f32[48,1152]{1,0:T(8,128)}, u32[]{:S(2)}) copy-start(f32[48,1152]{1,0:T(8,128)} %copy-done.19) | copy-start | bytes 663556
  499.7 15.2 %copy-start.18 = (f32[48,1152]{1,0:T(8,128)S(1)}, f32[48,1152]{1,0:T(8,128)}, u32[]{:S(2)}) copy-start(f32[48,1152]{1,0:T(8,128)} %copy-done.17) | copy-start | bytes 663556
  501.5 14.1 %copy-start.28 = (bf16[48,1152]{1,0:T(8,128)(2,1)S(1)}, bf16[48,1152]{1,0:T(8,128)(2,1)}, u32[]{:S(2)}) copy-start(bf16[48,1152]{1,0:T(8,128)(2,1)} %copy-done.27) | copy-start | bytes 331780
  503.2 13.0 %copy-start.34 = (f32[48,384]{1,0:T(8,128)S(1)}, f32[48,384]{1,0:T(8,128)}, u32[]{:S(2)}) copy-start(f32[48,384]{1,0:T(8,128)} %copy-done.33) | copy-start | bytes 221188
  506.1 10.8 %copy-start.32 = (f32[48,384]{1,0:T(8,128)S(1)}, f32[48,384]{1,0:T(8,128)}, u32[]{:S(2)}) copy-start(f32[48,384]{1,0:T(8,128)} %copy-done.31) | copy-start | bytes 221188
  508.9 8.6 %copy-start.30 = (f32[48,384]{1,0:T(8,128)S(1)}, f32[48,384]{1,0:T(8,128)}, u32[]{:S(2)}) copy-start(f32[48,384]{1,0:T(8,128)} %copy-done.29) | copy-start | bytes 221188
  508.9 9.3 %copy-start.39 = (bf16[48,384]{1,0:T(8,128)(2,1)S(1)}, bf16[48,384]{1,0:T(8,128)(2,1)}, u32[]{:S(2)}) copy-start(bf16[48,384]{1,0:T(8,128)(2,1)} %copy-done.38) | copy-start | bytes 110596
  508.9 9.9 %copy-start.6 = (f32[48,1536]{1,0:T(8,128)S(1)}, f32[48,1536]{1,0:T(8,128)}, u32[]{:S(2)}) copy-start(f32[48,1536]{1,0:T(8,128)} %copy-done.5) | copy-start | bytes 884740
  508.9 10.6 %copy-start.4 = (f32[48,1536]{1,0:T(8,128)S(1)}, f32[48,1536]{1,0:T(8,128)}, u32[]{:S(2)}) copy-start(f32[48,1536]{1,0:T(8,128)} %copy-done.3) | copy-start | bytes 884740
  508.9 12.0 %copy-start.26 = (bf16[48,1536]{1,0:T(8,128)(2,1)S(1)}, bf16[48,1536]{1,0:T(8,128)(2,1)}, u32[]{:S(2)}) copy-start(bf16[48,1536]{1,0:T(8,128)(2,1)} %copy-done.25) | copy-start | bytes 442372
  513.5 10.9 %copy-start.62 = (f32[2,768]{1,0:T(2,128)S(1)}, f32[2,768]{1,0:T(2,128)}, u32[]{:S(2)}) copy-start(f32[2,768]{1,0:T(2,128)} %copy-done.61) | copy-start | bytes 18436
  513.5 11.5 %copy-start.60 = (f32[2,768]{1,0:T(2,128)S(1)}, f32[2,768]{1,0:T(2,128)}, u32[]{:S(2)}) copy-start(f32[2,768]{1,0:T(2,128)} %copy-done.59) | copy-start | bytes 18436
  513.5 12.1 %copy-start.58 = (f32[2,768]{1,0:T(2,128)S(1)}, f32[2,768]{1,0:T(2,128)}, u32[]{:S(2)}) copy-start(f32[2,768]{1,0:T(2,128)} %copy-done.57) | copy-start | bytes 18436
  513.5 12.7 %copy-start.56 = (f32[2,768]{1,0:T(2,128)S(1)}, f32[2,768]{1,0:T(2,128)}, u32[]{:S(2)}) copy-start(f32[2,768]{1,0:T(2,128)} %copy-done.55) | copy-start | bytes 18436
  513.5 13.3 %copy-start.54 = (f32[2,768]{1,0:T(2,128)S(1)}, f32[2,768]{1,0:T(2,128)}, u32[]{:S(2)}) copy-start(f32[2,768]{1,0:T(2,128)} %copy-done.53) | copy-start | bytes 18436
  513.5 13.9 %copy-start.52 = (f32[2,768]{1,0:T(2,128)S(1)}, f32[2,768]{1,0:T(2,128)}, u32[]{:S(2)}) copy-start(f32[2,768]{1,0:T(2,128)} %copy-done.51) | copy-start | bytes 18436
  (60 other events, 82.1 us)

commit v5 on v4

--- a/solution.py
+++ b/solution.py
@@ -120,13 +120,12 @@
     return spread.transpose(1, 0, 2)
 
 
-def scores_to_table(scores, rows):
-    table = pl.pallas_call(
+def scores_to_table(scores):
+    return pl.pallas_call(
         table_kernel,
         out_shape=jax.ShapeDtypeStruct((HEADS, TABLE_PAD), jnp.float32),
         name="table_kernel",
     )(scores.transpose(1, 0, 2))
-    return table[:, :rows].T
 
 
 def scores_of(keyed, query, bias, allowed):
@@ -449,7 +448,7 @@
 
 
 def whole_step(
-    values_low, cot_low, normed_low, full, shards, gains, shifts, biases, bias, labels, rows, scale
+    values_low, cot_low, normed_low, full, shards, gains, shifts, biases, bias, labels, scale
 ):
     attend = full[0]
     width = attend.shape[0]
@@ -506,7 +505,7 @@
         grad_triple, grad_scores, others = attend_backward(
             triple, grad_mixed, log_total, bias, labels, others
         )
-    grad_position = scores_to_table(grad_scores, rows)
+    grad_position = scores_to_table(grad_scores)
     grad_attend = jnp.einsum(
         "wtc,wet->ce", windowed, grad_triple, preferred_element_type=jnp.float32
     )
@@ -657,7 +656,7 @@
             self.flight(phase, step, part).start()
 
     def stage(self, number):
-        for phase in (1, 2, 3):
+        for phase in (3, 2, 1):
             if 0 <= number - phase + 1 < 4:
                 self.advance(phase, number - phase + 1)
 
@@ -817,12 +816,12 @@
                 self.flight(3, step, part).start()
 
     def stage(self, number):
+        if 0 <= number - 2 < 4:
+            self.fourth(self.order[number - 2])
+        if 0 <= number - 1 < 4:
+            self.third(self.order[number - 1])
         if number < 4:
             self.second(self.order[number])
-        if 0 <= number - 1 < 4:
-            self.third(self.order[number - 1])
-        if 0 <= number - 2 < 4:
-            self.fourth(self.order[number - 2])
 
     def finish(self):
         for part in range(self.count):
@@ -923,24 +922,41 @@
     return jnp.sum(jnp.sum(values, axis=0, keepdims=True), axis=1, keepdims=True)
 
 
-def finish_kernel(scale, *refs):
-    refs = list(refs)
-
-    def take(count):
-        taken = refs[:count]
-        del refs[:count]
-        return taken
-
-    owned, masters, firsts, seconds = take(4), take(4), take(4), take(4)
-    lines, bias_lines, (table_grad,) = take(4), take(4), take(1)
-    small_masters, small_firsts, small_seconds = take(4), take(4), take(4)
-    outs = [take(4) for _ in range(4)]
-    small_outs = [take(3) for _ in range(4)]
-    (pair_ref,) = take(1)
-    updates = take(4)
-    packs = take(3)
-    incoming = take(3)
-    square_ref, square_in, sends, receives = refs
+FINISH_STEPS = 3
+
+
+def moment_kernel(*refs):
+    owned, masters, firsts, seconds = refs[:4], refs[4:8], refs[8:12], refs[12:16]
+    outs, square_ref = [refs[16 + 3 * slot : 19 + 3 * slot] for slot in range(4)], refs[28]
+    place = lax.broadcasted_iota(jnp.int32, (8, 128), 0)
+    lane = lax.broadcasted_iota(jnp.int32, (8, 128), 1)
+    vector = jnp.zeros((8, 128), jnp.float32)
+    for slot in range(4):
+        rows, width = masters[slot].shape
+        sums = [jnp.zeros((16, width), jnp.float32)] * 2
+        for start in range(0, rows, 16):
+            at = slice(start, start + 16)
+            weight = masters[slot][at, :]
+            results = moments(
+                weight, firsts[slot][at, :], seconds[slot][at, :], owned[slot][at, :], decay_rate
+            )
+            for side in range(3):
+                outs[slot][side][at, :] = results[side]
+            sums = [sums[0] + weight * weight, sums[1] + results[2] * results[2]]
+        for side in range(2):
+            vector = jnp.where((place == slot) & (lane == side), total_of(sums[side]), vector)
+
+    @pl.when(pl.program_id(0) == 0)
+    def _():
+        square_ref[...] = jnp.zeros_like(square_ref)
+
+    square_ref[...] += vector
+
+
+def sum_kernel(*refs):
+    lines, bias_lines, table_ref, square_ref = refs[:4], refs[4:8], refs[8], refs[9]
+    packs, incoming = refs[10:14], refs[14:18]
+    sends, receives = refs[18:]
     z, y, c, x = places()
     hops = [
         device(z, y, 1 - c, x),
@@ -956,144 +972,134 @@
     for part in bias_lines:
         packs[1][:, start : start + part.shape[1]] = part[...]
         start += part.shape[1]
-    packs[2][...] = table_grad[...]
-
-    def matrix(slot):
-        rows, width = masters[slot].shape
-
-        def step(index, carry):
-            at = pl.ds(pl.multiple_of(index * 16, 16), 16)
-            weight = masters[slot][at, :]
-            momentum, variance, update = moments(
-                weight, firsts[slot][at, :], seconds[slot][at, :], owned[slot][at, :], decay_rate
-            )
-            outs[slot][1][at, :] = momentum
-            outs[slot][2][at, :] = variance
-            updates[slot][at, :] = update
-            return (carry[0] + weight * weight, carry[1] + update * update)
-
-        zero = jnp.zeros((16, width), jnp.float32)
-        left, right = lax.fori_loop(0, rows // 16, step, (zero, zero))
-        return total_of(left), total_of(right)
-
-    squares = []
+    packs[2][...] = table_ref[...]
+    packs[3][...] = square_ref[...]
     for hop in range(5):
         copies = [
-            remote(packs[k], incoming[k].at[hop], sends, receives, hop * 3 + k, hops[hop])
-            for k in range(3)
+            remote(packs[k], incoming[k].at[hop], sends, receives, hop * 4 + k, hops[hop])
+            for k in range(4)
         ]
         for copy in copies:
             copy.start()
-        if hop < 4:
-            squares.append(matrix(hop))
-        for k in range(3):
+        for k in range(4):
             copies[k].wait()
             packs[k][...] = packs[k][...] + incoming[k][hop]
-    place = lax.broadcasted_iota(jnp.int32, (8, 128), 0)
-    lane = lax.broadcasted_iota(jnp.int32, (8, 128), 1)
-    vector = jnp.zeros((8, 128), jnp.float32)
-    for slot in range(4):
-        for side in range(2):
-            here = (place == slot) & (lane == side)
-            vector = jnp.where(here, squares[slot][side], vector)
-    square_ref[...] = vector
-    small_grads = (packs[0].at[0:2], packs[0].at[2:4], packs[1], packs[2])
-    small_updates = []
-    for hop in range(5):
-        copy = remote(square_ref, square_in.at[hop], sends, receives, 15 + hop, hops[hop])
-        copy.start()
-        if hop < 4:
-            weight = small_masters[hop][...]
-            momentum, variance, update = moments(
-                weight,
-                small_firsts[hop][...],
-                small_seconds[hop][...],
-                small_grads[hop][...] * scale,
-                0.0,
-            )
-            small_outs[hop][1][...] = momentum
-            small_outs[hop][2][...] = variance
-            left = jnp.sqrt(total_of(weight * weight))
-            right = jnp.sqrt(total_of(update * update))
-            small_outs[hop][0][...] = weight - learn_rate * left / (right + adam_eps) * update
-            small_updates.append((left, right))
-        copy.wait()
-        square_ref[...] = square_ref[...] + square_in[hop]
-    norms = jnp.sqrt(square_ref[...])
-    pairs = norms
-    for slot in range(4):
-        for side in range(2):
-            here = (place == 4 + slot) & (lane == side)
-            pairs = jnp.where(here, small_updates[slot][side], pairs)
-    pair_ref[...] = pairs
+
+
+def apply_kernel(scale, *refs):
+    masters, updates, packs = refs[:4], refs[4:8], refs[8:12]
+    small = [refs[12 + 3 * slot : 15 + 3 * slot] for slot in range(4)]
+    outs = [refs[24 + 2 * slot : 26 + 2 * slot] for slot in range(4)]
+    small_outs = [refs[32 + 3 * slot : 35 + 3 * slot] for slot in range(4)]
+    pair_ref = refs[44]
+    norms = jnp.sqrt(packs[3][...])
     for slot in range(4):
         left, right = norms[slot : slot + 1, 0:1], norms[slot : slot + 1, 1:2]
         rate = learn_rate * left / (right + adam_eps)
-
-        def apply(index, carry):
-            at = pl.ds(pl.multiple_of(index * 16, 16), 16)
+        for start in range(0, masters[slot].shape[0], 16):
+            at = slice(start, start + 16)
             fresh = masters[slot][at, :] - rate * updates[slot][at, :]
             outs[slot][0][at, :] = fresh
-            outs[slot][3][at, :] = fresh.astype(jnp.bfloat16)
-            return carry
-
-        lax.fori_loop(0, masters[slot].shape[0] // 16, apply, 0)
+            outs[slot][1][at, :] = fresh.astype(jnp.bfloat16)
+
+    @pl.when(pl.program_id(0) == 0)
+    def _():
+        place = lax.broadcasted_iota(jnp.int32, (8, 128), 0)
+        lane = lax.broadcasted_iota(jnp.int32, (8, 128), 1)
+        pairs = norms
+        gradients = (
+            packs[0][0:2, :],
+            packs[0][2:4, :],
+            packs[1][...],
+            packs[2][:, : small[3][0].shape[1]],
+        )
+        for slot in range(4):
+            weight = small[slot][0][...]
+            momentum, variance, update = moments(
+                weight, small[slot][1][...], small[slot][2][...], gradients[slot] * scale, 0.0
+            )
+            left = jnp.sqrt(total_of(weight * weight))
+            right = jnp.sqrt(total_of(update * update))
+            small_outs[slot][0][...] = weight - learn_rate * left / (right + adam_eps) * update
+            small_outs[slot][1][...] = momentum
+            small_outs[slot][2][...] = variance
+            for side, value in enumerate((left, right)):
+                pairs = jnp.where((place == 4 + slot) & (lane == side), value, pairs)
+        pair_ref[...] = pairs
 
 
 def finish_all(owned, masters, firsts, seconds, small, scale):
+    wide = jnp.float32
     shapes = [master.shape for master in masters[:4]]
-    flat = lambda entry: entry[None] if entry.ndim == 1 else entry
-    small_masters = [flat(entry) for entry in masters[4:]]
-    small_firsts = [flat(entry) for entry in firsts[4:]]
-    small_seconds = [flat(entry) for entry in seconds[4:]]
-    small_shapes = [entry.shape for entry in small_masters]
-    wide = jnp.float32
-    out_shape = []
-    for shape in shapes:
-        out_shape = out_shape + [jax.ShapeDtypeStruct(shape, wide)] * 3
-        out_shape = out_shape + [jax.ShapeDtypeStruct(shape, jnp.bfloat16)]
-    for shape in small_shapes:
-        out_shape = out_shape + [jax.ShapeDtypeStruct(shape, wide)] * 3
-    out_shape = out_shape + [jax.ShapeDtypeStruct((8, 128), wide)]
-    pack_shapes = [(4, small_shapes[0][1]), small_shapes[2], small_shapes[3]]
-    args = (
-        tuple(owned)
-        + tuple(masters[:4])
-        + tuple(firsts[:4])
-        + tuple(seconds[:4])
-        + tuple(line[None] for line in small[0])
-        + tuple(line[None] for line in small[1])
-        + (small[2],)
-        + tuple(small_masters)
-        + tuple(small_firsts)
-        + tuple(small_seconds)
-    )
+
+    def flat(slot, entry):
+        return entry[None] if entry.ndim == 1 else entry.T if slot == 3 else entry
+
+    def blocks(count):
+        return [
+            pl.BlockSpec((rows // FINISH_STEPS, cols), lambda step: (step, 0))
+            for rows, cols in shapes
+            for _ in range(count)
+        ]
+
+    def whole(shape):
+        return pl.BlockSpec(shape, lambda step: (0, 0))
+
+    def like(shape, kind=wide):
+        return jax.ShapeDtypeStruct(shape, kind)
+
+    first_out = pl.pallas_call(
+        moment_kernel,
+        grid=(FINISH_STEPS,),
+        in_specs=blocks(1) * 4,
+        out_specs=blocks(3) + [whole((8, 128))],
+        out_shape=[like(shape) for shape in shapes for _ in range(3)] + [like((8, 128))],
+        name="moment_kernel",
+    )(*owned, *masters[:4], *firsts[:4], *seconds[:4])
+    width = small[0][0].shape[0]
+    pack_shapes = [(4, width), (1, masters[6].shape[0]), small[2].shape, (8, 128)]
     inside = pl.BlockSpec(memory_space=pltpu.VMEM)
+    packs = pl.pallas_call(
+        sum_kernel,
+        in_specs=[inside] * 10,
+        out_specs=[inside] * 4,
+        out_shape=[like(shape) for shape in pack_shapes],
+        scratch_shapes=[pltpu.VMEM((5,) + shape, wide) for shape in pack_shapes]
+        + [pltpu.SemaphoreType.DMA((20,))] * 2,
+        compiler_params=pltpu.CompilerParams(collective_id=2, has_side_effects=True),
+        name="sum_kernel",
+    )(
+        *[line[None] for line in small[0]],
+        *[line[None] for line in small[1]],
+        small[2],
+        first_out[-1],
+    )
+    small_in = [
+        flat(slot, kind[4 + slot]) for slot in range(4) for kind in (masters, firsts, seconds)
+    ]
+    small_shapes = [entry.shape for entry in small_in]
     outs = pl.pallas_call(
-        functools.partial(finish_kernel, scale),
-        in_specs=[inside] * len(args),
-        out_specs=[inside] * len(out_shape),
-        out_shape=out_shape,
-        scratch_shapes=[pltpu.VMEM(shape, wide) for shape in shapes]
-        + [pltpu.VMEM(shape, wide) for shape in pack_shapes]
-        + [pltpu.VMEM((5,) + shape, wide) for shape in pack_shapes]
-        + [
-            pltpu.VMEM((8, 128), wide),
-            pltpu.VMEM((5, 8, 128), wide),
-            pltpu.SemaphoreType.DMA((20,)),
-            pltpu.SemaphoreType.DMA((20,)),
-        ],
-        compiler_params=pltpu.CompilerParams(
-            collective_id=2, has_side_effects=True, vmem_limit_bytes=40 * 2**20
-        ),
-        name="finish_kernel",
-    )(*args)
-    outs = list(outs)
+        functools.partial(apply_kernel, scale),
+        grid=(FINISH_STEPS,),
+        in_specs=blocks(1) * 2
+        + [whole(shape) for shape in pack_shapes]
+        + [whole(shape) for shape in small_shapes],
+        out_specs=blocks(2) + [whole(shape) for shape in small_shapes] + [whole((8, 128))],
+        out_shape=[like(shape, kind) for shape in shapes for kind in (wide, jnp.bfloat16)]
+        + [like(shape) for shape in small_shapes]
+        + [like((8, 128))],
+        name="apply_kernel",
+    )(*masters[:4], *[first_out[3 * slot + 2] for slot in range(4)], *packs, *small_in)
+    results = []
+    for slot in range(4):
+        fresh, copy = outs[2 * slot : 2 * slot + 2]
+        results = results + [fresh, first_out[3 * slot], first_out[3 * slot + 1], copy]
     for slot in range(4):
         for side in range(3):
-            at = 16 + 3 * slot + side
-            outs[at] = outs[at].reshape(masters[4 + slot].shape)
-    return outs[:-1] + [outs[-1][:, :2]]
+            entry = outs[8 + 3 * slot + side]
+            entry = entry[0] if slot == 2 else entry.T if slot == 3 else entry
+            results.append(entry)
+    return results + [outs[-1][:, :2]]
 
 
 def moments(weight, first, second, gradient, decay):
@@ -1180,7 +1186,6 @@
         biases,
         bias,
         labels,
-        position.shape[0],
         1.0 / tokens_all,
     )
     result_low, grad_input = leave(result_low, grad_input, images)
@@ -1194,7 +1199,7 @@
             jnp.stack(lines[:2]) / tokens_all,
             jnp.stack(lines[2:]) / tokens_all,
             jnp.concatenate(bias_lines) / tokens_all,
-            table_grad / tokens_all,
+            table_grad[:, : position.shape[0]].T / tokens_all,
         ),
         ("dp", "shard"),
     )

time: 539 us -> 487 us (0.904)
  local copies, waits for them, and re-layouts: 102 us -> 51 us
  Pallas kernels: 358 us -> 352 us
    unnamed x212 -> x65, local copies, waits for them, and re-layouts: 61.6 us -> 4.24 us
    pallas_call x1 -> x3, Pallas kernels: 54.9 us -> 31.5 us  [the longest x1 22 us: finish_all(): pl.pallas_call(sum_kernel, in_specs=[inside] * 10, out_specs=[inside] * 4...]
    pallas_call x1, Pallas kernels: 23.8 us -> 31.7 us  [scatter_one(): pl.pallas_call(scatter_kernel, in_specs=[pl.BlockSpec(memory_space=pl.ANY...]
    pallas_call x1, Pallas kernels: 30.3 us -> 37.1 us  [gather_one(): pl.pallas_call(gather_kernel, in_specs=[anywhere], out_specs=anywhere, ou...]
where the time goes in v5:
time: 487 us; the launch traced here: 478 us
  Pallas kernels  352 us (72%)
  local copies, waits for them, and re-layouts  51 us (10%)
  matrix products  42.7 us (9%)
  other arithmetic  29.9 us (6%)
    pallas_call x1, Pallas kernels, attend_forward(): pl.pallas_call(forward_riding, grid=(windows,), in_specs=in_specs + [anyw...  90.9 us
    pallas_call x1, Pallas kernels, attend_backward(): pl.pallas_call(backward_riding, grid=(windows,), in_specs=in_specs + [pl....  81.5 us
    pallas_call x1, Pallas kernels, feed(): pl.pallas_call(functools.partial(feed_kernel, scale), grid=(hidden // FEE...  55.1 us
    pallas_call x1, Pallas kernels, gather_one(): pl.pallas_call(gather_kernel, in_specs=[anywhere], out_specs=anywhere, ou...  37.1 us
    pallas_call x1, Pallas kernels, scatter_one(): pl.pallas_call(scatter_kernel, in_specs=[pl.BlockSpec(memory_space=pl.ANY...  31.7 us
    pallas_call x1, Pallas kernels, finish_all(): pl.pallas_call(sum_kernel, in_specs=[inside] * 10, out_specs=[inside] * 4...  22 us
    dot_general x1, matrix products, whole_step(): jnp.einsum('wtc,ce->wet', windowed, attend, preferred_element_type=jnp.fl...  12 us
    dot_general x1, matrix products, whole_step(): jnp.einsum('wtc,wet->ce', windowed, grad_triple, preferred_element_type=j...  11.8 us

profile of v5, /device:TPU:0, one launch (start us, length us, event | category | flops | bytes accessed | tf_op | source)
XLA Modules:
  0.0 477.5 jit_solution(1679217682454338895)
XLA Ops:
  0.7 1.9 slice_reduce_fusion.2
  2.6 1.9 slice_reduce_fusion
  4.6 8.8 %entry_kernel.1 = (bf16[1152,768]{1,0:T(8,128)(2,1)}, bf16[1152,768]{1,0:T(8,128)(2,1)}, bf16[1152,768]{1,0:T(8,128)(2,1)}) custom-call(bf16[2,576,768]{2,1,0:T(8,128)(2,1)} %value_ref.1, bf16[2,576,768]{2,1,0:T(8,128)(2,1)} %cot_ref.1, f32[1,768]{1,0:T(1,128)} %get-tuple-element.260.gain_ref, f32[1,768]{1,0:T(1,128)} %get-tuple-element.262.shift_ref), custom_call_target="tpu_custom_call" | custom-call | tf_op jit(solution)/shard_map/entry_kernel/pallas_call | solution.py:227
  14.0 37.1 %gather_kernel.1 = bf16[4,2,2,3,16,2304]{5,4,3,2,1,0:T(8,128)(2,1)} custom-call(bf16[3,16,1152]{2,1,0:T(8,128)(2,1)} %bitcast.79), custom_call_target="tpu_custom_call" | custom-call | tf_op jit(solution)/shard_map/gather_kernel/pallas_call | solution.py:692
  51.2 12.0 %fusion.triple_ref = bf16[8,2304,144]{2,1,0:T(8,128)(2,1)} fusion(f32[2304]{0:T(1024)S(1)} %slice-done, bf16[8,144,768]{2,1,0:T(8,128)(2,1)S(1)} %bitcast.88, bf16[768,2304,1]{1,0,2:T(8,128)(2,1)} %bitcast.72), kind=kOutput, calls=%fused_computation.2 | convolution fusion | flops 4082171904 | bytes 10626048 | tf_op jit(solution)/shard_map/wtc,ce->wet/dot_general | solution.py:460
  63.8 5.8 %bias_kernel.1 = f32[144,24,144]{2,1,0:T(8,128)} custom-call(f32[24,640]{1,0:T(8,128)} %pad.4.table_ref), custom_call_target="tpu_custom_call" | custom-call | tf_op jit(solution)/shard_map/bias_kernel/pallas_call | solution.py:115
  69.6 5.0 %copy.105 = f32[144,24,144]{2,0,1:T(8,128)} copy(f32[144,24,144]{2,1,0:T(8,128)} %bias_kernel.1) | data formatting | bytes 3981312 | tf_op jit(solution)/shard_map/bias_kernel/pallas_call | solution.py:115
  78.2 90.9 %forward_kernel.1 = (bf16[8,768,144]{2,1,0:T(8,128)(2,1)}, f32[8,24,1,144]{3,2,1,0:T(1,128)}, bf16[4,2,2,48,768]{4,3,2,1,0:T(8,128)(2,1)}, bf16[4,2,2,48,3072]{4...) custom-call(bf16[8,2304,144]{2,1,0:T(8,128)(2,1)} %fusion.triple_ref, f32[24,144,144]{2,1,0:T(8,128)} %bitcast.63, ...), custom_call_target="tpu_custom_call" | custom-call | tf_op jit(solution)/shard_map/forward_kernel/pallas_call | solution.py:303
  169.2 4.8 %copy.89 = bf16[8,144,768]{2,1,0:T(8,128)(2,1)} copy(bf16[8,144,768]{1,2,0:T(8,128)(2,1)} %bitcast.74) | data formatting | bytes 3538944 | tf_op jit(solution)/shard_map/wct,ce->wte/dot_general | solution.py:468
  174.6 4.1 fusion.19
  180.3 1.8 fusion.32
  182.1 3.9 copy.90.turned_ref
  186.0 2.6 add_convert_fusion.1.norm_ref
  189.7 55.1 %feed_kernel.1 = (bf16[1152,768]{1,0:T(8,128)(2,1)}, f32[1152,768]{1,0:T(8,128)}, bf16[3072,768]{1,0:T(8,128)(2,1)}, bf16[768,3072]{1,0:T(8,128)(2,1)}, f32[1,3072]{1,0:T(1,128)}) custom-call(bf16[1152,768]{1,0:T(8,128)(2,1)} %add_convert_fusion.1.norm_ref, bf16[768,1152]{1,0:T(8,128)(2,1)} %copy.90.turned_ref, bf16[1152,768]{1,0:T(8,128)(2,1)} %get-tuple-element.93.cot_ref, ...), custom_call_target="tpu_custom_call" | custom-call | tf_op jit(solution)/shard_map/feed_kernel/pallas_call | solution.py:428
  244.9 4.0 multiply_reduce_fusion
  252.8 2.9 fusion.10
  255.7 2.8 convolution_convert_fusion
  258.5 4.4 copy.91
  262.9 81.5 %backward_kernel.1 = (bf16[8,2304,144]{2,1,0:T(8,128)(2,1)}, f32[24,144,144]{2,1,0:T(8,128)}, f32[48,384]{1,0:T(8,128)}, f32[48,1536]{1,0:T(8,128)}, f32[192,384]{1,0:T(8,128)}) custom-call(bf16[8,2304,144]{2,1,0:T(8,128)(2,1)} %fusion.triple_ref, bf16[8,768,144]{2,1,0:T(8,128)(2,1)} %bitcast.66, f32[8,24,1,144]{3,2,1,0:T(1,128)} %get-tuple-element.98.log_ref, ...), custom_call_target="tpu_custom_call" | custom-call | tf_op jit(solution)/shard_map/backward_kernel/pallas_call | solution.py:341
  344.4 11.8 %fusion.1 = bf16[768,2304]{1,0:T(8,128)(2,1)S(1)} fusion(bf16[8,144,768]{2,1,0:T(8,128)(2,1)} %bitcast.87, bf16[8,2304,144]{2,1,0:T(8,128)(2,1)} %get-tuple-element.101), kind=kOutput, calls=%fused_computation.4 | convolution fusion | flops 4080402432 | bytes 10616832 | tf_op jit(solution)/shard_map/wtc,wet->ce/dot_general | solution.py:509
  356.2 31.7 %scatter_kernel.1 = f32[3,16,1152]{2,1,0:T(8,128)S(1)} custom-call(bf16[4,2,2,3,16,2304]{5,4,3,2,1,0:T(8,128)(2,1)S(1)} %bitcast.60), custom_call_target="tpu_custom_call" | custom-call | tf_op jit(solution)/shard_map/scatter_kernel/pallas_call | solution.py:874
  388.6 5.1 %moment_kernel.1 = (f32[48,1152]{1,0:T(8,128)}, f32[48,1152]{1,0:T(8,128)}, f32[48,1152]{1,0:T(8,128)}, f32[48,384]{1,0:T(8,128)}, f32[48,384]{1,0:T(8,128)}, /*...) custom-call(f32[48,1152]{1,0:T(8,128)} %bitcast.61, ...), custom_call_target="tpu_custom_call" | custom-call | tf_op jit(solution)/shard_map/moment_kernel/pallas_call | solution.py:1051
  393.7 11.0 %copy.95 = bf16[8,144,2304]{2,1,0:T(8,128)(2,1)} copy(bf16[8,144,2304]{1,2,0:T(8,128)(2,1)} %bitcast.62) | data formatting | bytes 10616832 | tf_op jit(solution)/shard_map/wet,ce->wtc/dot_general | solution.py:513
  405.4 9.1 %fusion.15 = (f32[768]{0:T(1024)S(1)}, f32[1152]{0:T(1024)S(1)}, f32[1152]{0:T(1024)S(1)}, f32[1152,768]{1,0:T(8,128)S(1)}) fusion(f32[768]{0:T(1024)S(1)} %copy-done.23, f32[1152]{0:T(1024)S(1)} %broadcast_multiply_fusion, bf16[1152,768]{1,0:T(8,128)(2,1)} %get-tuple-element.89, bf16[1152,2304]{1,0:T(8,128)(2,1)} %bitcast.67, bf16[768,2304]{1,0:T(8,128)(2,1)} %bitcast.73), kind=kOutput, calls=%fused_computation.47 | convolution fusion | flops 4083938304 | bytes 14175744 | tf_op jit(solution)/shard_map/wet,ce->wtc/dot_general | solution.py:513
  414.6 1.7 fusion.9
  416.3 3.5 convert_reduce_fusion.2
  421.6 3.8 copy.104
  425.5 5.5 %table_kernel.1.refs_8_ = f32[24,640]{1,0:T(8,128)} custom-call(f32[144,24,144]{2,1,0:T(8,128)} %bitcast.65), custom_call_target="tpu_custom_call" | custom-call | tf_op jit(solution)/shard_map/table_kernel/pallas_call | solution.py:124
  431.0 5.3 %convert_reduce_fusion = f32[2304]{0:T(1024)S(1)} fusion(bf16[8,2304,144]{2,1,0:T(8,128)(2,1)} %get-tuple-element.101), kind=kLoop, calls=%fused_computation | loop fusion | flops 5306112 | bytes 5317632 | tf_op jit(solution)/shard_map/reduce_sum | solution.py:512
  438.7 22.0 %sum_kernel.1 = (f32[4,768]{1,0:T(4,128)}, f32[1,6912]{1,0:T(1,128)}, f32[24,640]{1,0:T(8,128)}, f32[8,128]{1,0:T(8,128)}) custom-call(f32[1,768]{1,0:T(1,128)} %reshape.188.refs_0_, f32[1,768]{1,0:T(1,128)} %reshape.189.refs_1_, f32[1,768]{1,0:T(1,128)} %reshape.190.refs_2_, f32[1,768]{1,0:T(1,128)} %reshape.191.refs_3_, ...), custom_call_target="tpu_custom_call" | custom-call | tf_op jit(solution)/shard_map/sum_kernel/pallas_call | solution.py:1062
  462.6 4.4 apply_kernel.1
  472.6 4.5 exit_kernel.1
  (102 shorter events, 25.2 us)
Async XLA Ops:
  0.7 12.7 %copy-start.12 = (f32[48,1152]{1,0:T(8,128)S(1)}, f32[48,1152]{1,0:T(8,128)}, u32[]{:S(2)}) copy-start(f32[48,1152]{1,0:T(8,128)} %refs_0_.1) | copy-start | bytes 663556
  4.6 46.6 %slice-start = ((f32[6912]{0:T(1024)}), f32[2304]{0:T(1024)S(1)}, s32[]{:S(2)}) async-start(f32[6912]{0:T(1024)} %param.48), calls=%async_computation | async-start | bytes 24576 | tf_op jit(solution)/shard_map/slice | solution.py:461
  13.3 37.8 %copy-start.30 = (bf16[1152,768]{1,0:T(8,128)(2,1)S(1)}, bf16[1152,768]{1,0:T(8,128)(2,1)}, u32[]{:S(2)}) copy-start(bf16[1152,768]{1,0:T(8,128)(2,1)} %get-tuple-element.90) | copy-start | bytes 5308420
  51.2 12.0 %copy-start.14 = (f32[529,24]{0,1:T(8,128)S(1)}, f32[529,24]{0,1:T(8,128)}, u32[]{:S(2)}) copy-start(f32[529,24]{0,1:T(8,128)} %param.51) | copy-start | bytes 152356
  69.6 5.0 %copy-start.29 = (s32[576]{0:T(1024)S(1)}, s32[576]{0:T(1024)}, u32[]{:S(2)}) copy-start(s32[576]{0:T(1024)} %param.29) | copy-start | bytes 6916
  69.6 6.6 %copy-start.10 = (f32[48,1536]{1,0:T(8,128)S(1)}, f32[48,1536]{1,0:T(8,128)}, u32[]{:S(2)}) copy-start(f32[48,1536]{1,0:T(8,128)} %refs_2_.1) | copy-start | bytes 884740
  69.6 7.3 %copy-start.11 = (f32[192,384]{1,0:T(8,128)S(1)}, f32[192,384]{1,0:T(8,128)}, u32[]{:S(2)}) copy-start(f32[192,384]{1,0:T(8,128)} %refs_3_.1) | copy-start | bytes 884740
  69.6 8.0 %copy-start.13 = (f32[48,384]{1,0:T(8,128)S(1)}, f32[48,384]{1,0:T(8,128)}, u32[]{:S(2)}) copy-start(f32[48,384]{1,0:T(8,128)} %refs_1_.1) | copy-start | bytes 221188
  169.2 4.8 %copy-start.15 = (f32[6912]{0:T(1024)S(1)}, f32[6912]{0:T(1024)}, u32[]{:S(2)}) copy-start(f32[6912]{0:T(1024)} %param.48) | copy-start | bytes 82948
  178.6 7.3 %copy-start.1 = (f32[1152,768]{1,0:T(8,128)}, f32[1152,768]{1,0:T(8,128)S(1)}, u32[]{:S(2)}) copy-start(f32[1152,768]{1,0:T(8,128)S(1)} %get-tuple-element.264.middle_ref) | copy-start | bytes 10616836
  178.6 1.6 copy-start.18
  178.7 1.6 copy-start.22
  179.2 1.0 copy-start.20
  186.0 2.6 copy-start.28
  186.0 3.2 copy-start.16
  189.7 55.1 %copy-start.2 = (f32[1152,768]{1,0:T(8,128)S(1)}, f32[1152,768]{1,0:T(8,128)}, u32[]{:S(2)}) copy-start(f32[1152,768]{1,0:T(8,128)} %copy-done.1) | copy-start | bytes 10616836
  189.7 55.1 %copy-start.19 = (f32[768]{0:T(1024)S(1)}, f32[768]{0:T(1024)}, u32[]{:S(2)}) copy-start(f32[768]{0:T(1024)} %get-tuple-element.249) | copy-start | bytes 9220
  244.9 4.0 copy-start.21
  244.9 4.0 copy-start.7
  248.9 1.5 copy-start.3
  248.9 2.0 copy-start.5
  250.9 1.9 copy-start.9
  252.8 2.9 copy-start.31
  393.7 11.7 %copy-start.23 = (f32[768]{0:T(1024)S(1)}, f32[768]{0:T(1024)}, u32[]{:S(2)}) copy-start(f32[768]{0:T(1024)} %get-tuple-element.248) | copy-start | bytes 9220
  405.4 9.1 %copy-start.6 = (bf16[1152,768]{1,0:T(8,128)(2,1)S(1)}, bf16[1152,768]{1,0:T(8,128)(2,1)}, u32[]{:S(2)}) copy-start(bf16[1152,768]{1,0:T(8,128)(2,1)} %get-tuple-element.89) | copy-start | bytes 5308420
  414.6 1.8 copy-start.4
  416.3 5.3 %copy-start.8 = (f32[24,144,144]{2,1,0:T(8,128)S(1)}, f32[24,144,144]{2,1,0:T(8,128)}, u32[]{:S(2)}) copy-start(f32[24,144,144]{2,1,0:T(8,128)} %get-tuple-element.112) | copy-start | bytes 5971972
  431.0 6.5 %copy-start.27 = (f32[768]{0:T(1024)S(1)}, f32[768]{0:T(1024)}, u32[]{:S(2)}) copy-start(f32[768]{0:T(1024)} %get-tuple-element.240) | copy-start | bytes 9220
  431.0 7.1 %copy-start.26 = (f32[768]{0:T(1024)S(1)}, f32[768]{0:T(1024)}, u32[]{:S(2)}) copy-start(f32[768]{0:T(1024)} %get-tuple-element.244) | copy-start | bytes 9220
  431.0 29.7 %copy-start.17 = (f32[6912]{0:T(1024)S(1)}, f32[6912]{0:T(1024)}, u32[]{:S(2)}) copy-start(f32[6912]{0:T(1024)} %param.48) | copy-start | bytes 82948
  431.0 30.4 %copy-start.24 = (f32[6912]{0:T(1024)S(1)}, f32[6912]{0:T(1024)}, u32[]{:S(2)}) copy-start(f32[6912]{0:T(1024)} %param.49) | copy-start | bytes 82948
  431.0 31.0 %copy-start.25 = (f32[6912]{0:T(1024)S(1)}, f32[6912]{0:T(1024)}, u32[]{:S(2)}) copy-start(f32[6912]{0:T(1024)} %param.50) | copy-start | bytes 82948
  (1 other events, 0.7 us)
